TPU v7x, 128 devices: a whole 4x4x4 slice. The times are simulated.
128 devices in a mesh: occ: 8 (over y, core), vir: 16 (over x, z).
Axes of the slice: x: 4, y: 4, z: 4, core: 2. Of those that a mesh axis runs over, the one named last changes fastest.
Arguments:
- amplitudes: bfloat16 [32, 32, 256, 256], P('vir', None, 'occ'), may hold values from -0.0234375 to 0.0234375
- pair_factor: bfloat16 [256, 256, 512], P('vir', 'occ'), may hold values from -1.296875 to 1.296875
- block_factor: bfloat16 [32, 256, 512], P(None, None, ('occ', 'vir')), may hold values from -1.296875 to 1.296875
- cycle_matrix: bfloat16 [8192, 8192], P('occ', 'vir'), may hold values from -0.0625 to 0.0625
- occ_energy: float32 [32], replicated, may hold values from -2 to -0.3
- block_energy: float32 [32], replicated, may hold values from 0.2 to 3
- virt_energy: float32 [256], replicated, may hold values from 0.2 to 3
Outputs:
- update: float32 [1024, 8192], P('occ', 'vir')
All inputs are finite; a program needn't handle non-finite values.
Results may differ from a plain program's by a relative error of at most 0.0035.
Values may be sent and summed in bfloat16 or wider, within the bound.
No kernel may reach another device: no remote copies, remote signals or barrier semaphores. Data moves between devices by JAX's collectives and lax.ppermute only.
A program may use at most 128 MiB of HBM per device.

v0:
```python
import jax
import jax.numpy as jnp
from jax import lax
from jax.experimental import pallas as pl
from jax.experimental.pallas import tpu as pltpu
from jax.sharding import PartitionSpec as P


BF16, F32 = jnp.bfloat16, jnp.float32
OCC, VIR = ("y", "core"), ("x", "z")
ALL_CZ = [(c, z) for c in range(2) for z in range(4)]


def amplitude_route(alpha):
    return [(c * 4 + z, (z // 2) * 4 + 2 * c + ((z % 2) ^ alpha)) for c, z in ALL_CZ]


def ring(value, axis, shift):
    n = lax.axis_size(axis)
    return lax.ppermute(value, axis, [(i, (i + shift) % n) for i in range(n)])


def sibling(value):
    return lax.ppermute(value, "core", [(0, 1), (1, 0)])


def integrals_kernel(where_ref, *refs):
    pairs, blocks, out_ref, rhs = refs[:4], refs[4:8], refs[8], refs[9]
    nd, nb, naux = pairs[0].shape
    two, nq, nc = blocks[0].shape
    for far, ref in zip((0, 1, 3, 2), blocks):
        start = pl.multiple_of(((where_ref[0] + 4 - far) % 4) * nq, nq)
        for k in range(two):
            rhs[pl.ds(start, nq), k * nc : (k + 1) * nc] = ref[k]
    for s, ref in enumerate(pairs):
        got = jnp.dot(
            ref[...].reshape(nd * nb, naux), rhs[...], preferred_element_type=F32
        ).astype(BF16)
        for k in range(two):
            for d in range(nd):
                out_ref[(k * 4 + s) * nb : (k * 4 + s + 1) * nb, d * nc : (d + 1) * nc] = got[
                    d * nb : (d + 1) * nb, k * nc : (k + 1) * nc
                ]


def form_integrals(where, pairs, blocks):
    nd, nb, naux = pairs[0].shape
    na, nq, nc = blocks[0].shape
    step = 2
    return pl.pallas_call(
        integrals_kernel,
        grid_spec=pltpu.PrefetchScalarGridSpec(
            num_scalar_prefetch=1,
            grid=(na // step,),
            in_specs=[pl.BlockSpec((nd, nb, naux), lambda g, w: (0, 0, 0))] * 4
            + [pl.BlockSpec((step, nq, nc), lambda g, w: (g, 0, 0))] * 4,
            out_specs=pl.BlockSpec((step * 4 * nb, nd * nc), lambda g, w: (g, 0)),
            scratch_shapes=[pltpu.VMEM((naux, step * nc), BF16)],
        ),
        out_shape=jax.ShapeDtypeStruct((na * 4 * nb, nd * nc), BF16),
        cost_estimate=pl.CostEstimate(
            flops=8 * nd * nb * naux * na * nc, bytes_accessed=12 << 20, transcendentals=0
        ),
        name="integrals",
    )(where, *pairs, *blocks)


def turn_kernel(where_ref, zero_ref, one_ref, out_ref):
    nd, _, nc = zero_ref.shape
    flip = where_ref[0] == 1
    for d in range(nd):
        p, q = zero_ref[d], one_ref[d]
        pair = jnp.concatenate([jnp.where(flip, q, p), jnp.where(flip, p, q)], axis=0)
        out_ref[d * nc : (d + 1) * nc, :] = pair.T


def turn(where, zero, one):
    nd, rows, nc = zero.shape
    return pl.pallas_call(
        turn_kernel,
        in_specs=[pl.BlockSpec(memory_space=pltpu.SMEM)]
        + [pl.BlockSpec(memory_space=pltpu.VMEM)] * 2,
        out_specs=pl.BlockSpec(memory_space=pltpu.VMEM),
        out_shape=jax.ShapeDtypeStruct((nd * nc, 2 * rows), BF16),
        name="turn",
    )(where, zero, one)


def ladder_kernel(where_ref, *refs):
    amps, w_ref, out_ref, turned = refs[:-3], refs[-3], refs[-2], refs[-1]
    depth, wide = amps[0].shape
    j = pl.program_id(1)

    @pl.when((pl.program_id(0) == 0) & (j == 0))
    def _():
        for n in range(6):
            at = n % 2 * wide
            turned[n // 2, :, at : at + wide] = amps[n][...]
        for n in range(4):
            at = n % 2 * wide
            row = n // 2 * (depth // 2)
            turned[3, row : row + depth // 2, at : at + wide] = amps[6 + n][...]

    got = jnp.dot(w_ref[...], turned[j], preferred_element_type=F32).astype(BF16)
    _, two, nz, na, nb, _ = out_ref.shape
    for side in range(two):
        c = where_ref[4] ^ side
        for s in range(nz):
            for a in range(na):
                row = (a * nz + s) * nb
                out_ref[0, c, where_ref[5] ^ s, a] = got[
                    row : row + nb, side * wide : (side + 1) * wide
                ]


def partial_ladder(where, amps, w):
    wide = amps[0].shape[1]
    nrow, depth = w.shape
    step, nz, nb = 512, 4, 16
    na = step // (nz * nb)
    return pl.pallas_call(
        ladder_kernel,
        grid_spec=pltpu.PrefetchScalarGridSpec(
            num_scalar_prefetch=1,
            grid=(nrow // step, 4),
            in_specs=[pl.BlockSpec(v.shape, lambda g, j, h: (0, 0)) for v in amps]
            + [pl.BlockSpec((step, depth), lambda g, j, h: (g, 0))],
            out_specs=pl.BlockSpec(
                (1, 2, nz, na, nb, wide), lambda g, j, h: (h[j], 0, 0, g, 0, 0)
            ),
            scratch_shapes=[pltpu.VMEM((4, depth, 2 * wide), BF16)],
        ),
        out_shape=jax.ShapeDtypeStruct((4, 2, nz, nrow // (nz * nb), nb, wide), BF16),
        cost_estimate=pl.CostEstimate(
            flops=16 * nrow * depth * wide, bytes_accessed=18 << 20, transcendentals=0
        ),
        name="ladder",
    )(where, *amps, w)


def settle_kernel(parts_ref, direct_ref, holes_ref, total, swapped):
    ny, two, nz, part, wide = parts_ref.shape
    rows = two * part
    nb = 16
    na = rows // nb
    ni = wide // na
    nj = wide // ni
    for h in range(two):
        acc = parts_ref[0, h, 0].astype(F32)
        for p in range(1, ny * nz):
            acc = acc + parts_ref[p // nz, h, p % nz].astype(F32)
        total[h * part : (h + 1) * part] = acc
    per = wide // nj
    for group in range(nb // per):
        blocks = [total[pl.ds(group * per + k, na, stride=nb), :] for k in range(per)]
        for i in range(ni):
            direct_ref[i * na : (i + 1) * na, group * wide : (group + 1) * wide] = jnp.concatenate(
                [m[:, i * nj : (i + 1) * nj] for m in blocks], axis=1
            )
        for k, m in enumerate(blocks):
            flipped = m.T
            swapped[pl.ds(group * per + k, nj, stride=nb), :] = jnp.concatenate(
                [flipped[i * nj : (i + 1) * nj, :] for i in range(ni)], axis=1
            )
    held = swapped[...].astype(BF16)
    for p in range(holes_ref.shape[0]):
        holes_ref[p] = held


def settle(parts):
    rows, wide = parts.shape[1] * parts.shape[3], parts.shape[4]
    return pl.pallas_call(
        settle_kernel,
        out_shape=(
            jax.ShapeDtypeStruct((128, 512), F32),
            jax.ShapeDtypeStruct((16, rows, wide), BF16),
        ),
        scratch_shapes=[pltpu.VMEM((rows, wide), F32), pltpu.VMEM((rows, wide), F32)],
        name="settle",
    )(parts)


def cycle_kernel(where_ref, holes_ref, *refs):
    pieces, (direct_ref, row_ref, col_ref, out_ref) = refs[:10], refs[10:]
    peers, _, nb, wide = holes_ref.shape
    acc = direct_ref[...]
    chunks = [(s, side, n * 2 + side, 0, 4) for n, s in enumerate((0, 3, 1)) for side in (0, 1)]
    chunks += [(2, side, 6 + 2 * part + side, 2 * part, 2) for part in (0, 1) for side in (0, 1)]
    for shift, side, at, base, count in chunks:
        owner = ((where_ref[0] + shift) % 4) * 2 + (where_ref[1] ^ side)
        lhs = jnp.concatenate(
            [
                holes_ref[:, owner * 4 + base + k].reshape(peers * nb, wide).T
                for k in range(count)
            ],
            axis=1,
        )
        acc = acc + jnp.dot(lhs, pieces[at][...], preferred_element_type=F32)
    out_ref[...] = acc / (row_ref[...] + col_ref[...])


def finish(where, holes, pieces, direct, row, col):
    return pl.pallas_call(
        cycle_kernel,
        in_specs=[pl.BlockSpec(memory_space=pltpu.SMEM)]
        + [pl.BlockSpec(memory_space=pltpu.VMEM)] * (len(pieces) + 4),
        out_specs=pl.BlockSpec(memory_space=pltpu.VMEM),
        out_shape=jax.ShapeDtypeStruct(direct.shape, F32),
        name="cycle",
    )(where, holes, *pieces, direct, row, col)


def update(
    amplitudes, pair_factor, block_factor, cycle_matrix, occ_energy, block_energy, virt_energy
):
    y, core, x, z = (lax.axis_index(n) for n in ("y", "core", "x", "z"))
    half = z % 2
    ni, nj, nd, nc = amplitudes.shape

    def scalars(*values):
        return jnp.stack([jnp.asarray(v, jnp.int32) for v in values])

    na, _, nq = block_factor.shape
    block = block_factor.reshape(2, na // 2, 2, nc // 2, nq).transpose(0, 2, 1, 4, 3)
    block = jnp.broadcast_to(block[:, None, None], (2, 4, 2, 2, na // 2, nq, nc // 2))
    block = lax.all_to_all(
        block.reshape(32, na // 2, nq, nc // 2), ("core", "x", "z"), 0, 0, tiled=True
    )
    block = block.transpose(1, 0, 2, 3).reshape(na // 2, 32 * nq, nc // 2)

    flat = amplitudes.reshape(ni * nj, nd, nc)
    own = [
        lax.ppermute(
            lax.dynamic_slice_in_dim(flat, (half ^ alpha) * (nc // 2), nc // 2, 2).transpose(
                1, 0, 2
            ),
            ("core", "z"),
            amplitude_route(alpha),
        )
        for alpha in range(2)
    ]
    own = turn(scalars(half), *own)

    left, right = ring(own, "x", 1), ring(own, "x", -1)
    blocks = [block] + [ring(block, "y", k) for k in (1, 3, 2)]
    turned = pair_factor.transpose(1, 0, 2)
    turned, own = lax.optimization_barrier((turned, own))
    pair = [lax.ppermute(turned, ("core", "z"), amplitude_route(alpha)) for alpha in range(2)]
    before, after = ring(cycle_matrix, "y", 1), ring(cycle_matrix, "y", -1)

    left, right, *blocks = lax.optimization_barrier((left, right, *blocks))
    mid = own.shape[0] // 2
    far = [ring(left[:mid], "x", 1), ring(right[mid:], "x", -1)]
    pair += [sibling(v) for v in pair]
    amps = []
    for v in (own, left, right):
        amps += [v, sibling(v)]
    for v in far:
        amps += [v, sibling(v)]

    w = form_integrals(scalars(y), pair, blocks)
    w, before, after = lax.optimization_barrier((w, before, after))

    spots = scalars(x, (x + 3) % 4, (x + 1) % 4, (x + 2) % 4, core, 2 * core + half)
    parts = partial_ladder(spots, amps, w)
    parts = parts.reshape(32, -1, parts.shape[-1])
    parts = lax.all_to_all(parts, ("y", "core", "z"), 0, 0, tiled=True)
    direct, holes = settle(parts.reshape(4, 2, 4, -1, parts.shape[-1]))
    holes = lax.all_to_all(holes.reshape(16, nj, 16, 128), VIR, 0, 0, tiled=True)

    mid = cycle_matrix.shape[0] // 2
    matrix = []
    ends = ring(before[:mid], "y", 1), ring(after[mid:], "y", -1)
    for v in (cycle_matrix, before, after, *ends):
        matrix += [v, sibling(v)]

    occ_rows = nj // 8
    cols = virt_energy.shape[0] // 16
    occ_here = lax.dynamic_slice_in_dim(occ_energy, (2 * y + core) * occ_rows, occ_rows, 0)
    virt_here = lax.dynamic_slice_in_dim(virt_energy, (4 * x + z) * cols, cols, 0)
    row = (block_energy[None, :] - occ_here[:, None]).reshape(-1, 1)
    col = (virt_here[:, None] - occ_energy[None, :]).reshape(1, -1)
    return finish(scalars(y, core), holes, matrix, direct, row, col)


def solution(mesh):
    fine = jax.sharding.Mesh(mesh.devices.reshape(4, 2, 4, 4), ("y", "core", "x", "z"))
    return jax.shard_map(
        update,
        mesh=fine,
        in_specs=(
            P(VIR, None, OCC, None),
            P(VIR, OCC, None),
            P(None, None, OCC + VIR),
            P(OCC, VIR),
            P(),
            P(),
            P(),
        ),
        out_specs=P(OCC, VIR),
        check_vma=False,
    )
```

profile of v0, /device:TPU:0, one launch (start us, length us, event | category | flops | bytes accessed | tf_op | source)
XLA Modules:
  0.0 206.6 jit_solution(8767695009706640942)
XLA Ops:
  0.0 1.8 copy.13
  1.9 0.0 copy-start.4
  1.9 1.2 dynamic-slice_bitcast_fusion
  3.0 1.7 collective-permute-start
  4.7 2.0 collective-permute-start.1
  6.8 0.2 broadcast_in_dim.2
  7.1 21.7 %all_to_all.15 = bf16[32,16,4,128]{3,2,1,0:T(4,128)(2,1)S(1)} all-to-all(bf16[32,16,4,128]{3,2,1,0:T(4,128)(2,1)S(1)} %bitcast.29), channel_id=1, replica_groups=mesh['y'=4,'core'=2,'x'=4,'z'=4] {'core','x','z'}, dimensions={0} | all-to-all | bytes 1048576 | tf_op jit(solution)/shard_map/all_to_all | solution.py:226
  28.7 0.2 copy.15
  29.0 1.6 collective-permute-start.5
  30.6 1.1 copy.18
  31.7 1.7 collective-permute-start.6
  33.4 2.0 collective-permute-start.7
  35.4 0.8 copy-done.2
  36.2 0.2 copy-done.3
  36.4 2.5 %turn.1.refs_0_ = bf16[4096,128]{1,0:T(8,128)(2,1)} custom-call(s32[1]{0:T(128)} %bitcast.8.where_ref, bf16[32,64,128]{2,1,0:T(8,128)(2,1)} %copy-done.2, bf16[32,64,128]{2,1,0:T(8,128)(2,1)} %copy-done.3), custom_call_target="tpu_custom_call" | custom-call | tf_op jit(solution)/shard_map/turn/pallas_call | solution.py:79
  38.9 1.7 collective-permute-start.14
  40.6 1.5 collective-permute-start.3
  42.0 2.2 %collective-permute-done.5.refs_5_ = bf16[16,128,128]{2,1,0:T(8,128)(2,1)S(1)} collective-permute-done((bf16[16,128,128]{2,1,0:T(8,128)(2,1)S(1)}, bf16[16,128,128]{2,1,0:T(8,128)(2,1)S(1)}, u32[]{:S(2)}, u32[]{:S(2)}) %collective-permute-start.5) | collective-permute-done | bytes 524320 | tf_op jit(solution)/shard_map/ppermute | solution.py:20
  44.3 2.8 %collective-permute-start.4 = (bf16[4096,128]{1,0:T(8,128)(2,1)}, bf16[4096,128]{1,0:T(8,128)(2,1)}, u32[]{:S(2)}, u32[]{:S(2)}) collective-permute-start(bf16[4096,128]{1,0:T(8,128)(2,1)} %turn.1.refs_0_), channel_id=1, source_target_pairs={{0,12},{4,0},{8,4},{12,8},{1,13},{5,1},{9,5},{13,9},{2,14},{6,2},{... | collective-permute-start | bytes 3145736 | tf_op jit(solution)/shard_map/ppermute | solution.py:20
  47.0 1.2 collective-permute-start.18
  48.2 9.4 %collective-permute-done.7.refs_7_ = bf16[16,128,128]{2,1,0:T(8,128)(2,1)S(1)} collective-permute-done((bf16[16,128,128]{2,1,0:T(8,128)(2,1)S(1)}, bf16[16,128,128]{2,1,0:T(8,128)(2,1)S(1)}, u32[]{:S(2)}, u32[]{:S(2)}) %collective-permute-start.7) | collective-permute-done | bytes 524320 | tf_op jit(solution)/shard_map/ppermute | solution.py:20
  57.6 2.2 %collective-permute-start.19 = (bf16[1024,512]{1,0:T(8,128)(2,1)}, bf16[1024,512]{1,0:T(8,128)(2,1)}, u32[]{:S(2)}, u32[]{:S(2)}) collective-permute-start(bf16[1024,512]{1,0:T(8,128)(2,1)} %refs_0_.1), channel_id=1, source_target_pairs={{0,96},{32,0},{64,32},{96,64},{1,97},{33,1},{65,33},{97,65},{2,98}... | collective-permute-start | bytes 3145736 | tf_op jit(solution)/shard_map/ppermute | solution.py:20
  59.8 0.3 collective-permute-start.15
  60.0 9.1 %collective-permute-done.15.refs_1_ = bf16[32,16,512]{2,1,0:T(8,128)(2,1)S(1)} collective-permute-done((bf16[32,16,512]{2,1,0:T(8,128)(2,1)}, bf16[32,16,512]{2,1,0:T(8,128)(2,1)S(1)}, u32[]{:S(2)}, u32[]{:S(2)}) %collective-permute-start.15) | collective-permute-done | bytes 524320 | tf_op jit(solution)/shard_map/ppermute | solution.py:248
  69.2 0.5 collective-permute-start.17
  69.7 0.1 collective-permute-start.2
  69.8 1.1 slice.13
  70.9 8.3 %collective-permute-done.18.refs_2_ = bf16[1024,512]{1,0:T(8,128)(2,1)S(1)} collective-permute-done((bf16[1024,512]{1,0:T(8,128)(2,1)}, bf16[1024,512]{1,0:T(8,128)(2,1)S(1)}, u32[]{:S(2)}, u32[]{:S(2)}) %collective-permute-start.18) | collective-permute-done | bytes 1048608 | tf_op jit(solution)/shard_map/ppermute | solution.py:20
  79.2 1.5 collective-permute-start.10
  80.7 0.9 collective-permute-done.19.refs_4_
  81.5 2.9 %collective-permute-start.12 = (bf16[2048,128]{1,0:T(8,128)(2,1)S(1)}, bf16[2048,128]{1,0:T(8,128)(2,1)}, u32[]{:S(2)}, u32[]{:S(2)}) collective-permute-start(bf16[2048,128]{1,0:T(8,128)(2,1)S(1)} %slice.13), channel_id=1, source_target_pairs={{0,12},{4,0},{8,4},{12,8},{1,13},{5,1},{9,5},{13,9},{2,14},{6,2},{... | collective-permute-start | bytes 1572872 | tf_op jit(solution)/shard_map/ppermute | solution.py:20
  84.4 0.1 collective-permute-start.8
  84.5 0.5 collective-permute-start.9
  85.0 5.4 %collective-permute-done.10.refs_6_ = bf16[2048,128]{1,0:T(8,128)(2,1)} collective-permute-done((bf16[2048,128]{1,0:T(8,128)(2,1)S(1)}, bf16[2048,128]{1,0:T(8,128)(2,1)}, u32[]{:S(2)}, u32[]{:S(2)}) %collective-permute-start.10) | collective-permute-done | bytes 524320 | tf_op jit(solution)/shard_map/ppermute | solution.py:20
  90.4 3.2 %collective-permute-done.12.refs_8_ = bf16[2048,128]{1,0:T(8,128)(2,1)} collective-permute-done((bf16[2048,128]{1,0:T(8,128)(2,1)S(1)}, bf16[2048,128]{1,0:T(8,128)(2,1)}, u32[]{:S(2)}, u32[]{:S(2)}) %collective-permute-start.12) | collective-permute-done | bytes 524320 | tf_op jit(solution)/shard_map/ppermute | solution.py:20
  93.6 0.1 collective-permute-start.13
  93.7 0.6 stack.40.where_ref
  94.3 10.6 %integrals.1.refs_10_ = bf16[1024,4096]{1,0:T(8,128)(2,1)} custom-call(s32[1]{0:T(128)} %bitcast.where_ref, bf16[32,16,512]{2,1,0:T(8,128)(2,1)} %copy-done.13, bf16[32,16,512]{2,1,0:T(8,128)(2,1)} %copy-done.14, bf16[32,16,512]{2,1,0:T(8,128)(2,1)} %copy-done.15, bf16[32,16,512]{2,1,0:T(8,128)(2,1)} %copy-done.16, bf16[16,128,128]{2,1,0:T(8,128)(2,1)} %bitcast.34, ...), custom_call_target="tpu_custom_call" | custom-call | flops 4294967296 | bytes 12582912 | tf_op jit(solution)/shard_map/integrals/pallas_call | solution.py:50
  105.0 1.0 copy-done.10
  105.9 19.1 %ladder.1 = bf16[4,2,4,16,16,128]{5,4,3,2,1,0:T(8,128)(2,1)} custom-call(s32[6]{0:T(128)} %stack.40.where_ref, bf16[4096,128]{1,0:T(8,128)(2,1)} %turn.1.refs_0_, bf16[4096,128]{1,0:T(8,128)(2,1)} %collective-permute-done.2.refs_1_, bf16[4096,128]{1,0:T(8,128)(2,1)} %copy-done.6, bf16[4096,128]{1,0:T(8,128)(2,1)} %copy-done.10, ...), custom_call_target="tpu_custom_call" | custom-call | flops 8589934592 | bytes 18874368 | tf_op jit(solution)/shard_map/ladder/pallas_call | solution.py:121
  125.0 34.2 %all_to_all.16 = bf16[32,256,128]{2,1,0:T(8,128)(2,1)} all-to-all(bf16[32,256,128]{2,1,0:T(8,128)(2,1)} %bitcast.28), channel_id=1, replica_groups=mesh['y'=4,'core'=2,'x'=4,'z'=4] {'y','core','z'}, dimensions={0} | all-to-all | bytes 4194304 | tf_op jit(solution)/shard_map/all_to_all | solution.py:267
  159.3 4.0 %settle.1 = (f32[128,512]{1,0:T(8,128)}, bf16[16,512,128]{2,1,0:T(8,128)(2,1)}) custom-call(bf16[4,2,4,256,128]{4,3,2,1,0:T(8,128)(2,1)} %bitcast.25), custom_call_target="tpu_custom_call" | custom-call | tf_op jit(solution)/shard_map/settle/pallas_call | solution.py:172
  163.3 6.2 %all-to-all-start.2 = ((bf16[16,32,16,128]{3,2,1,0:T(8,128)(2,1)}), bf16[16,32,16,128]{3,2,1,0:T(8,128)(2,1)S(1)}, u32[]{:S(2)}, u32[]{:S(2)}) async-start(bf16[16,32,16,128]{3,2,1,0:T(8,128)(2,1)} %bitcast.27), calls=%async_computation.2 | async-start | bytes 4194304 | tf_op jit(solution)/shard_map/all_to_all | solution.py:269
  169.5 0.0 copy-start.17
  169.5 0.0 copy-start.8
  169.5 0.0 copy-start.9
  169.5 0.8 slice.14
  170.3 0.6 collective-permute-start.23
  171.0 1.9 slice.15
  172.8 2.6 %collective-permute-start.25 = (bf16[512,512]{1,0:T(8,128)(2,1)}, bf16[512,512]{1,0:T(8,128)(2,1)}, u32[]{:S(2)}, u32[]{:S(2)}) collective-permute-start(bf16[512,512]{1,0:T(8,128)(2,1)} %slice.15), channel_id=1, source_target_pairs={{0,96},{32,0},{64,32},{96,64},{1,97},{33,1},{65,33},{97,65},{2,98}... | collective-permute-start | bytes 1572872 | tf_op jit(solution)/shard_map/ppermute | solution.py:20
  175.5 0.5 collective-permute-start.21
  176.0 0.0 collective-permute-start.22
  176.0 0.1 dynamic_slice.15
  176.0 8.8 %collective-permute-done.23.refs_6_ = bf16[512,512]{1,0:T(8,128)(2,1)} collective-permute-done((bf16[512,512]{1,0:T(8,128)(2,1)}, bf16[512,512]{1,0:T(8,128)(2,1)}, u32[]{:S(2)}, u32[]{:S(2)}) %collective-permute-start.23) | collective-permute-done | bytes 524320 | tf_op jit(solution)/shard_map/ppermute | solution.py:20
  184.9 1.1 collective-permute-done.25.refs_8_
  186.0 0.1 broadcast_subtract_fusion
  186.1 0.7 sub.53.refs_12_
  186.8 0.1 dynamic_slice.14
  186.9 0.1 broadcast_subtract_fusion.1
  186.9 0.7 sub.54.refs_11_
  187.7 0.6 pad_add_fusion.where_ref
  188.3 10.8 %all-to-all-done.2.holes_ref = bf16[16,32,16,128]{3,2,1,0:T(8,128)(2,1)S(1)} async-done(((bf16[16,32,16,128]{3,2,1,0:T(8,128)(2,1)}), bf16[16,32,16,128]{3,2,1,0:T(8,128)(2,1)S(1)}, u32[]{:S(2)}, u32[]{:S(2)}) %all-to-all-start.2) | async-done | bytes 2097184 | tf_op jit(solution)/shard_map/all_to_all | solution.py:269
  199.2 1.3 copy-done
  200.5 6.0 %cycle.1 = f32[128,512]{1,0:T(8,128)} custom-call(s32[2]{0:T(128)} %pad_add_fusion.where_ref, bf16[16,32,16,128]{3,2,1,0:T(8,128)(2,1)} %copy-done, bf16[1024,512]{1,0:T(8,128)(2,1)} %refs_0_.1, bf16[1024,512]{1,0:T(8,128)(2,1)} %collective-permute-done.20.refs_1_, bf16[1024,512]{1,0:T(8,128)(2,1)} %copy-done.1, ...), custom_call_target="tpu_custom_call" | custom-call | tf_op jit(solution)/shard_map/cycle/pallas_call | solution.py:203
  (54 shorter events, 0.2 us)
Async XLA Ops:
  0.0 6.8 %copy-start.7 = (bf16[32,256,4]{1,2,0:T(4,128)(2,1)S(1)}, bf16[32,256,4]{1,2,0:T(4,128)(2,1)}, u32[]{:S(2)}) copy-start(bf16[32,256,4]{1,2,0:T(4,128)(2,1)} %param.9) | copy-start | bytes 196612
  1.9 28.8 %copy-start.4 = (bf16[16,32,512]{2,1,0:T(8,128)(2,1)S(1)}, bf16[16,32,512]{2,1,0:T(8,128)(2,1)}, u32[]{:S(2)}) copy-start(bf16[16,32,512]{2,1,0:T(8,128)(2,1)} %param.8) | copy-start | bytes 1572868
  3.0 32.3 %collective-permute-start = (bf16[32,64,128]{2,1,0:T(8,128)(2,1)}, bf16[32,64,128]{2,1,0:T(8,128)(2,1)S(1)}, u32[]{:S(2)}, u32[]{:S(2)}) collective-permute-start(bf16[32,64,128]{2,1,0:T(8,128)(2,1)} %get-tuple-element.32), channel_id=1, source_target_pairs={{0,0},{1,1},{2,16},{3,17},{16,2},{17,3},{18,18},{19,19},{4,4},{5,5... | collective-permute-start | bytes 1572872 | tf_op jit(solution)/shard_map/ppermute | solution.py:233
  4.7 30.6 %collective-permute-start.1 = (bf16[32,64,128]{2,1,0:T(8,128)(2,1)}, bf16[32,64,128]{2,1,0:T(8,128)(2,1)S(1)}, u32[]{:S(2)}, u32[]{:S(2)}) collective-permute-start(bf16[32,64,128]{2,1,0:T(8,128)(2,1)} %get-tuple-element.31), channel_id=1, source_target_pairs={{0,1},{1,0},{2,17},{3,16},{16,3},{17,2},{18,19},{19,18},{4,5},{5,4... | collective-permute-start | bytes 1572872 | tf_op jit(solution)/shard_map/ppermute | solution.py:233
  29.0 40.8 %copy-start.5 = (bf16[16,32,4,128]{3,2,1,0:T(4,128)(2,1)}, bf16[16,32,4,128]{3,2,1,0:T(4,128)(2,1)S(1)}, u32[]{:S(2)}) copy-start(bf16[16,32,4,128]{3,2,1,0:T(4,128)(2,1)S(1)} %copy.15) | copy-start | bytes 1572868
  29.0 15.3 %collective-permute-start.5 = (bf16[16,128,128]{2,1,0:T(8,128)(2,1)S(1)}, bf16[16,128,128]{2,1,0:T(8,128)(2,1)S(1)}, u32[]{:S(2)}, u32[]{:S(2)}) collective-permute-start(bf16[16,128,128]{2,1,0:T(8,128)(2,1)S(1)} %bitcast.31), channel_id=1, source_target_pairs={{0,32},{32,64},{64,96},{96,0},{1,33},{33,65},{65,97},{97,1},{2,34}... | collective-permute-start | bytes 1572872 | tf_op jit(solution)/shard_map/ppermute | solution.py:20
  31.7 15.3 %collective-permute-start.6 = (bf16[16,128,128]{2,1,0:T(8,128)(2,1)S(1)}, bf16[16,128,128]{2,1,0:T(8,128)(2,1)}, u32[]{:S(2)}, u32[]{:S(2)}) collective-permute-start(bf16[16,128,128]{2,1,0:T(8,128)(2,1)S(1)} %bitcast.32), channel_id=1, source_target_pairs={{0,96},{32,0},{64,32},{96,64},{1,97},{33,1},{65,33},{97,65},{2,98}... | collective-permute-start | bytes 1572872 | tf_op jit(solution)/shard_map/ppermute | solution.py:20
  33.4 24.2 %collective-permute-start.7 = (bf16[16,128,128]{2,1,0:T(8,128)(2,1)S(1)}, bf16[16,128,128]{2,1,0:T(8,128)(2,1)S(1)}, u32[]{:S(2)}, u32[]{:S(2)}) collective-permute-start(bf16[16,128,128]{2,1,0:T(8,128)(2,1)S(1)} %bitcast.33), channel_id=1, source_target_pairs={{0,64},{32,96},{64,0},{96,32},{1,65},{33,97},{65,1},{97,33},{2,66}... | collective-permute-start | bytes 1572872 | tf_op jit(solution)/shard_map/ppermute | solution.py:20
  35.4 0.8 copy-start.2
  35.4 1.0 copy-start.3
  38.9 20.9 %collective-permute-start.14 = (bf16[32,16,512]{2,1,0:T(8,128)(2,1)}, bf16[32,16,512]{2,1,0:T(8,128)(2,1)S(1)}, u32[]{:S(2)}, u32[]{:S(2)}) collective-permute-start(bf16[32,16,512]{2,1,0:T(8,128)(2,1)} %bitcast.24), channel_id=1, source_target_pairs={{0,0},{1,1},{2,16},{3,17},{16,2},{17,3},{18,18},{19,19},{4,4},{5,5... | collective-permute-start | bytes 1572872 | tf_op jit(solution)/shard_map/ppermute | solution.py:248
  40.6 28.6 %collective-permute-start.3 = (bf16[4096,128]{1,0:T(8,128)(2,1)}, bf16[4096,128]{1,0:T(8,128)(2,1)S(1)}, u32[]{:S(2)}, u32[]{:S(2)}) collective-permute-start(bf16[4096,128]{1,0:T(8,128)(2,1)} %turn.1.refs_0_), channel_id=1, source_target_pairs={{0,4},{4,8},{8,12},{12,0},{1,5},{5,9},{9,13},{13,1},{2,6},{6,10},{... | collective-permute-start | bytes 3145736 | tf_op jit(solution)/shard_map/ppermute | solution.py:20
  44.3 2.8 %copy-start.11 = (bf16[16,128,128]{2,1,0:T(8,128)(2,1)}, bf16[16,128,128]{2,1,0:T(8,128)(2,1)S(1)}, u32[]{:S(2)}) copy-start(bf16[16,128,128]{2,1,0:T(8,128)(2,1)S(1)} %collective-permute-done.5.refs_5_) | copy-start | bytes 1572868
  44.3 25.4 %collective-permute-start.4 = (bf16[4096,128]{1,0:T(8,128)(2,1)}, bf16[4096,128]{1,0:T(8,128)(2,1)}, u32[]{:S(2)}, u32[]{:S(2)}) collective-permute-start(bf16[4096,128]{1,0:T(8,128)(2,1)} %turn.1.refs_0_), channel_id=1, source_target_pairs={{0,12},{4,0},{8,4},{12,8},{1,13},{5,1},{9,5},{13,9},{2,14},{6,2},{... | collective-permute-start | bytes 3145736 | tf_op jit(solution)/shard_map/ppermute | solution.py:20
  47.0 32.1 %collective-permute-start.18 = (bf16[1024,512]{1,0:T(8,128)(2,1)}, bf16[1024,512]{1,0:T(8,128)(2,1)S(1)}, u32[]{:S(2)}, u32[]{:S(2)}) collective-permute-start(bf16[1024,512]{1,0:T(8,128)(2,1)} %refs_0_.1), channel_id=1, source_target_pairs={{0,32},{32,64},{64,96},{96,0},{1,33},{33,65},{65,97},{97,1},{2,34}... | collective-permute-start | bytes 3145736 | tf_op jit(solution)/shard_map/ppermute | solution.py:20
  57.6 26.8 %copy-start.12 = (bf16[16,128,128]{2,1,0:T(8,128)(2,1)}, bf16[16,128,128]{2,1,0:T(8,128)(2,1)S(1)}, u32[]{:S(2)}) copy-start(bf16[16,128,128]{2,1,0:T(8,128)(2,1)S(1)} %collective-permute-done.7.refs_7_) | copy-start | bytes 1572868
  57.6 24.0 %collective-permute-start.19 = (bf16[1024,512]{1,0:T(8,128)(2,1)}, bf16[1024,512]{1,0:T(8,128)(2,1)}, u32[]{:S(2)}, u32[]{:S(2)}) collective-permute-start(bf16[1024,512]{1,0:T(8,128)(2,1)} %refs_0_.1), channel_id=1, source_target_pairs={{0,96},{32,0},{64,32},{96,64},{1,97},{33,1},{65,33},{97,65},{2,98}... | collective-permute-start | bytes 3145736 | tf_op jit(solution)/shard_map/ppermute | solution.py:20
  59.8 33.8 %copy-start.13 = (bf16[32,16,512]{2,1,0:T(8,128)(2,1)}, bf16[32,16,512]{2,1,0:T(8,128)(2,1)S(1)}, u32[]{:S(2)}) copy-start(bf16[32,16,512]{2,1,0:T(8,128)(2,1)S(1)} %collective-permute-done.14.refs_0_) | copy-start | bytes 1572868
  59.8 9.4 %collective-permute-start.15 = (bf16[32,16,512]{2,1,0:T(8,128)(2,1)}, bf16[32,16,512]{2,1,0:T(8,128)(2,1)S(1)}, u32[]{:S(2)}, u32[]{:S(2)}) collective-permute-start(bf16[32,16,512]{2,1,0:T(8,128)(2,1)} %bitcast.24), channel_id=1, source_target_pairs={{0,1},{1,0},{2,17},{3,16},{16,3},{17,2},{18,19},{19,18},{4,5},{5,4... | collective-permute-start | bytes 1572872 | tf_op jit(solution)/shard_map/ppermute | solution.py:248
  69.2 24.4 %copy-start.14 = (bf16[32,16,512]{2,1,0:T(8,128)(2,1)}, bf16[32,16,512]{2,1,0:T(8,128)(2,1)S(1)}, u32[]{:S(2)}) copy-start(bf16[32,16,512]{2,1,0:T(8,128)(2,1)S(1)} %collective-permute-done.15.refs_1_) | copy-start | bytes 1572868
  69.2 15.2 %collective-permute-start.16 = (bf16[32,16,512]{2,1,0:T(8,128)(2,1)S(1)}, bf16[32,16,512]{2,1,0:T(8,128)(2,1)S(1)}, u32[]{:S(2)}, u32[]{:S(2)}) collective-permute-start(bf16[32,16,512]{2,1,0:T(8,128)(2,1)S(1)} %collective-permute-done.14.refs_0_), channel_id=1, source_target_pairs={{0,16},{16,0},{1,17},{17,1},{2,18},{18,2},{3,19},{19,3},{4,20},{20... | collective-permute-start | bytes 1572872 | tf_op jit(solution)/shard_map/ppermute | solution.py:24
  69.2 35.7 %copy-start.6 = (bf16[4096,128]{1,0:T(8,128)(2,1)}, bf16[4096,128]{1,0:T(8,128)(2,1)S(1)}, u32[]{:S(2)}) copy-start(bf16[4096,128]{1,0:T(8,128)(2,1)S(1)} %collective-permute-done.3.refs_2_) | copy-start | bytes 3145732
  69.2 15.3 %collective-permute-start.17 = (bf16[32,16,512]{2,1,0:T(8,128)(2,1)S(1)}, bf16[32,16,512]{2,1,0:T(8,128)(2,1)S(1)}, u32[]{:S(2)}, u32[]{:S(2)}) collective-permute-start(bf16[32,16,512]{2,1,0:T(8,128)(2,1)S(1)} %collective-permute-done.15.refs_1_), channel_id=1, source_target_pairs={{0,16},{16,0},{1,17},{17,1},{2,18},{18,2},{3,19},{19,3},{4,20},{20... | collective-permute-start | bytes 1572872 | tf_op jit(solution)/shard_map/ppermute | solution.py:24
  69.7 35.2 %collective-permute-start.2 = (bf16[4096,128]{1,0:T(8,128)(2,1)}, bf16[4096,128]{1,0:T(8,128)(2,1)}, u32[]{:S(2)}, u32[]{:S(2)}) collective-permute-start(bf16[4096,128]{1,0:T(8,128)(2,1)} %turn.1.refs_0_), channel_id=1, source_target_pairs={{0,16},{16,0},{1,17},{17,1},{2,18},{18,2},{3,19},{19,3},{4,20},{20... | collective-permute-start | bytes 3145736 | tf_op jit(solution)/shard_map/ppermute | solution.py:24
  79.2 96.3 %copy-start.1 = (bf16[1024,512]{1,0:T(8,128)(2,1)}, bf16[1024,512]{1,0:T(8,128)(2,1)S(1)}, u32[]{:S(2)}) copy-start(bf16[1024,512]{1,0:T(8,128)(2,1)S(1)} %collective-permute-done.18.refs_2_) | copy-start | bytes 3145732
  79.2 11.2 %collective-permute-start.10 = (bf16[2048,128]{1,0:T(8,128)(2,1)S(1)}, bf16[2048,128]{1,0:T(8,128)(2,1)}, u32[]{:S(2)}, u32[]{:S(2)}) collective-permute-start(bf16[2048,128]{1,0:T(8,128)(2,1)S(1)} %slice.12), channel_id=1, source_target_pairs={{0,4},{4,8},{8,12},{12,0},{1,5},{5,9},{9,13},{13,1},{2,6},{6,10},{... | collective-permute-start | bytes 1572872 | tf_op jit(solution)/shard_map/ppermute | solution.py:20
  81.5 12.0 %collective-permute-start.12 = (bf16[2048,128]{1,0:T(8,128)(2,1)S(1)}, bf16[2048,128]{1,0:T(8,128)(2,1)}, u32[]{:S(2)}, u32[]{:S(2)}) collective-permute-start(bf16[2048,128]{1,0:T(8,128)(2,1)S(1)} %slice.13), channel_id=1, source_target_pairs={{0,12},{4,0},{8,4},{12,8},{1,13},{5,1},{9,5},{13,9},{2,14},{6,2},{... | collective-permute-start | bytes 1572872 | tf_op jit(solution)/shard_map/ppermute | solution.py:20
  84.4 9.2 %copy-start.15 = (bf16[32,16,512]{2,1,0:T(8,128)(2,1)}, bf16[32,16,512]{2,1,0:T(8,128)(2,1)S(1)}, u32[]{:S(2)}) copy-start(bf16[32,16,512]{2,1,0:T(8,128)(2,1)S(1)} %collective-permute-done.16.refs_2_) | copy-start | bytes 1572868
  84.4 20.5 %collective-permute-start.8 = (bf16[4096,128]{1,0:T(8,128)(2,1)S(1)}, bf16[4096,128]{1,0:T(8,128)(2,1)S(1)}, u32[]{:S(2)}, u32[]{:S(2)}) collective-permute-start(bf16[4096,128]{1,0:T(8,128)(2,1)S(1)} %collective-permute-done.3.refs_2_), channel_id=1, source_target_pairs={{0,16},{16,0},{1,17},{17,1},{2,18},{18,2},{3,19},{19,3},{4,20},{20... | collective-permute-start | bytes 3145736 | tf_op jit(solution)/shard_map/ppermute | solution.py:24
  84.5 9.1 %copy-start.16 = (bf16[32,16,512]{2,1,0:T(8,128)(2,1)}, bf16[32,16,512]{2,1,0:T(8,128)(2,1)S(1)}, u32[]{:S(2)}) copy-start(bf16[32,16,512]{2,1,0:T(8,128)(2,1)S(1)} %collective-permute-done.17.refs_3_) | copy-start | bytes 1572868
  84.5 20.4 %collective-permute-start.9 = (bf16[4096,128]{1,0:T(8,128)(2,1)}, bf16[4096,128]{1,0:T(8,128)(2,1)}, u32[]{:S(2)}, u32[]{:S(2)}) collective-permute-start(bf16[4096,128]{1,0:T(8,128)(2,1)} %collective-permute-done.4.refs_4_), channel_id=1, source_target_pairs={{0,16},{16,0},{1,17},{17,1},{2,18},{18,2},{3,19},{19,3},{4,20},{20... | collective-permute-start | bytes 3145736 | tf_op jit(solution)/shard_map/ppermute | solution.py:24
  90.4 14.5 %collective-permute-start.11 = (bf16[2048,128]{1,0:T(8,128)(2,1)}, bf16[2048,128]{1,0:T(8,128)(2,1)}, u32[]{:S(2)}, u32[]{:S(2)}) collective-permute-start(bf16[2048,128]{1,0:T(8,128)(2,1)} %collective-permute-done.10.refs_6_), channel_id=1, source_target_pairs={{0,16},{16,0},{1,17},{17,1},{2,18},{18,2},{3,19},{19,3},{4,20},{20... | collective-permute-start | bytes 1572872 | tf_op jit(solution)/shard_map/ppermute | solution.py:24
  93.6 11.3 %collective-permute-start.13 = (bf16[2048,128]{1,0:T(8,128)(2,1)}, bf16[2048,128]{1,0:T(8,128)(2,1)}, u32[]{:S(2)}, u32[]{:S(2)}) collective-permute-start(bf16[2048,128]{1,0:T(8,128)(2,1)} %collective-permute-done.12.refs_8_), channel_id=1, source_target_pairs={{0,16},{16,0},{1,17},{17,1},{2,18},{18,2},{3,19},{19,3},{4,20},{20... | collective-permute-start | bytes 1572872 | tf_op jit(solution)/shard_map/ppermute | solution.py:24
  104.9 1.0 copy-start.10
  163.3 35.9 %all-to-all-start.2 = ((bf16[16,32,16,128]{3,2,1,0:T(8,128)(2,1)}), bf16[16,32,16,128]{3,2,1,0:T(8,128)(2,1)S(1)}, u32[]{:S(2)}, u32[]{:S(2)}) async-start(bf16[16,32,16,128]{3,2,1,0:T(8,128)(2,1)} %bitcast.27), calls=%async_computation.2 | async-start | bytes 4194304 | tf_op jit(solution)/shard_map/all_to_all | solution.py:269
  169.5 6.5 %copy-start.17 = (f32[256]{0:T(256)S(1)}, f32[256]{0:T(256)}, u32[]{:S(2)}) copy-start(f32[256]{0:T(256)} %param.13) | copy-start | bytes 3076
  169.5 16.5 %copy-start.8 = (f32[32]{0:T(128)S(1)}, f32[32]{0:T(128)}, u32[]{:S(2)}) copy-start(f32[32]{0:T(128)} %param.11) | copy-start | bytes 388
  169.5 17.4 %copy-start.9 = (f32[32]{0:T(128)S(1)}, f32[32]{0:T(128)}, u32[]{:S(2)}) copy-start(f32[32]{0:T(128)} %param.12) | copy-start | bytes 388
  170.3 14.5 %collective-permute-start.23 = (bf16[512,512]{1,0:T(8,128)(2,1)}, bf16[512,512]{1,0:T(8,128)(2,1)}, u32[]{:S(2)}, u32[]{:S(2)}) collective-permute-start(bf16[512,512]{1,0:T(8,128)(2,1)} %slice.14), channel_id=1, source_target_pairs={{0,32},{32,64},{64,96},{96,0},{1,33},{33,65},{65,97},{97,1},{2,34}... | collective-permute-start | bytes 1572872 | tf_op jit(solution)/shard_map/ppermute | solution.py:20
  172.8 13.2 %collective-permute-start.25 = (bf16[512,512]{1,0:T(8,128)(2,1)}, bf16[512,512]{1,0:T(8,128)(2,1)}, u32[]{:S(2)}, u32[]{:S(2)}) collective-permute-start(bf16[512,512]{1,0:T(8,128)(2,1)} %slice.15), channel_id=1, source_target_pairs={{0,96},{32,0},{64,32},{96,64},{1,97},{33,1},{65,33},{97,65},{2,98}... | collective-permute-start | bytes 1572872 | tf_op jit(solution)/shard_map/ppermute | solution.py:20
  175.5 12.9 %collective-permute-start.20 = (bf16[1024,512]{1,0:T(8,128)(2,1)}, bf16[1024,512]{1,0:T(8,128)(2,1)}, u32[]{:S(2)}, u32[]{:S(2)}) collective-permute-start(bf16[1024,512]{1,0:T(8,128)(2,1)} %refs_0_.1), channel_id=1, source_target_pairs={{0,16},{16,0},{1,17},{17,1},{2,18},{18,2},{3,19},{19,3},{4,20},{20... | collective-permute-start | bytes 3145736 | tf_op jit(solution)/shard_map/ppermute | solution.py:24
  175.5 12.9 %collective-permute-start.21 = (bf16[1024,512]{1,0:T(8,128)(2,1)S(1)}, bf16[1024,512]{1,0:T(8,128)(2,1)}, u32[]{:S(2)}, u32[]{:S(2)}) collective-permute-start(bf16[1024,512]{1,0:T(8,128)(2,1)S(1)} %collective-permute-done.18.refs_2_), channel_id=1, source_target_pairs={{0,16},{16,0},{1,17},{17,1},{2,18},{18,2},{3,19},{19,3},{4,20},{20... | collective-permute-start | bytes 3145736 | tf_op jit(solution)/shard_map/ppermute | solution.py:24
  176.0 12.4 %collective-permute-start.22 = (bf16[1024,512]{1,0:T(8,128)(2,1)}, bf16[1024,512]{1,0:T(8,128)(2,1)}, u32[]{:S(2)}, u32[]{:S(2)}) collective-permute-start(bf16[1024,512]{1,0:T(8,128)(2,1)} %collective-permute-done.19.refs_4_), channel_id=1, source_target_pairs={{0,16},{16,0},{1,17},{17,1},{2,18},{18,2},{3,19},{19,3},{4,20},{20... | collective-permute-start | bytes 3145736 | tf_op jit(solution)/shard_map/ppermute | solution.py:24
  184.9 3.4 %collective-permute-start.24 = (bf16[512,512]{1,0:T(8,128)(2,1)}, bf16[512,512]{1,0:T(8,128)(2,1)}, u32[]{:S(2)}, u32[]{:S(2)}) collective-permute-start(bf16[512,512]{1,0:T(8,128)(2,1)} %collective-permute-done.23.refs_6_), channel_id=1, source_target_pairs={{0,16},{16,0},{1,17},{17,1},{2,18},{18,2},{3,19},{19,3},{4,20},{20... | collective-permute-start | bytes 1572872 | tf_op jit(solution)/shard_map/ppermute | solution.py:24
  186.0 2.3 %collective-permute-start.26 = (bf16[512,512]{1,0:T(8,128)(2,1)}, bf16[512,512]{1,0:T(8,128)(2,1)}, u32[]{:S(2)}, u32[]{:S(2)}) collective-permute-start(bf16[512,512]{1,0:T(8,128)(2,1)} %collective-permute-done.25.refs_8_), channel_id=1, source_target_pairs={{0,16},{16,0},{1,17},{17,1},{2,18},{18,2},{3,19},{19,3},{4,20},{20... | collective-permute-start | bytes 1572872 | tf_op jit(solution)/shard_map/ppermute | solution.py:24
  199.2 1.3 copy-start
where the time goes:
time: 208 us; the launch traced here: 207 us
  waiting for transfers between devices  59.3 us (29%)
  blocking collectives  55.9 us (27%)
  Pallas kernels  42.2 us (20%)
  starting transfers between devices  34 us (16%)
  local copies, waits for them, and re-layouts  14 us (7%)
    ppermute x11, waiting for transfers between devices, ring(): return lax.ppermute(value, axis, [(i, (i + shift) % n) for i in range(n)])  39.3 us
    all_to_all x1, blocking collectives, update(): parts = lax.all_to_all(parts, ('y', 'core', 'z'), 0, 0, tiled=True)  34.2 us
    all_to_all x1, blocking collectives, update(): lax.all_to_all(block.reshape(32, na // 2, nq, nc // 2), ('core', 'x', 'z'...  21.7 us
    ppermute x11, starting transfers between devices, ring(): return lax.ppermute(value, axis, [(i, (i + shift) % n) for i in range(n)])  20.5 us
    pallas_call x1, Pallas kernels, partial_ladder(): pl.pallas_call(ladder_kernel, grid_spec=pltpu.PrefetchScalarGridSpec(num_...  19.1 us
    all_to_all x1, waiting for transfers between devices, update(): lax.all_to_all(holes.reshape(16, nj, 16, 128), VIR, 0, 0, tiled=True)  10.8 us
    pallas_call x1, Pallas kernels, form_integrals(): pl.pallas_call(integrals_kernel, grid_spec=pltpu.PrefetchScalarGridSpec(n...  10.6 us
    ppermute x2, waiting for transfers between devices, update(): lax.ppermute(turned, ('core', 'z'), amplitude_route(alpha))  9.14 us
  transfers between devices with their start and end apart: 28, of which 10 were waited for; matrix products, arithmetic and copies ran while one was open for 4% of the time, Pallas kernels for 6%

commit v1 on v0

--- a/solution.py
+++ b/solution.py
@@ -43,17 +43,18 @@
                 ]
 
 
-def form_integrals(where, pairs, blocks):
+def form_integrals(where, pairs, blocks, part, parts):
     nd, nb, naux = pairs[0].shape
     na, nq, nc = blocks[0].shape
-    step = 2
+    na, step = na // parts, 2
+    skip = part * na // step
     return pl.pallas_call(
         integrals_kernel,
         grid_spec=pltpu.PrefetchScalarGridSpec(
             num_scalar_prefetch=1,
             grid=(na // step,),
             in_specs=[pl.BlockSpec((nd, nb, naux), lambda g, w: (0, 0, 0))] * 4
-            + [pl.BlockSpec((step, nq, nc), lambda g, w: (g, 0, 0))] * 4,
+            + [pl.BlockSpec((step, nq, nc), lambda g, w: (g + skip, 0, 0))] * 4,
             out_specs=pl.BlockSpec((step * 4 * nb, nd * nc), lambda g, w: (g, 0)),
             scratch_shapes=[pltpu.VMEM((naux, step * nc), BF16)],
         ),
@@ -87,19 +88,29 @@
 
 
 def ladder_kernel(where_ref, *refs):
-    amps, w_ref, out_ref, turned = refs[:-3], refs[-3], refs[-2], refs[-1]
+    amps, w_ref, out_ref, turned, sems = refs[:-4], refs[-4], refs[-3], refs[-2], refs[-1]
     depth, wide = amps[0].shape
-    j = pl.program_id(1)
-
-    @pl.when((pl.program_id(0) == 0) & (j == 0))
+    g, j = pl.program_id(0), pl.program_id(1)
+
+    def load(n):
+        at = pl.ds(n % 2 * wide, wide)
+        if n < 6:
+            spot = turned.at[n // 2, :, at]
+        else:
+            spot = turned.at[3, pl.ds((n - 6) // 2 * (depth // 2), depth // 2), at]
+        return pltpu.make_async_copy(amps[n], spot, sems.at[n])
+
+    @pl.when((g == 0) & (j == 0))
     def _():
-        for n in range(6):
-            at = n % 2 * wide
-            turned[n // 2, :, at : at + wide] = amps[n][...]
-        for n in range(4):
-            at = n % 2 * wide
-            row = n // 2 * (depth // 2)
-            turned[3, row : row + depth // 2, at : at + wide] = amps[6 + n][...]
+        for n in range(10):
+            load(n).start()
+
+    for chunk in range(4):
+
+        @pl.when((g == 0) & (j == chunk))
+        def _():
+            for n in (2 * chunk, 2 * chunk + 1) if chunk < 3 else range(6, 10):
+                load(n).wait()
 
     got = jnp.dot(w_ref[...], turned[j], preferred_element_type=F32).astype(BF16)
     _, two, nz, na, nb, _ = out_ref.shape
@@ -116,40 +127,44 @@
 def partial_ladder(where, amps, w):
     wide = amps[0].shape[1]
     nrow, depth = w.shape
-    step, nz, nb = 512, 4, 16
+    step, nz, nb = 256, 4, 16
     na = step // (nz * nb)
     return pl.pallas_call(
         ladder_kernel,
         grid_spec=pltpu.PrefetchScalarGridSpec(
             num_scalar_prefetch=1,
             grid=(nrow // step, 4),
-            in_specs=[pl.BlockSpec(v.shape, lambda g, j, h: (0, 0)) for v in amps]
+            in_specs=[pl.BlockSpec(memory_space=pl.ANY) for _ in amps]
             + [pl.BlockSpec((step, depth), lambda g, j, h: (g, 0))],
             out_specs=pl.BlockSpec(
                 (1, 2, nz, na, nb, wide), lambda g, j, h: (h[j], 0, 0, g, 0, 0)
             ),
-            scratch_shapes=[pltpu.VMEM((4, depth, 2 * wide), BF16)],
+            scratch_shapes=[
+                pltpu.VMEM((4, depth, 2 * wide), BF16),
+                pltpu.SemaphoreType.DMA((len(amps),)),
+            ],
         ),
         out_shape=jax.ShapeDtypeStruct((4, 2, nz, nrow // (nz * nb), nb, wide), BF16),
         cost_estimate=pl.CostEstimate(
-            flops=16 * nrow * depth * wide, bytes_accessed=18 << 20, transcendentals=0
+            flops=16 * nrow * depth * wide, bytes_accessed=14 << 20, transcendentals=0
         ),
         name="ladder",
     )(where, *amps, w)
 
 
-def settle_kernel(parts_ref, direct_ref, holes_ref, total, swapped):
-    ny, two, nz, part, wide = parts_ref.shape
-    rows = two * part
+def settle_kernel(first_ref, second_ref, direct_ref, holes_ref, total, swapped):
+    ny, two, nz, part, wide = first_ref.shape
+    rows = 2 * two * part
     nb = 16
     na = rows // nb
     ni = wide // na
     nj = wide // ni
-    for h in range(two):
-        acc = parts_ref[0, h, 0].astype(F32)
+    for n in range(2 * two):
+        h, ref = n // 2, (first_ref, second_ref)[n % 2]
+        acc = ref[0, h, 0].astype(F32)
         for p in range(1, ny * nz):
-            acc = acc + parts_ref[p // nz, h, p % nz].astype(F32)
-        total[h * part : (h + 1) * part] = acc
+            acc = acc + ref[p // nz, h, p % nz].astype(F32)
+        total[n * part : (n + 1) * part] = acc
     per = wide // nj
     for group in range(nb // per):
         blocks = [total[pl.ds(group * per + k, na, stride=nb), :] for k in range(per)]
@@ -167,8 +182,8 @@
         holes_ref[p] = held
 
 
-def settle(parts):
-    rows, wide = parts.shape[1] * parts.shape[3], parts.shape[4]
+def settle(first, second):
+    rows, wide = 2 * first.shape[1] * first.shape[3], first.shape[4]
     return pl.pallas_call(
         settle_kernel,
         out_shape=(
@@ -177,7 +192,7 @@
         ),
         scratch_shapes=[pltpu.VMEM((rows, wide), F32), pltpu.VMEM((rows, wide), F32)],
         name="settle",
-    )(parts)
+    )(first, second)
 
 
 def cycle_kernel(where_ref, holes_ref, *refs):
@@ -252,20 +267,24 @@
     mid = own.shape[0] // 2
     far = [ring(left[:mid], "x", 1), ring(right[mid:], "x", -1)]
     pair += [sibling(v) for v in pair]
-    amps = []
-    for v in (own, left, right):
+    amps = [own, sibling(own)]
+    for v in (left, right, *far):
         amps += [v, sibling(v)]
-    for v in far:
-        amps += [v, sibling(v)]
-
-    w = form_integrals(scalars(y), pair, blocks)
+
+    w = form_integrals(scalars(y), pair, blocks, 0, 2)
     w, before, after = lax.optimization_barrier((w, before, after))
 
     spots = scalars(x, (x + 3) % 4, (x + 1) % 4, (x + 2) % 4, core, 2 * core + half)
-    parts = partial_ladder(spots, amps, w)
-    parts = parts.reshape(32, -1, parts.shape[-1])
-    parts = lax.all_to_all(parts, ("y", "core", "z"), 0, 0, tiled=True)
-    direct, holes = settle(parts.reshape(4, 2, 4, -1, parts.shape[-1]))
+
+    def exchanged(parts):
+        parts = parts.reshape(32, -1, parts.shape[-1])
+        parts = lax.all_to_all(parts, ("y", "core", "z"), 0, 0, tiled=True)
+        return parts.reshape(4, 2, 4, -1, parts.shape[-1])
+
+    first = exchanged(partial_ladder(spots, amps, w))
+    w = form_integrals(scalars(y), pair, blocks, 1, 2)
+    second = exchanged(partial_ladder(spots, amps, w))
+    direct, holes = settle(first, second)
     holes = lax.all_to_all(holes.reshape(16, nj, 16, 128), VIR, 0, 0, tiled=True)
 
     mid = cycle_matrix.shape[0] // 2

time: 208 us -> 196 us (0.942)
  blocking collectives: 55.9 us -> 24.5 us
  starting transfers between devices: 34 us -> 63.6 us
  waiting for transfers between devices: 59.3 us -> 41.6 us
  Pallas kernels: 42.2 us -> 48.4 us
    all_to_all x2 -> x1, blocking collectives: 55.9 us -> 24.5 us  [exchanged(): parts = lax.all_to_all(parts, ('y', 'core', 'z'), 0, 0, tiled=True)]
    ppermute x11, waiting for transfers between devices: 39.3 us -> 20.4 us  [ring(): return lax.ppermute(value, axis, [(i, (i + shift) % n) for i in range(n)])]
    ppermute x12, starting transfers between devices: 1.76 us -> 19.1 us  [sibling(): return lax.ppermute(value, 'core', [(0, 1), (1, 0)])]
    all_to_all x0 -> x2, starting transfers between devices: none -> 13.3 us  [the longest x1 8.41 us: update(): lax.all_to_all(block.reshape(32, na // 2, nq, nc // 2), ('core', 'x', 'z'...]
    ppermute x2, waiting for transfers between devices: 9.14 us -> 0.01 us  [update(): lax.ppermute(turned, ('core', 'z'), amplitude_route(alpha))]
    all_to_all x0 -> x2, waiting for transfers between devices: none -> 5.52 us  [the longest x1 5.52 us: update(): lax.all_to_all(block.reshape(32, na // 2, nq, nc // 2), ('core', 'x', 'z'...]
    ppermute x2, waiting for transfers between devices: 0.01 us -> 4.71 us  [update(): lax.ppermute(lax.dynamic_slice_in_dim(flat, (half ^ alpha) * (nc // 2), n...]
    pallas_call x1 -> x2, Pallas kernels: 19.1 us -> 23.1 us  [partial_ladder(): pl.pallas_call(ladder_kernel, grid_spec=pltpu.PrefetchScalarGridSpec(num_...]
  transfers between devices with their start and end apart: 28 -> 30, of which waited for: 10 -> 8; matrix products, arithmetic and copies ran while one was open for 4% -> 6% of each run, Pallas kernels for 6% -> 20%
where the time goes in v1:
time: 196 us; the launch traced here: 195 us
  starting transfers between devices  63.6 us (32%)
  Pallas kernels  48.4 us (25%)
  waiting for transfers between devices  41.6 us (21%)
  blocking collectives  24.5 us (12%)
  local copies, waits for them, and re-layouts  15.5 us (8%)
    all_to_all x1, blocking collectives, exchanged(): parts = lax.all_to_all(parts, ('y', 'core', 'z'), 0, 0, tiled=True)  24.5 us
    pallas_call x2, Pallas kernels, partial_ladder(): pl.pallas_call(ladder_kernel, grid_spec=pltpu.PrefetchScalarGridSpec(num_...  23.1 us
    ppermute x11, waiting for transfers between devices, ring(): return lax.ppermute(value, axis, [(i, (i + shift) % n) for i in range(n)])  20.4 us
    ppermute x11, starting transfers between devices, ring(): return lax.ppermute(value, axis, [(i, (i + shift) % n) for i in range(n)])  19.6 us
    ppermute x12, starting transfers between devices, sibling(): return lax.ppermute(value, 'core', [(0, 1), (1, 0)])  19.1 us
    pallas_call x2, Pallas kernels, form_integrals(): pl.pallas_call(integrals_kernel, grid_spec=pltpu.PrefetchScalarGridSpec(n...  12.8 us
    all_to_all x1, waiting for transfers between devices, update(): lax.all_to_all(holes.reshape(16, nj, 16, 128), VIR, 0, 0, tiled=True)  10.9 us
    all_to_all x1, starting transfers between devices, update(): lax.all_to_all(block.reshape(32, na // 2, nq, nc // 2), ('core', 'x', 'z'...  8.41 us
  transfers between devices with their start and end apart: 30, of which 8 were waited for; matrix products, arithmetic and copies ran while one was open for 6% of the time, Pallas kernels for 20%

profile of v1, /device:TPU:0, one launch (start us, length us, event | category | flops | bytes accessed | tf_op | source)
XLA Modules:
  0.0 194.6 jit_solution(12881829195583418049)
XLA Ops:
  0.0 0.9 reshape.79
  0.9 1.1 broadcast_in_dim.2
  2.0 8.4 %all-to-all-start = ((bf16[32,16,4,128]{3,2,1,0:T(4,128)(2,1)}), bf16[32,16,4,128]{3,2,1,0:T(4,128)(2,1)S(1)}, u32[]{:S(2)}, u32[]{:S(2)}) async-start(bf16[32,16,4,128]{3,2,1,0:T(4,128)(2,1)} %bitcast.13), calls=%async_computation | async-start | bytes 1048576 | tf_op jit(solution)/shard_map/all_to_all | solution.py:241
  10.4 1.8 copy.13
  12.2 1.2 dynamic-slice_bitcast_fusion
  13.4 1.7 collective-permute-start
  15.1 1.8 collective-permute-start.1
  16.9 5.5 %all-to-all-done = bf16[32,16,4,128]{3,2,1,0:T(4,128)(2,1)S(1)} async-done(((bf16[32,16,4,128]{3,2,1,0:T(4,128)(2,1)}), bf16[32,16,4,128]{3,2,1,0:T(4,128)(2,1)S(1)}, u32[]{:S(2)}, u32[]{:S(2)}) %all-to-all-start) | async-done | bytes 524320 | tf_op jit(solution)/shard_map/all_to_all | solution.py:241
  22.4 0.2 copy.15
  22.7 1.6 collective-permute-start.5
  24.3 1.7 collective-permute-start.6
  26.0 4.7 %collective-permute-done.1.one_ref = bf16[32,64,128]{2,1,0:T(8,128)(2,1)S(1)} collective-permute-done((bf16[32,64,128]{2,1,0:T(8,128)(2,1)}, bf16[32,64,128]{2,1,0:T(8,128)(2,1)S(1)}, u32[]{:S(2)}, u32[]{:S(2)}) %collective-permute-start.1) | collective-permute-done | bytes 524320 | tf_op jit(solution)/shard_map/ppermute | solution.py:248
  30.7 0.8 copy-done.13
  31.5 2.5 %turn.1.refs_0_ = bf16[4096,128]{1,0:T(8,128)(2,1)} custom-call(s32[1]{0:T(128)} %bitcast.8.where_ref, bf16[32,64,128]{2,1,0:T(8,128)(2,1)} %copy-done.12, bf16[32,64,128]{2,1,0:T(8,128)(2,1)} %copy-done.13), custom_call_target="tpu_custom_call" | custom-call | tf_op jit(solution)/shard_map/turn/pallas_call | solution.py:80
  34.0 1.5 collective-permute-start.3
  35.5 1.8 collective-permute-start.4
  37.2 0.3 copy.18
  37.5 0.7 collective-permute-start.14
  38.3 1.3 collective-permute-start.15
  39.6 3.2 %collective-permute-start.7 = (bf16[16,128,128]{2,1,0:T(8,128)(2,1)S(1)}, bf16[16,128,128]{2,1,0:T(8,128)(2,1)S(1)}, u32[]{:S(2)}, u32[]{:S(2)}) collective-permute-start(bf16[16,128,128]{2,1,0:T(8,128)(2,1)S(1)} %bitcast.29), channel_id=1, source_target_pairs={{0,64},{32,96},{64,0},{96,32},{1,65},{33,97},{65,1},{97,33},{2,66}... | collective-permute-start | bytes 1572872 | tf_op jit(solution)/shard_map/ppermute | solution.py:20
  42.8 11.4 %collective-permute-start.16 = (bf16[32,16,512]{2,1,0:T(8,128)(2,1)S(1)}, bf16[32,16,512]{2,1,0:T(8,128)(2,1)S(1)}, u32[]{:S(2)}, u32[]{:S(2)}) collective-permute-start(bf16[32,16,512]{2,1,0:T(8,128)(2,1)S(1)} %collective-permute-done.14.refs_0_), channel_id=1, source_target_pairs={{0,16},{16,0},{1,17},{17,1},{2,18},{18,2},{3,19},{19,3},{4,20},{20... | collective-permute-start | bytes 1572872 | tf_op jit(solution)/shard_map/ppermute | solution.py:24
  54.2 4.5 %collective-permute-start.17 = (bf16[32,16,512]{2,1,0:T(8,128)(2,1)S(1)}, bf16[32,16,512]{2,1,0:T(8,128)(2,1)S(1)}, u32[]{:S(2)}, u32[]{:S(2)}) collective-permute-start(bf16[32,16,512]{2,1,0:T(8,128)(2,1)S(1)} %collective-permute-done.15.refs_1_), channel_id=1, source_target_pairs={{0,16},{16,0},{1,17},{17,1},{2,18},{18,2},{3,19},{19,3},{4,20},{20... | collective-permute-start | bytes 1572872 | tf_op jit(solution)/shard_map/ppermute | solution.py:24
  58.7 0.1 collective-permute-start.2
  58.8 0.7 copy-done.9
  59.5 0.7 collective-permute-done.4.refs_4_
  60.1 1.1 slice.12
  61.2 0.1 collective-permute-start.10
  61.3 1.1 slice.13
  62.4 3.3 %collective-permute-start.12 = (bf16[2048,128]{1,0:T(8,128)(2,1)S(1)}, bf16[2048,128]{1,0:T(8,128)(2,1)}, u32[]{:S(2)}, u32[]{:S(2)}) collective-permute-start(bf16[2048,128]{1,0:T(8,128)(2,1)S(1)} %slice.13), channel_id=1, source_target_pairs={{0,12},{4,0},{8,4},{12,8},{1,13},{5,1},{9,5},{13,9},{2,14},{6,2},{... | collective-permute-start | bytes 1572872 | tf_op jit(solution)/shard_map/ppermute | solution.py:20
  65.7 1.1 collective-permute-start.8
  66.7 0.7 collective-permute-start.9
  67.5 0.1 copy-done.11
  67.5 9.2 %collective-permute-done.10.refs_6_ = bf16[2048,128]{1,0:T(8,128)(2,1)S(1)} collective-permute-done((bf16[2048,128]{1,0:T(8,128)(2,1)S(1)}, bf16[2048,128]{1,0:T(8,128)(2,1)S(1)}, u32[]{:S(2)}, u32[]{:S(2)}) %collective-permute-start.10) | collective-permute-done | bytes 524320 | tf_op jit(solution)/shard_map/ppermute | solution.py:20
  76.7 0.4 collective-permute-start.11
  77.1 0.6 collective-permute-done.12.refs_8_
  77.7 0.4 collective-permute-start.13
  78.1 0.7 stack.41.where_ref
  78.8 1.9 collective-permute-start.18
  80.6 1.4 collective-permute-start.19
  82.1 6.4 %integrals.3.refs_10_ = bf16[512,4096]{1,0:T(8,128)(2,1)} custom-call(s32[1]{0:T(128)} %bitcast.where_ref, bf16[32,16,512]{2,1,0:T(8,128)(2,1)} %copy-done.7, bf16[32,16,512]{2,1,0:T(8,128)(2,1)} %copy-done.8, bf16[32,16,512]{2,1,0:T(8,128)(2,1)} %copy-done.10, bf16[32,16,512]{2,1,0:T(8,128)(2,1)} %copy-done.11, bf16[16,128,128]{2,1,0:T(8,128)(2,1)} %bitcast.30, ...), custom_call_target="tpu_custom_call" | custom-call | flops 2147483648 | bytes 12582912 | tf_op jit(solution)/shard_map/integrals/pallas_call | solution.py:51
  88.5 11.5 %ladder.3 = bf16[4,2,4,8,16,128]{5,4,3,2,1,0:T(8,128)(2,1)} custom-call(s32[6]{0:T(128)} %stack.41.where_ref, bf16[4096,128]{1,0:T(8,128)(2,1)} %turn.1.refs_0_, bf16[4096,128]{1,0:T(8,128)(2,1)} %collective-permute-done.2.refs_1_, bf16[4096,128]{1,0:T(8,128)(2,1)} %collective-permute-done.3.refs_2_, bf16[4096,128]{1,0:T(8,128)(2,1)} %collective-permute-done.8.refs_3_, ...), custom_call_target="tpu_custom_call" | custom-call | flops 4294967296 | bytes 14680064 | tf_op jit(solution)/shard_map/ladder/pallas_call | solution.py:132
  100.0 4.9 %all-to-all-start.2 = ((bf16[32,128,128]{2,1,0:T(8,128)(2,1)}), bf16[32,128,128]{2,1,0:T(8,128)(2,1)S(1)}, u32[]{:S(2)}, u32[]{:S(2)}) async-start(bf16[32,128,128]{2,1,0:T(8,128)(2,1)} %bitcast.37), calls=%async_computation.2 | async-start | bytes 2097152 | tf_op jit(solution)/shard_map/all_to_all | solution.py:281
  105.0 6.4 %integrals.2.refs_10_ = bf16[512,4096]{1,0:T(8,128)(2,1)} custom-call(s32[1]{0:T(128)} %bitcast.where_ref, bf16[32,16,512]{2,1,0:T(8,128)(2,1)} %copy-done.7, bf16[32,16,512]{2,1,0:T(8,128)(2,1)} %copy-done.8, bf16[32,16,512]{2,1,0:T(8,128)(2,1)} %copy-done.10, bf16[32,16,512]{2,1,0:T(8,128)(2,1)} %copy-done.11, bf16[16,128,128]{2,1,0:T(8,128)(2,1)} %bitcast.31, ...), custom_call_target="tpu_custom_call" | custom-call | flops 2147483648 | bytes 12582912 | tf_op jit(solution)/shard_map/integrals/pallas_call | solution.py:51
  111.4 11.5 %ladder.2 = bf16[4,2,4,8,16,128]{5,4,3,2,1,0:T(8,128)(2,1)} custom-call(s32[6]{0:T(128)} %stack.41.where_ref, bf16[4096,128]{1,0:T(8,128)(2,1)} %turn.1.refs_0_, bf16[4096,128]{1,0:T(8,128)(2,1)} %collective-permute-done.2.refs_1_, bf16[4096,128]{1,0:T(8,128)(2,1)} %collective-permute-done.3.refs_2_, bf16[4096,128]{1,0:T(8,128)(2,1)} %collective-permute-done.8.refs_3_, ...), custom_call_target="tpu_custom_call" | custom-call | flops 4294967296 | bytes 14680064 | tf_op jit(solution)/shard_map/ladder/pallas_call | solution.py:132
  122.9 24.5 %all_to_all.20 = bf16[32,128,128]{2,1,0:T(8,128)(2,1)} all-to-all(bf16[32,128,128]{2,1,0:T(8,128)(2,1)} %bitcast.38), channel_id=1, replica_groups=mesh['y'=4,'core'=2,'x'=4,'z'=4] {'y','core','z'}, dimensions={0} | all-to-all | bytes 2097152 | tf_op jit(solution)/shard_map/all_to_all | solution.py:281
  147.5 4.0 %settle.1 = (f32[128,512]{1,0:T(8,128)}, bf16[16,512,128]{2,1,0:T(8,128)(2,1)}) custom-call(bf16[4,2,4,128,128]{4,3,2,1,0:T(8,128)(2,1)} %bitcast.33, bf16[4,2,4,128,128]{4,3,2,1,0:T(8,128)(2,1)} %bitcast.32), custom_call_target="tpu_custom_call" | custom-call | tf_op jit(solution)/shard_map/settle/pallas_call | solution.py:187
  151.5 6.1 %all-to-all-start.3 = ((bf16[16,32,16,128]{3,2,1,0:T(8,128)(2,1)}), bf16[16,32,16,128]{3,2,1,0:T(8,128)(2,1)S(1)}, u32[]{:S(2)}, u32[]{:S(2)}) async-start(bf16[16,32,16,128]{3,2,1,0:T(8,128)(2,1)} %bitcast.35), calls=%async_computation.3 | async-start | bytes 4194304 | tf_op jit(solution)/shard_map/all_to_all | solution.py:288
  157.6 0.8 slice.14
  158.4 0.6 collective-permute-start.23
  159.0 1.9 slice.15
  160.9 2.6 %collective-permute-start.25 = (bf16[512,512]{1,0:T(8,128)(2,1)}, bf16[512,512]{1,0:T(8,128)(2,1)}, u32[]{:S(2)}, u32[]{:S(2)}) collective-permute-start(bf16[512,512]{1,0:T(8,128)(2,1)} %slice.15), channel_id=1, source_target_pairs={{0,96},{32,0},{64,32},{96,64},{1,97},{33,1},{65,33},{97,65},{2,98}... | collective-permute-start | bytes 1572872 | tf_op jit(solution)/shard_map/ppermute | solution.py:20
  163.5 0.5 collective-permute-start.21
  164.0 0.1 dynamic_slice.15
  164.1 8.8 %collective-permute-done.23.refs_6_ = bf16[512,512]{1,0:T(8,128)(2,1)} collective-permute-done((bf16[512,512]{1,0:T(8,128)(2,1)}, bf16[512,512]{1,0:T(8,128)(2,1)}, u32[]{:S(2)}, u32[]{:S(2)}) %collective-permute-start.23) | collective-permute-done | bytes 524320 | tf_op jit(solution)/shard_map/ppermute | solution.py:20
  172.9 1.1 collective-permute-done.25.refs_8_
  174.1 0.1 broadcast_subtract_fusion
  174.2 0.7 sub.53.refs_12_
  174.8 0.1 dynamic_slice.14
  174.9 0.1 broadcast_subtract_fusion.1
  175.0 0.7 sub.54.refs_11_
  175.7 0.6 pad_add_fusion.where_ref
  176.3 10.9 %all-to-all-done.3.holes_ref = bf16[16,32,16,128]{3,2,1,0:T(8,128)(2,1)S(1)} async-done(((bf16[16,32,16,128]{3,2,1,0:T(8,128)(2,1)}), bf16[16,32,16,128]{3,2,1,0:T(8,128)(2,1)S(1)}, u32[]{:S(2)}, u32[]{:S(2)}) %all-to-all-start.3) | async-done | bytes 2097184 | tf_op jit(solution)/shard_map/all_to_all | solution.py:288
  187.3 1.3 copy-done
  188.6 6.0 %cycle.1 = f32[128,512]{1,0:T(8,128)} custom-call(s32[2]{0:T(128)} %pad_add_fusion.where_ref, bf16[16,32,16,128]{3,2,1,0:T(8,128)(2,1)} %copy-done, bf16[1024,512]{1,0:T(8,128)(2,1)} %refs_0_.1, bf16[1024,512]{1,0:T(8,128)(2,1)} %collective-permute-done.20.refs_1_, bf16[1024,512]{1,0:T(8,128)(2,1)} %copy-done.3, ...), custom_call_target="tpu_custom_call" | custom-call | tf_op jit(solution)/shard_map/cycle/pallas_call | solution.py:218
  (61 shorter events, 0.2 us)
Async XLA Ops:
  2.0 35.3 %copy-start.14 = (bf16[16,32,512]{2,1,0:T(8,128)(2,1)S(1)}, bf16[16,32,512]{2,1,0:T(8,128)(2,1)}, u32[]{:S(2)}) copy-start(bf16[16,32,512]{2,1,0:T(8,128)(2,1)} %param.8) | copy-start | bytes 1572868
  2.0 20.5 %all-to-all-start = ((bf16[32,16,4,128]{3,2,1,0:T(4,128)(2,1)}), bf16[32,16,4,128]{3,2,1,0:T(4,128)(2,1)S(1)}, u32[]{:S(2)}, u32[]{:S(2)}) async-start(bf16[32,16,4,128]{3,2,1,0:T(4,128)(2,1)} %bitcast.13), calls=%async_computation | async-start | bytes 1048576 | tf_op jit(solution)/shard_map/all_to_all | solution.py:241
  13.4 12.6 %collective-permute-start = (bf16[32,64,128]{2,1,0:T(8,128)(2,1)}, bf16[32,64,128]{2,1,0:T(8,128)(2,1)S(1)}, u32[]{:S(2)}, u32[]{:S(2)}) collective-permute-start(bf16[32,64,128]{2,1,0:T(8,128)(2,1)} %get-tuple-element.32), channel_id=1, source_target_pairs={{0,0},{1,1},{2,16},{3,17},{16,2},{17,3},{18,18},{19,19},{4,4},{5,5... | collective-permute-start | bytes 1572872 | tf_op jit(solution)/shard_map/ppermute | solution.py:248
  15.1 15.6 %collective-permute-start.1 = (bf16[32,64,128]{2,1,0:T(8,128)(2,1)}, bf16[32,64,128]{2,1,0:T(8,128)(2,1)S(1)}, u32[]{:S(2)}, u32[]{:S(2)}) collective-permute-start(bf16[32,64,128]{2,1,0:T(8,128)(2,1)} %get-tuple-element.31), channel_id=1, source_target_pairs={{0,1},{1,0},{2,17},{3,16},{16,3},{17,2},{18,19},{19,18},{4,5},{5,4... | collective-permute-start | bytes 1572872 | tf_op jit(solution)/shard_map/ppermute | solution.py:248
  22.7 59.4 %copy-start.1 = (bf16[16,32,4,128]{3,2,1,0:T(4,128)(2,1)}, bf16[16,32,4,128]{3,2,1,0:T(4,128)(2,1)S(1)}, u32[]{:S(2)}) copy-start(bf16[16,32,4,128]{3,2,1,0:T(4,128)(2,1)S(1)} %copy.15) | copy-start | bytes 1572868
  22.7 15.6 %collective-permute-start.5 = (bf16[16,128,128]{2,1,0:T(8,128)(2,1)S(1)}, bf16[16,128,128]{2,1,0:T(8,128)(2,1)S(1)}, u32[]{:S(2)}, u32[]{:S(2)}) collective-permute-start(bf16[16,128,128]{2,1,0:T(8,128)(2,1)S(1)} %bitcast.27), channel_id=1, source_target_pairs={{0,32},{32,64},{64,96},{96,0},{1,33},{33,65},{65,97},{97,1},{2,34}... | collective-permute-start | bytes 1572872 | tf_op jit(solution)/shard_map/ppermute | solution.py:20
  24.3 15.2 %collective-permute-start.6 = (bf16[16,128,128]{2,1,0:T(8,128)(2,1)S(1)}, bf16[16,128,128]{2,1,0:T(8,128)(2,1)S(1)}, u32[]{:S(2)}, u32[]{:S(2)}) collective-permute-start(bf16[16,128,128]{2,1,0:T(8,128)(2,1)S(1)} %bitcast.28), channel_id=1, source_target_pairs={{0,96},{32,0},{64,32},{96,64},{1,97},{33,1},{65,33},{97,65},{2,98}... | collective-permute-start | bytes 1572872 | tf_op jit(solution)/shard_map/ppermute | solution.py:20
  26.0 4.7 %copy-start.12 = (bf16[32,64,128]{2,1,0:T(8,128)(2,1)}, bf16[32,64,128]{2,1,0:T(8,128)(2,1)S(1)}, u32[]{:S(2)}) copy-start(bf16[32,64,128]{2,1,0:T(8,128)(2,1)S(1)} %collective-permute-done.zero_ref) | copy-start | bytes 1572868
  30.7 0.8 copy-start.13
  34.0 25.5 %collective-permute-start.3 = (bf16[4096,128]{1,0:T(8,128)(2,1)}, bf16[4096,128]{1,0:T(8,128)(2,1)}, u32[]{:S(2)}, u32[]{:S(2)}) collective-permute-start(bf16[4096,128]{1,0:T(8,128)(2,1)} %turn.1.refs_0_), channel_id=1, source_target_pairs={{0,4},{4,8},{8,12},{12,0},{1,5},{5,9},{9,13},{13,1},{2,6},{6,10},{... | collective-permute-start | bytes 3145736 | tf_op jit(solution)/shard_map/ppermute | solution.py:20
  35.5 24.7 %collective-permute-start.4 = (bf16[4096,128]{1,0:T(8,128)(2,1)}, bf16[4096,128]{1,0:T(8,128)(2,1)}, u32[]{:S(2)}, u32[]{:S(2)}) collective-permute-start(bf16[4096,128]{1,0:T(8,128)(2,1)} %turn.1.refs_0_), channel_id=1, source_target_pairs={{0,12},{4,0},{8,4},{12,8},{1,13},{5,1},{9,5},{13,9},{2,14},{6,2},{... | collective-permute-start | bytes 3145736 | tf_op jit(solution)/shard_map/ppermute | solution.py:20
  37.5 5.2 %collective-permute-start.14 = (bf16[32,16,512]{2,1,0:T(8,128)(2,1)S(1)}, bf16[32,16,512]{2,1,0:T(8,128)(2,1)S(1)}, u32[]{:S(2)}, u32[]{:S(2)}) collective-permute-start(bf16[32,16,512]{2,1,0:T(8,128)(2,1)S(1)} %bitcast.39), channel_id=1, source_target_pairs={{0,0},{1,1},{2,16},{3,17},{16,2},{17,3},{18,18},{19,19},{4,4},{5,5... | collective-permute-start | bytes 1572872 | tf_op jit(solution)/shard_map/ppermute | solution.py:263
  38.3 43.8 %copy-start.5 = (bf16[16,128,128]{2,1,0:T(8,128)(2,1)}, bf16[16,128,128]{2,1,0:T(8,128)(2,1)S(1)}, u32[]{:S(2)}) copy-start(bf16[16,128,128]{2,1,0:T(8,128)(2,1)S(1)} %collective-permute-done.5.refs_5_) | copy-start | bytes 1572868
  38.3 15.9 %collective-permute-start.15 = (bf16[32,16,512]{2,1,0:T(8,128)(2,1)S(1)}, bf16[32,16,512]{2,1,0:T(8,128)(2,1)S(1)}, u32[]{:S(2)}, u32[]{:S(2)}) collective-permute-start(bf16[32,16,512]{2,1,0:T(8,128)(2,1)S(1)} %bitcast.40), channel_id=1, source_target_pairs={{0,1},{1,0},{2,17},{3,16},{16,3},{17,2},{18,19},{19,18},{4,5},{5,4... | collective-permute-start | bytes 1572872 | tf_op jit(solution)/shard_map/ppermute | solution.py:263
  39.5 41.1 %copy-start.6 = (bf16[16,128,128]{2,1,0:T(8,128)(2,1)}, bf16[16,128,128]{2,1,0:T(8,128)(2,1)S(1)}, u32[]{:S(2)}) copy-start(bf16[16,128,128]{2,1,0:T(8,128)(2,1)S(1)} %collective-permute-done.6.refs_6_) | copy-start | bytes 1572868
  39.6 19.1 %collective-permute-start.7 = (bf16[16,128,128]{2,1,0:T(8,128)(2,1)S(1)}, bf16[16,128,128]{2,1,0:T(8,128)(2,1)S(1)}, u32[]{:S(2)}, u32[]{:S(2)}) collective-permute-start(bf16[16,128,128]{2,1,0:T(8,128)(2,1)S(1)} %bitcast.29), channel_id=1, source_target_pairs={{0,64},{32,96},{64,0},{96,32},{1,65},{33,97},{65,1},{97,33},{2,66}... | collective-permute-start | bytes 1572872 | tf_op jit(solution)/shard_map/ppermute | solution.py:20
  42.7 15.9 %copy-start.7 = (bf16[32,16,512]{2,1,0:T(8,128)(2,1)}, bf16[32,16,512]{2,1,0:T(8,128)(2,1)S(1)}, u32[]{:S(2)}) copy-start(bf16[32,16,512]{2,1,0:T(8,128)(2,1)S(1)} %collective-permute-done.14.refs_0_) | copy-start | bytes 1572868
  42.8 22.9 %collective-permute-start.16 = (bf16[32,16,512]{2,1,0:T(8,128)(2,1)S(1)}, bf16[32,16,512]{2,1,0:T(8,128)(2,1)S(1)}, u32[]{:S(2)}, u32[]{:S(2)}) collective-permute-start(bf16[32,16,512]{2,1,0:T(8,128)(2,1)S(1)} %collective-permute-done.14.refs_0_), channel_id=1, source_target_pairs={{0,16},{16,0},{1,17},{17,1},{2,18},{18,2},{3,19},{19,3},{4,20},{20... | collective-permute-start | bytes 1572872 | tf_op jit(solution)/shard_map/ppermute | solution.py:24
  54.2 11.5 %copy-start.8 = (bf16[32,16,512]{2,1,0:T(8,128)(2,1)}, bf16[32,16,512]{2,1,0:T(8,128)(2,1)S(1)}, u32[]{:S(2)}) copy-start(bf16[32,16,512]{2,1,0:T(8,128)(2,1)S(1)} %collective-permute-done.15.refs_1_) | copy-start | bytes 1572868
  54.2 12.6 %collective-permute-start.17 = (bf16[32,16,512]{2,1,0:T(8,128)(2,1)S(1)}, bf16[32,16,512]{2,1,0:T(8,128)(2,1)S(1)}, u32[]{:S(2)}, u32[]{:S(2)}) collective-permute-start(bf16[32,16,512]{2,1,0:T(8,128)(2,1)S(1)} %collective-permute-done.15.refs_1_), channel_id=1, source_target_pairs={{0,16},{16,0},{1,17},{17,1},{2,18},{18,2},{3,19},{19,3},{4,20},{20... | collective-permute-start | bytes 1572872 | tf_op jit(solution)/shard_map/ppermute | solution.py:24
  58.7 0.8 copy-start.9
  58.7 20.1 %collective-permute-start.2 = (bf16[4096,128]{1,0:T(8,128)(2,1)}, bf16[4096,128]{1,0:T(8,128)(2,1)}, u32[]{:S(2)}, u32[]{:S(2)}) collective-permute-start(bf16[4096,128]{1,0:T(8,128)(2,1)} %turn.1.refs_0_), channel_id=1, source_target_pairs={{0,16},{16,0},{1,17},{17,1},{2,18},{18,2},{3,19},{19,3},{4,20},{20... | collective-permute-start | bytes 3145736 | tf_op jit(solution)/shard_map/ppermute | solution.py:24
  61.2 15.5 %collective-permute-start.10 = (bf16[2048,128]{1,0:T(8,128)(2,1)S(1)}, bf16[2048,128]{1,0:T(8,128)(2,1)S(1)}, u32[]{:S(2)}, u32[]{:S(2)}) collective-permute-start(bf16[2048,128]{1,0:T(8,128)(2,1)S(1)} %slice.12), channel_id=1, source_target_pairs={{0,4},{4,8},{8,12},{12,0},{1,5},{5,9},{9,13},{13,1},{2,6},{6,10},{... | collective-permute-start | bytes 1572872 | tf_op jit(solution)/shard_map/ppermute | solution.py:20
  62.4 15.3 %collective-permute-start.12 = (bf16[2048,128]{1,0:T(8,128)(2,1)S(1)}, bf16[2048,128]{1,0:T(8,128)(2,1)}, u32[]{:S(2)}, u32[]{:S(2)}) collective-permute-start(bf16[2048,128]{1,0:T(8,128)(2,1)S(1)} %slice.13), channel_id=1, source_target_pairs={{0,12},{4,0},{8,4},{12,8},{1,13},{5,1},{9,5},{13,9},{2,14},{6,2},{... | collective-permute-start | bytes 1572872 | tf_op jit(solution)/shard_map/ppermute | solution.py:20
  65.7 1.1 copy-start.10
  65.7 22.8 %collective-permute-start.8 = (bf16[4096,128]{1,0:T(8,128)(2,1)}, bf16[4096,128]{1,0:T(8,128)(2,1)}, u32[]{:S(2)}, u32[]{:S(2)}) collective-permute-start(bf16[4096,128]{1,0:T(8,128)(2,1)} %collective-permute-done.3.refs_2_), channel_id=1, source_target_pairs={{0,16},{16,0},{1,17},{17,1},{2,18},{18,2},{3,19},{19,3},{4,20},{20... | collective-permute-start | bytes 3145736 | tf_op jit(solution)/shard_map/ppermute | solution.py:24
  66.7 0.8 copy-start.11
  66.7 21.7 %collective-permute-start.9 = (bf16[4096,128]{1,0:T(8,128)(2,1)}, bf16[4096,128]{1,0:T(8,128)(2,1)}, u32[]{:S(2)}, u32[]{:S(2)}) collective-permute-start(bf16[4096,128]{1,0:T(8,128)(2,1)} %collective-permute-done.4.refs_4_), channel_id=1, source_target_pairs={{0,16},{16,0},{1,17},{17,1},{2,18},{18,2},{3,19},{19,3},{4,20},{20... | collective-permute-start | bytes 3145736 | tf_op jit(solution)/shard_map/ppermute | solution.py:24
  76.7 3.9 %copy-start.17 = (bf16[2048,128]{1,0:T(8,128)(2,1)}, bf16[2048,128]{1,0:T(8,128)(2,1)S(1)}, u32[]{:S(2)}) copy-start(bf16[2048,128]{1,0:T(8,128)(2,1)S(1)} %collective-permute-done.10.refs_6_) | copy-start | bytes 1572868
  76.7 3.9 %collective-permute-start.11 = (bf16[2048,128]{1,0:T(8,128)(2,1)S(1)}, bf16[2048,128]{1,0:T(8,128)(2,1)}, u32[]{:S(2)}, u32[]{:S(2)}) collective-permute-start(bf16[2048,128]{1,0:T(8,128)(2,1)S(1)} %collective-permute-done.10.refs_6_), channel_id=1, source_target_pairs={{0,16},{16,0},{1,17},{17,1},{2,18},{18,2},{3,19},{19,3},{4,20},{20... | collective-permute-start | bytes 1572872 | tf_op jit(solution)/shard_map/ppermute | solution.py:24
  77.7 10.8 %collective-permute-start.13 = (bf16[2048,128]{1,0:T(8,128)(2,1)}, bf16[2048,128]{1,0:T(8,128)(2,1)}, u32[]{:S(2)}, u32[]{:S(2)}) collective-permute-start(bf16[2048,128]{1,0:T(8,128)(2,1)} %collective-permute-done.12.refs_8_), channel_id=1, source_target_pairs={{0,16},{16,0},{1,17},{17,1},{2,18},{18,2},{3,19},{19,3},{4,20},{20... | collective-permute-start | bytes 1572872 | tf_op jit(solution)/shard_map/ppermute | solution.py:24
  78.8 32.6 %collective-permute-start.18 = (bf16[1024,512]{1,0:T(8,128)(2,1)}, bf16[1024,512]{1,0:T(8,128)(2,1)S(1)}, u32[]{:S(2)}, u32[]{:S(2)}) collective-permute-start(bf16[1024,512]{1,0:T(8,128)(2,1)} %refs_0_.1), channel_id=1, source_target_pairs={{0,32},{32,64},{64,96},{96,0},{1,33},{33,65},{65,97},{97,1},{2,34}... | collective-permute-start | bytes 3145736 | tf_op jit(solution)/shard_map/ppermute | solution.py:20
  80.6 30.7 %collective-permute-start.19 = (bf16[1024,512]{1,0:T(8,128)(2,1)}, bf16[1024,512]{1,0:T(8,128)(2,1)S(1)}, u32[]{:S(2)}, u32[]{:S(2)}) collective-permute-start(bf16[1024,512]{1,0:T(8,128)(2,1)} %refs_0_.1), channel_id=1, source_target_pairs={{0,96},{32,0},{64,32},{96,64},{1,97},{33,1},{65,33},{97,65},{2,98}... | collective-permute-start | bytes 3145736 | tf_op jit(solution)/shard_map/ppermute | solution.py:20
  100.0 22.9 %all-to-all-start.2 = ((bf16[32,128,128]{2,1,0:T(8,128)(2,1)}), bf16[32,128,128]{2,1,0:T(8,128)(2,1)S(1)}, u32[]{:S(2)}, u32[]{:S(2)}) async-start(bf16[32,128,128]{2,1,0:T(8,128)(2,1)} %bitcast.37), calls=%async_computation.2 | async-start | bytes 2097152 | tf_op jit(solution)/shard_map/all_to_all | solution.py:281
  111.3 52.2 %copy-start.3 = (bf16[1024,512]{1,0:T(8,128)(2,1)}, bf16[1024,512]{1,0:T(8,128)(2,1)S(1)}, u32[]{:S(2)}) copy-start(bf16[1024,512]{1,0:T(8,128)(2,1)S(1)} %collective-permute-done.18.refs_2_) | copy-start | bytes 3145732
  111.3 40.1 %copy-start.4 = (bf16[1024,512]{1,0:T(8,128)(2,1)}, bf16[1024,512]{1,0:T(8,128)(2,1)S(1)}, u32[]{:S(2)}) copy-start(bf16[1024,512]{1,0:T(8,128)(2,1)S(1)} %collective-permute-done.19.refs_4_) | copy-start | bytes 3145732
  122.9 24.5 %copy-start.2 = (bf16[32,128,128]{2,1,0:T(8,128)(2,1)}, bf16[32,128,128]{2,1,0:T(8,128)(2,1)S(1)}, u32[]{:S(2)}) copy-start(bf16[32,128,128]{2,1,0:T(8,128)(2,1)S(1)} %all-to-all-done.2) | copy-start | bytes 3145732
  147.5 16.6 %copy-start.18 = (f32[256]{0:T(256)S(1)}, f32[256]{0:T(256)}, u32[]{:S(2)}) copy-start(f32[256]{0:T(256)} %param.13) | copy-start | bytes 3076
  147.5 26.6 %copy-start.15 = (f32[32]{0:T(128)S(1)}, f32[32]{0:T(128)}, u32[]{:S(2)}) copy-start(f32[32]{0:T(128)} %param.11) | copy-start | bytes 388
  147.5 27.4 %copy-start.16 = (f32[32]{0:T(128)S(1)}, f32[32]{0:T(128)}, u32[]{:S(2)}) copy-start(f32[32]{0:T(128)} %param.12) | copy-start | bytes 388
  151.5 35.8 %all-to-all-start.3 = ((bf16[16,32,16,128]{3,2,1,0:T(8,128)(2,1)}), bf16[16,32,16,128]{3,2,1,0:T(8,128)(2,1)S(1)}, u32[]{:S(2)}, u32[]{:S(2)}) async-start(bf16[16,32,16,128]{3,2,1,0:T(8,128)(2,1)} %bitcast.35), calls=%async_computation.3 | async-start | bytes 4194304 | tf_op jit(solution)/shard_map/all_to_all | solution.py:288
  158.4 14.5 %collective-permute-start.23 = (bf16[512,512]{1,0:T(8,128)(2,1)}, bf16[512,512]{1,0:T(8,128)(2,1)}, u32[]{:S(2)}, u32[]{:S(2)}) collective-permute-start(bf16[512,512]{1,0:T(8,128)(2,1)} %slice.14), channel_id=1, source_target_pairs={{0,32},{32,64},{64,96},{96,0},{1,33},{33,65},{65,97},{97,1},{2,34}... | collective-permute-start | bytes 1572872 | tf_op jit(solution)/shard_map/ppermute | solution.py:20
  160.9 13.2 %collective-permute-start.25 = (bf16[512,512]{1,0:T(8,128)(2,1)}, bf16[512,512]{1,0:T(8,128)(2,1)}, u32[]{:S(2)}, u32[]{:S(2)}) collective-permute-start(bf16[512,512]{1,0:T(8,128)(2,1)} %slice.15), channel_id=1, source_target_pairs={{0,96},{32,0},{64,32},{96,64},{1,97},{33,1},{65,33},{97,65},{2,98}... | collective-permute-start | bytes 1572872 | tf_op jit(solution)/shard_map/ppermute | solution.py:20
  163.5 12.8 %collective-permute-start.20 = (bf16[1024,512]{1,0:T(8,128)(2,1)}, bf16[1024,512]{1,0:T(8,128)(2,1)}, u32[]{:S(2)}, u32[]{:S(2)}) collective-permute-start(bf16[1024,512]{1,0:T(8,128)(2,1)} %refs_0_.1), channel_id=1, source_target_pairs={{0,16},{16,0},{1,17},{17,1},{2,18},{18,2},{3,19},{19,3},{4,20},{20... | collective-permute-start | bytes 3145736 | tf_op jit(solution)/shard_map/ppermute | solution.py:24
  163.5 12.8 %collective-permute-start.21 = (bf16[1024,512]{1,0:T(8,128)(2,1)S(1)}, bf16[1024,512]{1,0:T(8,128)(2,1)}, u32[]{:S(2)}, u32[]{:S(2)}) collective-permute-start(bf16[1024,512]{1,0:T(8,128)(2,1)S(1)} %collective-permute-done.18.refs_2_), channel_id=1, source_target_pairs={{0,16},{16,0},{1,17},{17,1},{2,18},{18,2},{3,19},{19,3},{4,20},{20... | collective-permute-start | bytes 3145736 | tf_op jit(solution)/shard_map/ppermute | solution.py:24
  164.0 12.3 %collective-permute-start.22 = (bf16[1024,512]{1,0:T(8,128)(2,1)}, bf16[1024,512]{1,0:T(8,128)(2,1)}, u32[]{:S(2)}, u32[]{:S(2)}) collective-permute-start(bf16[1024,512]{1,0:T(8,128)(2,1)} %copy-done.4), channel_id=1, source_target_pairs={{0,16},{16,0},{1,17},{17,1},{2,18},{18,2},{3,19},{19,3},{4,20},{20... | collective-permute-start | bytes 3145736 | tf_op jit(solution)/shard_map/ppermute | solution.py:24
  172.9 3.4 %collective-permute-start.24 = (bf16[512,512]{1,0:T(8,128)(2,1)}, bf16[512,512]{1,0:T(8,128)(2,1)}, u32[]{:S(2)}, u32[]{:S(2)}) collective-permute-start(bf16[512,512]{1,0:T(8,128)(2,1)} %collective-permute-done.23.refs_6_), channel_id=1, source_target_pairs={{0,16},{16,0},{1,17},{17,1},{2,18},{18,2},{3,19},{19,3},{4,20},{20... | collective-permute-start | bytes 1572872 | tf_op jit(solution)/shard_map/ppermute | solution.py:24
  174.1 2.3 %collective-permute-start.26 = (bf16[512,512]{1,0:T(8,128)(2,1)}, bf16[512,512]{1,0:T(8,128)(2,1)}, u32[]{:S(2)}, u32[]{:S(2)}) collective-permute-start(bf16[512,512]{1,0:T(8,128)(2,1)} %collective-permute-done.25.refs_8_), channel_id=1, source_target_pairs={{0,16},{16,0},{1,17},{17,1},{2,18},{18,2},{3,19},{19,3},{4,20},{20... | collective-permute-start | bytes 1572872 | tf_op jit(solution)/shard_map/ppermute | solution.py:24
  187.3 1.3 copy-start

commit v2 on v0

--- a/solution.py
+++ b/solution.py
@@ -65,13 +65,14 @@
     )(where, *pairs, *blocks)
 
 
-def turn_kernel(where_ref, zero_ref, one_ref, out_ref):
+def turn_kernel(where_ref, zero_ref, one_ref, *out_refs):
     nd, _, nc = zero_ref.shape
     flip = where_ref[0] == 1
     for d in range(nd):
         p, q = zero_ref[d], one_ref[d]
         pair = jnp.concatenate([jnp.where(flip, q, p), jnp.where(flip, p, q)], axis=0)
-        out_ref[d * nc : (d + 1) * nc, :] = pair.T
+        at = d % (nd // 2) * nc
+        out_refs[d // (nd // 2)][at : at + nc, :] = pair.T
 
 
 def turn(where, zero, one):
@@ -80,37 +81,49 @@
         turn_kernel,
         in_specs=[pl.BlockSpec(memory_space=pltpu.SMEM)]
         + [pl.BlockSpec(memory_space=pltpu.VMEM)] * 2,
-        out_specs=pl.BlockSpec(memory_space=pltpu.VMEM),
-        out_shape=jax.ShapeDtypeStruct((nd * nc, 2 * rows), BF16),
+        out_specs=[pl.BlockSpec(memory_space=pltpu.VMEM)] * 2,
+        out_shape=[jax.ShapeDtypeStruct((nd * nc // 2, 2 * rows), BF16)] * 2,
         name="turn",
     )(where, zero, one)
 
 
 def ladder_kernel(where_ref, *refs):
-    amps, w_ref, out_ref, turned = refs[:-3], refs[-3], refs[-2], refs[-1]
+    amps, w_ref, out_ref, turned, sems = refs[:16], refs[16], refs[17], refs[18], refs[19]
     depth, wide = amps[0].shape
-    j = pl.program_id(1)
-
-    @pl.when((pl.program_id(0) == 0) & (j == 0))
+    g = pl.program_id(0)
+
+    def load(n):
+        chunk, part, side = n // 4, n // 2 % 2, n % 2
+        spot = turned.at[pl.ds(part * depth, depth), pl.ds((2 * chunk + side) * wide, wide)]
+        return pltpu.make_async_copy(amps[n], spot, sems.at[n])
+
+    @pl.when(g == 0)
     def _():
-        for n in range(6):
-            at = n % 2 * wide
-            turned[n // 2, :, at : at + wide] = amps[n][...]
+        for n in range(16):
+            load(n).start()
+
+    _, _, nz, na, nb, _ = out_ref.shape
+    for part in range(2):
+
+        @pl.when(g == 0)
+        def _():
+            for n in range(8 * part, 8 * part + 8):
+                load(n).wait()
+
+        got = jnp.dot(
+            w_ref[...],
+            turned[:, 4 * part * wide : 4 * (part + 1) * wide],
+            preferred_element_type=F32,
+        ).astype(BF16)
         for n in range(4):
-            at = n % 2 * wide
-            row = n // 2 * (depth // 2)
-            turned[3, row : row + depth // 2, at : at + wide] = amps[6 + n][...]
-
-    got = jnp.dot(w_ref[...], turned[j], preferred_element_type=F32).astype(BF16)
-    _, two, nz, na, nb, _ = out_ref.shape
-    for side in range(two):
-        c = where_ref[4] ^ side
-        for s in range(nz):
-            for a in range(na):
-                row = (a * nz + s) * nb
-                out_ref[0, c, where_ref[5] ^ s, a] = got[
-                    row : row + nb, side * wide : (side + 1) * wide
-                ]
+            y = where_ref[2 * part + n // 2]
+            c = where_ref[4] ^ (n % 2)
+            for s in range(nz):
+                for a in range(na):
+                    row = (a * nz + s) * nb
+                    out_ref[y, c, where_ref[5] ^ s, a] = got[
+                        row : row + nb, n * wide : (n + 1) * wide
+                    ]
 
 
 def partial_ladder(where, amps, w):
@@ -122,13 +135,14 @@
         ladder_kernel,
         grid_spec=pltpu.PrefetchScalarGridSpec(
             num_scalar_prefetch=1,
-            grid=(nrow // step, 4),
-            in_specs=[pl.BlockSpec(v.shape, lambda g, j, h: (0, 0)) for v in amps]
-            + [pl.BlockSpec((step, depth), lambda g, j, h: (g, 0))],
-            out_specs=pl.BlockSpec(
-                (1, 2, nz, na, nb, wide), lambda g, j, h: (h[j], 0, 0, g, 0, 0)
-            ),
-            scratch_shapes=[pltpu.VMEM((4, depth, 2 * wide), BF16)],
+            grid=(nrow // step,),
+            in_specs=[pl.BlockSpec(memory_space=pl.ANY) for _ in amps]
+            + [pl.BlockSpec((step, depth), lambda g, h: (g, 0))],
+            out_specs=pl.BlockSpec((4, 2, nz, na, nb, wide), lambda g, h: (0, 0, 0, g, 0, 0)),
+            scratch_shapes=[
+                pltpu.VMEM((depth, 8 * wide), BF16),
+                pltpu.SemaphoreType.DMA((len(amps),)),
+            ],
         ),
         out_shape=jax.ShapeDtypeStruct((4, 2, nz, nrow // (nz * nb), nb, wide), BF16),
         cost_estimate=pl.CostEstimate(
@@ -241,25 +255,23 @@
     ]
     own = turn(scalars(half), *own)
 
-    left, right = ring(own, "x", 1), ring(own, "x", -1)
+    low, high = own
+    left_low, right_high = ring(low, "x", 1), ring(high, "x", -1)
+    left_high, right_low = ring(high, "x", 1), ring(low, "x", -1)
     blocks = [block] + [ring(block, "y", k) for k in (1, 3, 2)]
     turned = pair_factor.transpose(1, 0, 2)
-    turned, own = lax.optimization_barrier((turned, own))
+    turned, *own = lax.optimization_barrier((turned, *own))
     pair = [lax.ppermute(turned, ("core", "z"), amplitude_route(alpha)) for alpha in range(2)]
     before, after = ring(cycle_matrix, "y", 1), ring(cycle_matrix, "y", -1)
-
-    left, right, *blocks = lax.optimization_barrier((left, right, *blocks))
-    mid = own.shape[0] // 2
-    far = [ring(left[:mid], "x", 1), ring(right[mid:], "x", -1)]
+    far = [ring(left_low, "x", 1), ring(right_high, "x", -1)]
     pair += [sibling(v) for v in pair]
     amps = []
-    for v in (own, left, right):
+    for v in (*own, left_low, left_high, right_low, right_high):
         amps += [v, sibling(v)]
     for v in far:
         amps += [v, sibling(v)]
 
     w = form_integrals(scalars(y), pair, blocks)
-    w, before, after = lax.optimization_barrier((w, before, after))
 
     spots = scalars(x, (x + 3) % 4, (x + 1) % 4, (x + 2) % 4, core, 2 * core + half)
     parts = partial_ladder(spots, amps, w)

time: 208 us -> 196 us (0.942)
  blocking collectives: 55.9 us -> 0 us
  waiting for transfers between devices: 59.3 us -> 87 us
  starting transfers between devices: 34 us -> 53.1 us
  Pallas kernels: 42.2 us -> 39.3 us
    all_to_all x2 -> x0, blocking collectives: 55.9 us -> none  [the longest x1 34.2 us: update(): parts = lax.all_to_all(parts, ('y', 'core', 'z'), 0, 0, tiled=True)]
    all_to_all x0 -> x2, waiting for transfers between devices: none -> 31.7 us  [the longest x1 25 us: update(): parts = lax.all_to_all(parts, ('y', 'core', 'z'), 0, 0, tiled=True)]
    all_to_all x0 -> x2, starting transfers between devices: none -> 16.4 us  [the longest x1 8.28 us: update(): lax.all_to_all(block.reshape(32, na // 2, nq, nc // 2), ('core', 'x', 'z'...]
    ppermute x11 -> x13, waiting for transfers between devices: 39.3 us -> 53.1 us  [ring(): return lax.ppermute(value, axis, [(i, (i + shift) % n) for i in range(n)])]
    all_to_all x1, waiting for transfers between devices: 10.8 us -> 0.61 us  [update(): lax.all_to_all(holes.reshape(16, nj, 16, 128), VIR, 0, 0, tiled=True)]
    ppermute x2, waiting for transfers between devices: 9.14 us -> 0.01 us  [update(): lax.ppermute(turned, ('core', 'z'), amplitude_route(alpha))]
    pallas_call x1, Pallas kernels: 19.1 us -> 16.1 us  [partial_ladder(): pl.pallas_call(ladder_kernel, grid_spec=pltpu.PrefetchScalarGridSpec(num_...]
    unnamed x38 -> x46, local copies, waits for them, and re-layouts: 6.31 us -> 5.32 us
  transfers between devices with their start and end apart: 28 -> 35, of which waited for: 10 -> 14; matrix products, arithmetic and copies ran while one was open for 4% -> 4% of each run, Pallas kernels for 6% -> 9%
where the time goes in v2:
time: 196 us; the launch traced here: 194 us
  waiting for transfers between devices  87 us (44%)
  starting transfers between devices  53.1 us (27%)
  Pallas kernels  39.3 us (20%)
  local copies, waits for them, and re-layouts  13.7 us (7%)
    ppermute x13, waiting for transfers between devices, ring(): return lax.ppermute(value, axis, [(i, (i + shift) % n) for i in range(n)])  53.1 us
    all_to_all x1, waiting for transfers between devices, update(): parts = lax.all_to_all(parts, ('y', 'core', 'z'), 0, 0, tiled=True)  25 us
    ppermute x13, starting transfers between devices, ring(): return lax.ppermute(value, axis, [(i, (i + shift) % n) for i in range(n)])  21.1 us
    pallas_call x1, Pallas kernels, partial_ladder(): pl.pallas_call(ladder_kernel, grid_spec=pltpu.PrefetchScalarGridSpec(num_...  16.1 us
    pallas_call x1, Pallas kernels, form_integrals(): pl.pallas_call(integrals_kernel, grid_spec=pltpu.PrefetchScalarGridSpec(n...  10.6 us
    all_to_all x1, starting transfers between devices, update(): lax.all_to_all(block.reshape(32, na // 2, nq, nc // 2), ('core', 'x', 'z'...  8.28 us
    all_to_all x1, starting transfers between devices, update(): parts = lax.all_to_all(parts, ('y', 'core', 'z'), 0, 0, tiled=True)  8.12 us
    all_to_all x1, waiting for transfers between devices, update(): lax.all_to_all(block.reshape(32, na // 2, nq, nc // 2), ('core', 'x', 'z'...  6.68 us
  transfers between devices with their start and end apart: 35, of which 14 were waited for; matrix products, arithmetic and copies ran while one was open for 4% of the time, Pallas kernels for 9%

profile of v2, /device:TPU:0, one launch (start us, length us, event | category | flops | bytes accessed | tf_op | source)
XLA Modules:
  0.0 194.2 jit_solution(11112121351469952456)
XLA Ops:
  0.0 1.0 reshape.73
  1.0 1.0 broadcast_in_dim.2
  2.0 8.3 %all-to-all-start = ((bf16[32,16,4,128]{3,2,1,0:T(4,128)(2,1)}), bf16[32,16,4,128]{3,2,1,0:T(4,128)(2,1)S(1)}, u32[]{:S(2)}, u32[]{:S(2)}) async-start(bf16[32,16,4,128]{3,2,1,0:T(4,128)(2,1)} %bitcast.13), calls=%async_computation | async-start | bytes 1048576 | tf_op jit(solution)/shard_map/all_to_all | solution.py:240
  10.3 0.6 copy.13
  11.0 1.2 dynamic-slice_bitcast_fusion
  12.2 1.7 collective-permute-start
  13.9 1.8 collective-permute-start.1
  15.7 6.7 %all-to-all-done = bf16[32,16,4,128]{3,2,1,0:T(4,128)(2,1)S(1)} async-done(((bf16[32,16,4,128]{3,2,1,0:T(4,128)(2,1)}), bf16[32,16,4,128]{3,2,1,0:T(4,128)(2,1)S(1)}, u32[]{:S(2)}, u32[]{:S(2)}) %all-to-all-start) | async-done | bytes 524320 | tf_op jit(solution)/shard_map/all_to_all | solution.py:240
  22.4 0.2 copy.15
  22.6 1.6 collective-permute-start.20
  24.3 0.3 copy.18
  24.6 1.7 collective-permute-start.21
  26.3 2.0 %collective-permute-start.22 = (bf16[16,128,128]{2,1,0:T(8,128)(2,1)S(1)}, bf16[16,128,128]{2,1,0:T(8,128)(2,1)}, u32[]{:S(2)}, u32[]{:S(2)}) collective-permute-start(bf16[16,128,128]{2,1,0:T(8,128)(2,1)S(1)} %bitcast.32), channel_id=1, source_target_pairs={{0,64},{32,96},{64,0},{96,32},{1,65},{33,97},{65,1},{97,33},{2,66}... | collective-permute-start | bytes 1572872 | tf_op jit(solution)/shard_map/ppermute | solution.py:20
  28.3 1.6 collective-permute-done.1.one_ref
  29.8 0.8 copy-done.7
  30.6 2.4 %turn.1 = (bf16[2048,128]{1,0:T(8,128)(2,1)}, bf16[2048,128]{1,0:T(8,128)(2,1)}) custom-call(s32[1]{0:T(128)} %bitcast.8.where_ref, bf16[32,64,128]{2,1,0:T(8,128)(2,1)} %copy-done.6, bf16[32,64,128]{2,1,0:T(8,128)(2,1)} %copy-done.7), custom_call_target="tpu_custom_call" | custom-call | tf_op jit(solution)/shard_map/turn/pallas_call | solution.py:80
  33.0 0.7 collective-permute-start.16
  33.7 2.2 %collective-permute-start.17 = (bf16[32,16,512]{2,1,0:T(8,128)(2,1)S(1)}, bf16[32,16,512]{2,1,0:T(8,128)(2,1)S(1)}, u32[]{:S(2)}, u32[]{:S(2)}) collective-permute-start(bf16[32,16,512]{2,1,0:T(8,128)(2,1)S(1)} %bitcast.35), channel_id=1, source_target_pairs={{0,1},{1,0},{2,17},{3,16},{16,3},{17,2},{18,19},{19,18},{4,5},{5,4... | collective-permute-start | bytes 1572872 | tf_op jit(solution)/shard_map/ppermute | solution.py:264
  35.9 1.7 collective-permute-done.20.refs_5_
  37.6 0.8 collective-permute-start.4
  38.4 9.5 %collective-permute-done.21.refs_6_ = bf16[16,128,128]{2,1,0:T(8,128)(2,1)S(1)} collective-permute-done((bf16[16,128,128]{2,1,0:T(8,128)(2,1)S(1)}, bf16[16,128,128]{2,1,0:T(8,128)(2,1)S(1)}, u32[]{:S(2)}, u32[]{:S(2)}) %collective-permute-start.21) | collective-permute-done | bytes 524320 | tf_op jit(solution)/shard_map/ppermute | solution.py:20
  47.8 2.0 %collective-permute-start.10 = (bf16[2048,128]{1,0:T(8,128)(2,1)}, bf16[2048,128]{1,0:T(8,128)(2,1)S(1)}, u32[]{:S(2)}, u32[]{:S(2)}) collective-permute-start(bf16[2048,128]{1,0:T(8,128)(2,1)} %get-tuple-element.15.refs_2_), channel_id=1, source_target_pairs={{0,12},{4,0},{8,4},{12,8},{1,13},{5,1},{9,5},{13,9},{2,14},{6,2},{... | collective-permute-start | bytes 1572872 | tf_op jit(solution)/shard_map/ppermute | solution.py:20
  49.9 0.6 collective-permute-start.6
  50.5 2.6 %collective-permute-start.8 = (bf16[2048,128]{1,0:T(8,128)(2,1)}, bf16[2048,128]{1,0:T(8,128)(2,1)}, u32[]{:S(2)}, u32[]{:S(2)}) collective-permute-start(bf16[2048,128]{1,0:T(8,128)(2,1)} %get-tuple-element.14.refs_0_), channel_id=1, source_target_pairs={{0,12},{4,0},{8,4},{12,8},{1,13},{5,1},{9,5},{13,9},{2,14},{6,2},{... | collective-permute-start | bytes 1572872 | tf_op jit(solution)/shard_map/ppermute | solution.py:20
  53.1 1.3 collective-permute-start.2
  54.4 0.1 collective-permute-start.3
  54.5 6.6 %collective-permute-done.10.refs_10_ = bf16[2048,128]{1,0:T(8,128)(2,1)S(1)} collective-permute-done((bf16[2048,128]{1,0:T(8,128)(2,1)}, bf16[2048,128]{1,0:T(8,128)(2,1)S(1)}, u32[]{:S(2)}, u32[]{:S(2)}) %collective-permute-start.10) | collective-permute-done | bytes 524320 | tf_op jit(solution)/shard_map/ppermute | solution.py:20
  61.1 4.0 %collective-permute-done.6.refs_6_ = bf16[2048,128]{1,0:T(8,128)(2,1)} collective-permute-done((bf16[2048,128]{1,0:T(8,128)(2,1)}, bf16[2048,128]{1,0:T(8,128)(2,1)}, u32[]{:S(2)}, u32[]{:S(2)}) %collective-permute-start.6) | collective-permute-done | bytes 524320 | tf_op jit(solution)/shard_map/ppermute | solution.py:20
  65.1 3.5 %collective-permute-done.8.refs_8_ = bf16[2048,128]{1,0:T(8,128)(2,1)} collective-permute-done((bf16[2048,128]{1,0:T(8,128)(2,1)}, bf16[2048,128]{1,0:T(8,128)(2,1)}, u32[]{:S(2)}, u32[]{:S(2)}) %collective-permute-start.8) | collective-permute-done | bytes 524320 | tf_op jit(solution)/shard_map/ppermute | solution.py:20
  68.7 0.9 collective-permute-start.12
  69.6 2.3 %collective-permute-start.14 = (bf16[2048,128]{1,0:T(8,128)(2,1)S(1)}, bf16[2048,128]{1,0:T(8,128)(2,1)}, u32[]{:S(2)}, u32[]{:S(2)}) collective-permute-start(bf16[2048,128]{1,0:T(8,128)(2,1)S(1)} %collective-permute-done.10.refs_10_), channel_id=1, source_target_pairs={{0,12},{4,0},{8,4},{12,8},{1,13},{5,1},{9,5},{13,9},{2,14},{6,2},{... | collective-permute-start | bytes 1572872 | tf_op jit(solution)/shard_map/ppermute | solution.py:20
  72.0 0.5 collective-permute-start.5
  72.4 0.1 collective-permute-start.7
  72.5 8.2 %collective-permute-done.12.refs_12_ = bf16[2048,128]{1,0:T(8,128)(2,1)} collective-permute-done((bf16[2048,128]{1,0:T(8,128)(2,1)S(1)}, bf16[2048,128]{1,0:T(8,128)(2,1)}, u32[]{:S(2)}, u32[]{:S(2)}) %collective-permute-start.12) | collective-permute-done | bytes 524320 | tf_op jit(solution)/shard_map/ppermute | solution.py:20
  80.8 0.5 collective-permute-start.13
  81.4 0.8 copy-done.19
  82.2 0.6 stack.40.where_ref
  82.8 10.6 %integrals.1.refs_16_ = bf16[1024,4096]{1,0:T(8,128)(2,1)} custom-call(s32[1]{0:T(128)} %bitcast.where_ref, bf16[32,16,512]{2,1,0:T(8,128)(2,1)} %copy-done.14, bf16[32,16,512]{2,1,0:T(8,128)(2,1)} %copy-done.15, bf16[32,16,512]{2,1,0:T(8,128)(2,1)} %copy-done.18, bf16[32,16,512]{2,1,0:T(8,128)(2,1)} %copy-done.20, bf16[16,128,128]{2,1,0:T(8,128)(2,1)} %bitcast.33, ...), custom_call_target="tpu_custom_call" | custom-call | flops 4294967296 | bytes 12582912 | tf_op jit(solution)/shard_map/integrals/pallas_call | solution.py:50
  93.5 16.1 %ladder.1 = bf16[4,2,4,16,16,128]{5,4,3,2,1,0:T(8,128)(2,1)} custom-call(s32[6]{0:T(128)} %stack.40.where_ref, bf16[2048,128]{1,0:T(8,128)(2,1)} %get-tuple-element.14.refs_0_, bf16[2048,128]{1,0:T(8,128)(2,1)} %copy-done.16, bf16[2048,128]{1,0:T(8,128)(2,1)} %get-tuple-element.15.refs_2_, bf16[2048,128]{1,0:T(8,128)(2,1)} %copy-done.17, ...), custom_call_target="tpu_custom_call" | custom-call | flops 8589934592 | bytes 18874368 | tf_op jit(solution)/shard_map/ladder/pallas_call | solution.py:134
  109.7 8.1 %all-to-all-start.1 = ((bf16[32,256,128]{2,1,0:T(8,128)(2,1)}), bf16[32,256,128]{2,1,0:T(8,128)(2,1)S(1)}, u32[]{:S(2)}, u32[]{:S(2)}) async-start(bf16[32,256,128]{2,1,0:T(8,128)(2,1)} %bitcast.28), calls=%async_computation.1 | async-start | bytes 4194304 | tf_op jit(solution)/shard_map/all_to_all | solution.py:279
  117.8 1.9 collective-permute-start.24
  119.7 1.4 collective-permute-start.26
  121.1 25.0 %all-to-all-done.1 = bf16[32,256,128]{2,1,0:T(8,128)(2,1)S(1)} async-done(((bf16[32,256,128]{2,1,0:T(8,128)(2,1)}), bf16[32,256,128]{2,1,0:T(8,128)(2,1)S(1)}, u32[]{:S(2)}, u32[]{:S(2)}) %all-to-all-start.1) | async-done | bytes 2097184 | tf_op jit(solution)/shard_map/all_to_all | solution.py:279
  146.1 1.4 copy-done
  147.5 4.1 %settle.1 = (f32[128,512]{1,0:T(8,128)}, bf16[16,512,128]{2,1,0:T(8,128)(2,1)}) custom-call(bf16[4,2,4,256,128]{4,3,2,1,0:T(8,128)(2,1)} %bitcast.25), custom_call_target="tpu_custom_call" | custom-call | tf_op jit(solution)/shard_map/settle/pallas_call | solution.py:186
  151.6 6.2 %all-to-all-start.2 = ((bf16[16,32,16,128]{3,2,1,0:T(8,128)(2,1)}), bf16[16,32,16,128]{3,2,1,0:T(8,128)(2,1)S(1)}, u32[]{:S(2)}, u32[]{:S(2)}) async-start(bf16[16,32,16,128]{3,2,1,0:T(8,128)(2,1)} %bitcast.27), calls=%async_computation.2 | async-start | bytes 4194304 | tf_op jit(solution)/shard_map/all_to_all | solution.py:281
  157.8 9.1 %collective-permute-done.24.refs_2_ = bf16[1024,512]{1,0:T(8,128)(2,1)S(1)} collective-permute-done((bf16[1024,512]{1,0:T(8,128)(2,1)}, bf16[1024,512]{1,0:T(8,128)(2,1)S(1)}, u32[]{:S(2)}, u32[]{:S(2)}) %collective-permute-start.24) | collective-permute-done | bytes 1048608 | tf_op jit(solution)/shard_map/ppermute | solution.py:20
  166.9 0.9 slice.8
  167.8 0.1 collective-permute-done.26.refs_4_
  167.9 1.9 slice.9
  169.7 3.2 %collective-permute-start.30 = (bf16[512,512]{1,0:T(8,128)(2,1)}, bf16[512,512]{1,0:T(8,128)(2,1)}, u32[]{:S(2)}, u32[]{:S(2)}) collective-permute-start(bf16[512,512]{1,0:T(8,128)(2,1)} %slice.9), channel_id=1, source_target_pairs={{0,96},{32,0},{64,32},{96,64},{1,97},{33,1},{65,33},{97,65},{2,98}... | collective-permute-start | bytes 1572872 | tf_op jit(solution)/shard_map/ppermute | solution.py:20
  172.9 0.5 collective-permute-start.25
  173.4 0.1 dynamic_slice.15
  173.5 9.2 %collective-permute-done.28.refs_6_ = bf16[512,512]{1,0:T(8,128)(2,1)} collective-permute-done((bf16[512,512]{1,0:T(8,128)(2,1)}, bf16[512,512]{1,0:T(8,128)(2,1)}, u32[]{:S(2)}, u32[]{:S(2)}) %collective-permute-start.28) | collective-permute-done | bytes 524320 | tf_op jit(solution)/shard_map/ppermute | solution.py:20
  182.7 1.1 collective-permute-done.30.refs_8_
  183.9 0.1 broadcast_subtract_fusion
  183.9 0.6 sub.53.refs_12_
  184.6 0.1 dynamic_slice.14
  184.7 0.1 broadcast_subtract_fusion.1
  184.7 0.7 sub.54.refs_11_
  185.5 0.6 pad_add_fusion.where_ref
  186.1 0.6 all-to-all-done.2.holes_ref
  186.7 1.4 copy-done.1
  188.1 6.1 %cycle.1 = f32[128,512]{1,0:T(8,128)} custom-call(s32[2]{0:T(128)} %pad_add_fusion.where_ref, bf16[16,32,16,128]{3,2,1,0:T(8,128)(2,1)} %copy-done.1, bf16[1024,512]{1,0:T(8,128)(2,1)} %refs_0_.1, bf16[1024,512]{1,0:T(8,128)(2,1)} %collective-permute-done.23.refs_1_, bf16[1024,512]{1,0:T(8,128)(2,1)} %copy-done.2, ...), custom_call_target="tpu_custom_call" | custom-call | tf_op jit(solution)/shard_map/cycle/pallas_call | solution.py:217
  (72 shorter events, 0.2 us)
Async XLA Ops:
  0.0 10.3 %copy-start.3 = (bf16[2,32,32,256]{3,2,1,0:T(8,128)(2,1)S(1)}, bf16[2,32,32,256]{3,2,1,0:T(8,128)(2,1)}, u32[]{:S(2)}) copy-start(bf16[2,32,32,256]{3,2,1,0:T(8,128)(2,1)} %param.7) | copy-start | bytes 3145732
  2.0 20.3 %all-to-all-start = ((bf16[32,16,4,128]{3,2,1,0:T(4,128)(2,1)}), bf16[32,16,4,128]{3,2,1,0:T(4,128)(2,1)S(1)}, u32[]{:S(2)}, u32[]{:S(2)}) async-start(bf16[32,16,4,128]{3,2,1,0:T(4,128)(2,1)} %bitcast.13), calls=%async_computation | async-start | bytes 1048576 | tf_op jit(solution)/shard_map/all_to_all | solution.py:240
  10.9 13.3 %copy-start.4 = (bf16[16,32,512]{2,1,0:T(8,128)(2,1)S(1)}, bf16[16,32,512]{2,1,0:T(8,128)(2,1)}, u32[]{:S(2)}) copy-start(bf16[16,32,512]{2,1,0:T(8,128)(2,1)} %param.8) | copy-start | bytes 1572868
  12.2 16.1 %collective-permute-start = (bf16[32,64,128]{2,1,0:T(8,128)(2,1)}, bf16[32,64,128]{2,1,0:T(8,128)(2,1)S(1)}, u32[]{:S(2)}, u32[]{:S(2)}) collective-permute-start(bf16[32,64,128]{2,1,0:T(8,128)(2,1)} %get-tuple-element.20), channel_id=1, source_target_pairs={{0,0},{1,1},{2,16},{3,17},{16,2},{17,3},{18,18},{19,19},{4,4},{5,5... | collective-permute-start | bytes 1572872 | tf_op jit(solution)/shard_map/ppermute | solution.py:247
  13.9 15.9 %collective-permute-start.1 = (bf16[32,64,128]{2,1,0:T(8,128)(2,1)}, bf16[32,64,128]{2,1,0:T(8,128)(2,1)S(1)}, u32[]{:S(2)}, u32[]{:S(2)}) collective-permute-start(bf16[32,64,128]{2,1,0:T(8,128)(2,1)} %get-tuple-element.19), channel_id=1, source_target_pairs={{0,1},{1,0},{2,17},{3,16},{16,3},{17,2},{18,19},{19,18},{4,5},{5,4... | collective-permute-start | bytes 1572872 | tf_op jit(solution)/shard_map/ppermute | solution.py:247
  22.6 60.2 %copy-start.5 = (bf16[16,32,4,128]{3,2,1,0:T(4,128)(2,1)}, bf16[16,32,4,128]{3,2,1,0:T(4,128)(2,1)S(1)}, u32[]{:S(2)}) copy-start(bf16[16,32,4,128]{3,2,1,0:T(4,128)(2,1)S(1)} %copy.15) | copy-start | bytes 1572868
  22.6 15.0 %collective-permute-start.20 = (bf16[16,128,128]{2,1,0:T(8,128)(2,1)S(1)}, bf16[16,128,128]{2,1,0:T(8,128)(2,1)S(1)}, u32[]{:S(2)}, u32[]{:S(2)}) collective-permute-start(bf16[16,128,128]{2,1,0:T(8,128)(2,1)S(1)} %bitcast.30), channel_id=1, source_target_pairs={{0,32},{32,64},{64,96},{96,0},{1,33},{33,65},{65,97},{97,1},{2,34}... | collective-permute-start | bytes 1572872 | tf_op jit(solution)/shard_map/ppermute | solution.py:20
  24.6 23.3 %collective-permute-start.21 = (bf16[16,128,128]{2,1,0:T(8,128)(2,1)S(1)}, bf16[16,128,128]{2,1,0:T(8,128)(2,1)S(1)}, u32[]{:S(2)}, u32[]{:S(2)}) collective-permute-start(bf16[16,128,128]{2,1,0:T(8,128)(2,1)S(1)} %bitcast.31), channel_id=1, source_target_pairs={{0,96},{32,0},{64,32},{96,64},{1,97},{33,1},{65,33},{97,65},{2,98}... | collective-permute-start | bytes 1572872 | tf_op jit(solution)/shard_map/ppermute | solution.py:20
  26.3 23.6 %collective-permute-start.22 = (bf16[16,128,128]{2,1,0:T(8,128)(2,1)S(1)}, bf16[16,128,128]{2,1,0:T(8,128)(2,1)}, u32[]{:S(2)}, u32[]{:S(2)}) collective-permute-start(bf16[16,128,128]{2,1,0:T(8,128)(2,1)S(1)} %bitcast.32), channel_id=1, source_target_pairs={{0,64},{32,96},{64,0},{96,32},{1,65},{33,97},{65,1},{97,33},{2,66}... | collective-permute-start | bytes 1572872 | tf_op jit(solution)/shard_map/ppermute | solution.py:20
  28.3 1.6 copy-start.6
  29.8 0.8 copy-start.7
  33.0 17.5 %collective-permute-start.16 = (bf16[32,16,512]{2,1,0:T(8,128)(2,1)S(1)}, bf16[32,16,512]{2,1,0:T(8,128)(2,1)S(1)}, u32[]{:S(2)}, u32[]{:S(2)}) collective-permute-start(bf16[32,16,512]{2,1,0:T(8,128)(2,1)S(1)} %bitcast.34), channel_id=1, source_target_pairs={{0,0},{1,1},{2,16},{3,17},{16,2},{17,3},{18,18},{19,19},{4,4},{5,5... | collective-permute-start | bytes 1572872 | tf_op jit(solution)/shard_map/ppermute | solution.py:264
  33.7 19.4 %collective-permute-start.17 = (bf16[32,16,512]{2,1,0:T(8,128)(2,1)S(1)}, bf16[32,16,512]{2,1,0:T(8,128)(2,1)S(1)}, u32[]{:S(2)}, u32[]{:S(2)}) collective-permute-start(bf16[32,16,512]{2,1,0:T(8,128)(2,1)S(1)} %bitcast.35), channel_id=1, source_target_pairs={{0,1},{1,0},{2,17},{3,16},{16,3},{17,2},{18,19},{19,18},{4,5},{5,4... | collective-permute-start | bytes 1572872 | tf_op jit(solution)/shard_map/ppermute | solution.py:264
  37.6 45.3 %copy-start.10 = (bf16[16,128,128]{2,1,0:T(8,128)(2,1)}, bf16[16,128,128]{2,1,0:T(8,128)(2,1)S(1)}, u32[]{:S(2)}) copy-start(bf16[16,128,128]{2,1,0:T(8,128)(2,1)S(1)} %collective-permute-done.20.refs_5_) | copy-start | bytes 1572868
  37.6 16.8 %collective-permute-start.4 = (bf16[2048,128]{1,0:T(8,128)(2,1)}, bf16[2048,128]{1,0:T(8,128)(2,1)S(1)}, u32[]{:S(2)}, u32[]{:S(2)}) collective-permute-start(bf16[2048,128]{1,0:T(8,128)(2,1)} %get-tuple-element.14.refs_0_), channel_id=1, source_target_pairs={{0,4},{4,8},{8,12},{12,0},{1,5},{5,9},{9,13},{13,1},{2,6},{6,10},{... | collective-permute-start | bytes 1572872 | tf_op jit(solution)/shard_map/ppermute | solution.py:20
  47.8 35.0 %copy-start.11 = (bf16[16,128,128]{2,1,0:T(8,128)(2,1)}, bf16[16,128,128]{2,1,0:T(8,128)(2,1)S(1)}, u32[]{:S(2)}) copy-start(bf16[16,128,128]{2,1,0:T(8,128)(2,1)S(1)} %collective-permute-done.21.refs_6_) | copy-start | bytes 1572868
  47.8 13.3 %collective-permute-start.10 = (bf16[2048,128]{1,0:T(8,128)(2,1)}, bf16[2048,128]{1,0:T(8,128)(2,1)S(1)}, u32[]{:S(2)}, u32[]{:S(2)}) collective-permute-start(bf16[2048,128]{1,0:T(8,128)(2,1)} %get-tuple-element.15.refs_2_), channel_id=1, source_target_pairs={{0,12},{4,0},{8,4},{12,8},{1,13},{5,1},{9,5},{13,9},{2,14},{6,2},{... | collective-permute-start | bytes 1572872 | tf_op jit(solution)/shard_map/ppermute | solution.py:20
  49.9 15.3 %collective-permute-start.6 = (bf16[2048,128]{1,0:T(8,128)(2,1)}, bf16[2048,128]{1,0:T(8,128)(2,1)}, u32[]{:S(2)}, u32[]{:S(2)}) collective-permute-start(bf16[2048,128]{1,0:T(8,128)(2,1)} %get-tuple-element.15.refs_2_), channel_id=1, source_target_pairs={{0,4},{4,8},{8,12},{12,0},{1,5},{5,9},{9,13},{13,1},{2,6},{6,10},{... | collective-permute-start | bytes 1572872 | tf_op jit(solution)/shard_map/ppermute | solution.py:20
  50.5 30.8 %copy-start.14 = (bf16[32,16,512]{2,1,0:T(8,128)(2,1)}, bf16[32,16,512]{2,1,0:T(8,128)(2,1)S(1)}, u32[]{:S(2)}) copy-start(bf16[32,16,512]{2,1,0:T(8,128)(2,1)S(1)} %collective-permute-done.16.refs_0_) | copy-start | bytes 1572868
  50.5 18.2 %collective-permute-start.8 = (bf16[2048,128]{1,0:T(8,128)(2,1)}, bf16[2048,128]{1,0:T(8,128)(2,1)}, u32[]{:S(2)}, u32[]{:S(2)}) collective-permute-start(bf16[2048,128]{1,0:T(8,128)(2,1)} %get-tuple-element.14.refs_0_), channel_id=1, source_target_pairs={{0,12},{4,0},{8,4},{12,8},{1,13},{5,1},{9,5},{13,9},{2,14},{6,2},{... | collective-permute-start | bytes 1572872 | tf_op jit(solution)/shard_map/ppermute | solution.py:20
  53.1 28.2 %copy-start.15 = (bf16[32,16,512]{2,1,0:T(8,128)(2,1)}, bf16[32,16,512]{2,1,0:T(8,128)(2,1)S(1)}, u32[]{:S(2)}) copy-start(bf16[32,16,512]{2,1,0:T(8,128)(2,1)S(1)} %collective-permute-done.17.refs_1_) | copy-start | bytes 1572868
  53.1 16.5 %collective-permute-start.2 = (bf16[2048,128]{1,0:T(8,128)(2,1)}, bf16[2048,128]{1,0:T(8,128)(2,1)S(1)}, u32[]{:S(2)}, u32[]{:S(2)}) collective-permute-start(bf16[2048,128]{1,0:T(8,128)(2,1)} %get-tuple-element.14.refs_0_), channel_id=1, source_target_pairs={{0,16},{16,0},{1,17},{17,1},{2,18},{18,2},{3,19},{19,3},{4,20},{20... | collective-permute-start | bytes 1572872 | tf_op jit(solution)/shard_map/ppermute | solution.py:24
  54.4 39.1 %copy-start.12 = (bf16[2048,128]{1,0:T(8,128)(2,1)}, bf16[2048,128]{1,0:T(8,128)(2,1)S(1)}, u32[]{:S(2)}) copy-start(bf16[2048,128]{1,0:T(8,128)(2,1)S(1)} %collective-permute-done.4.refs_4_) | copy-start | bytes 1572868
  54.4 17.5 %collective-permute-start.3 = (bf16[2048,128]{1,0:T(8,128)(2,1)}, bf16[2048,128]{1,0:T(8,128)(2,1)S(1)}, u32[]{:S(2)}, u32[]{:S(2)}) collective-permute-start(bf16[2048,128]{1,0:T(8,128)(2,1)} %get-tuple-element.15.refs_2_), channel_id=1, source_target_pairs={{0,16},{16,0},{1,17},{17,1},{2,18},{18,2},{3,19},{19,3},{4,20},{20... | collective-permute-start | bytes 1572872 | tf_op jit(solution)/shard_map/ppermute | solution.py:24
  61.1 32.4 %copy-start.13 = (bf16[2048,128]{1,0:T(8,128)(2,1)}, bf16[2048,128]{1,0:T(8,128)(2,1)S(1)}, u32[]{:S(2)}) copy-start(bf16[2048,128]{1,0:T(8,128)(2,1)S(1)} %collective-permute-done.10.refs_10_) | copy-start | bytes 1572868
  61.1 10.8 %collective-permute-start.18 = (bf16[32,16,512]{2,1,0:T(8,128)(2,1)S(1)}, bf16[32,16,512]{2,1,0:T(8,128)(2,1)S(1)}, u32[]{:S(2)}, u32[]{:S(2)}) collective-permute-start(bf16[32,16,512]{2,1,0:T(8,128)(2,1)S(1)} %collective-permute-done.16.refs_0_), channel_id=1, source_target_pairs={{0,16},{16,0},{1,17},{17,1},{2,18},{18,2},{3,19},{19,3},{4,20},{20... | collective-permute-start | bytes 1572872 | tf_op jit(solution)/shard_map/ppermute | solution.py:24
  65.1 7.3 %collective-permute-start.19 = (bf16[32,16,512]{2,1,0:T(8,128)(2,1)S(1)}, bf16[32,16,512]{2,1,0:T(8,128)(2,1)S(1)}, u32[]{:S(2)}, u32[]{:S(2)}) collective-permute-start(bf16[32,16,512]{2,1,0:T(8,128)(2,1)S(1)} %collective-permute-done.17.refs_1_), channel_id=1, source_target_pairs={{0,16},{16,0},{1,17},{17,1},{2,18},{18,2},{3,19},{19,3},{4,20},{20... | collective-permute-start | bytes 1572872 | tf_op jit(solution)/shard_map/ppermute | solution.py:24
  68.7 12.1 %collective-permute-start.12 = (bf16[2048,128]{1,0:T(8,128)(2,1)S(1)}, bf16[2048,128]{1,0:T(8,128)(2,1)}, u32[]{:S(2)}, u32[]{:S(2)}) collective-permute-start(bf16[2048,128]{1,0:T(8,128)(2,1)S(1)} %collective-permute-done.4.refs_4_), channel_id=1, source_target_pairs={{0,4},{4,8},{8,12},{12,0},{1,5},{5,9},{9,13},{13,1},{2,6},{6,10},{... | collective-permute-start | bytes 1572872 | tf_op jit(solution)/shard_map/ppermute | solution.py:20
  69.6 23.9 %copy-start.16 = (bf16[2048,128]{1,0:T(8,128)(2,1)}, bf16[2048,128]{1,0:T(8,128)(2,1)S(1)}, u32[]{:S(2)}) copy-start(bf16[2048,128]{1,0:T(8,128)(2,1)S(1)} %collective-permute-done.2.refs_1_) | copy-start | bytes 1572868
  69.6 11.2 %collective-permute-start.14 = (bf16[2048,128]{1,0:T(8,128)(2,1)S(1)}, bf16[2048,128]{1,0:T(8,128)(2,1)}, u32[]{:S(2)}, u32[]{:S(2)}) collective-permute-start(bf16[2048,128]{1,0:T(8,128)(2,1)S(1)} %collective-permute-done.10.refs_10_), channel_id=1, source_target_pairs={{0,12},{4,0},{8,4},{12,8},{1,13},{5,1},{9,5},{13,9},{2,14},{6,2},{... | collective-permute-start | bytes 1572872 | tf_op jit(solution)/shard_map/ppermute | solution.py:20
  71.9 9.4 %copy-start.17 = (bf16[2048,128]{1,0:T(8,128)(2,1)}, bf16[2048,128]{1,0:T(8,128)(2,1)S(1)}, u32[]{:S(2)}) copy-start(bf16[2048,128]{1,0:T(8,128)(2,1)S(1)} %collective-permute-done.3.refs_3_) | copy-start | bytes 1572868
  71.9 9.4 %collective-permute-start.11 = (bf16[2048,128]{1,0:T(8,128)(2,1)S(1)}, bf16[2048,128]{1,0:T(8,128)(2,1)S(1)}, u32[]{:S(2)}, u32[]{:S(2)}) collective-permute-start(bf16[2048,128]{1,0:T(8,128)(2,1)S(1)} %collective-permute-done.10.refs_10_), channel_id=1, source_target_pairs={{0,16},{16,0},{1,17},{17,1},{2,18},{18,2},{3,19},{19,3},{4,20},{20... | collective-permute-start | bytes 1572872 | tf_op jit(solution)/shard_map/ppermute | solution.py:24
  71.9 9.4 %copy-start.18 = (bf16[32,16,512]{2,1,0:T(8,128)(2,1)}, bf16[32,16,512]{2,1,0:T(8,128)(2,1)S(1)}, u32[]{:S(2)}) copy-start(bf16[32,16,512]{2,1,0:T(8,128)(2,1)S(1)} %collective-permute-done.18.refs_2_) | copy-start | bytes 1572868
  72.0 21.5 %collective-permute-start.5 = (bf16[2048,128]{1,0:T(8,128)(2,1)S(1)}, bf16[2048,128]{1,0:T(8,128)(2,1)}, u32[]{:S(2)}, u32[]{:S(2)}) collective-permute-start(bf16[2048,128]{1,0:T(8,128)(2,1)S(1)} %collective-permute-done.4.refs_4_), channel_id=1, source_target_pairs={{0,16},{16,0},{1,17},{17,1},{2,18},{18,2},{3,19},{19,3},{4,20},{20... | collective-permute-start | bytes 1572872 | tf_op jit(solution)/shard_map/ppermute | solution.py:24
  72.4 8.9 %copy-start.20 = (bf16[32,16,512]{2,1,0:T(8,128)(2,1)}, bf16[32,16,512]{2,1,0:T(8,128)(2,1)S(1)}, u32[]{:S(2)}) copy-start(bf16[32,16,512]{2,1,0:T(8,128)(2,1)S(1)} %collective-permute-done.19.refs_3_) | copy-start | bytes 1572868
  72.4 21.1 %collective-permute-start.7 = (bf16[2048,128]{1,0:T(8,128)(2,1)}, bf16[2048,128]{1,0:T(8,128)(2,1)}, u32[]{:S(2)}, u32[]{:S(2)}) collective-permute-start(bf16[2048,128]{1,0:T(8,128)(2,1)} %collective-permute-done.6.refs_6_), channel_id=1, source_target_pairs={{0,16},{16,0},{1,17},{17,1},{2,18},{18,2},{3,19},{19,3},{4,20},{20... | collective-permute-start | bytes 1572872 | tf_op jit(solution)/shard_map/ppermute | solution.py:24
  80.8 12.7 %collective-permute-start.9 = (bf16[2048,128]{1,0:T(8,128)(2,1)}, bf16[2048,128]{1,0:T(8,128)(2,1)}, u32[]{:S(2)}, u32[]{:S(2)}) collective-permute-start(bf16[2048,128]{1,0:T(8,128)(2,1)} %collective-permute-done.8.refs_8_), channel_id=1, source_target_pairs={{0,16},{16,0},{1,17},{17,1},{2,18},{18,2},{3,19},{19,3},{4,20},{20... | collective-permute-start | bytes 1572872 | tf_op jit(solution)/shard_map/ppermute | solution.py:24
  80.8 12.7 %collective-permute-start.13 = (bf16[2048,128]{1,0:T(8,128)(2,1)}, bf16[2048,128]{1,0:T(8,128)(2,1)}, u32[]{:S(2)}, u32[]{:S(2)}) collective-permute-start(bf16[2048,128]{1,0:T(8,128)(2,1)} %collective-permute-done.12.refs_12_), channel_id=1, source_target_pairs={{0,16},{16,0},{1,17},{17,1},{2,18},{18,2},{3,19},{19,3},{4,20},{20... | collective-permute-start | bytes 1572872 | tf_op jit(solution)/shard_map/ppermute | solution.py:24
  81.3 0.8 copy-start.19
  82.2 11.4 %collective-permute-start.15 = (bf16[2048,128]{1,0:T(8,128)(2,1)}, bf16[2048,128]{1,0:T(8,128)(2,1)}, u32[]{:S(2)}, u32[]{:S(2)}) collective-permute-start(bf16[2048,128]{1,0:T(8,128)(2,1)} %collective-permute-done.14.refs_14_), channel_id=1, source_target_pairs={{0,16},{16,0},{1,17},{17,1},{2,18},{18,2},{3,19},{19,3},{4,20},{20... | collective-permute-start | bytes 1572872 | tf_op jit(solution)/shard_map/ppermute | solution.py:24
  109.7 36.5 %all-to-all-start.1 = ((bf16[32,256,128]{2,1,0:T(8,128)(2,1)}), bf16[32,256,128]{2,1,0:T(8,128)(2,1)S(1)}, u32[]{:S(2)}, u32[]{:S(2)}) async-start(bf16[32,256,128]{2,1,0:T(8,128)(2,1)} %bitcast.28), calls=%async_computation.1 | async-start | bytes 4194304 | tf_op jit(solution)/shard_map/all_to_all | solution.py:279
  117.8 49.1 %collective-permute-start.24 = (bf16[1024,512]{1,0:T(8,128)(2,1)}, bf16[1024,512]{1,0:T(8,128)(2,1)S(1)}, u32[]{:S(2)}, u32[]{:S(2)}) collective-permute-start(bf16[1024,512]{1,0:T(8,128)(2,1)} %refs_0_.1), channel_id=1, source_target_pairs={{0,32},{32,64},{64,96},{96,0},{1,33},{33,65},{65,97},{97,1},{2,34}... | collective-permute-start | bytes 3145736 | tf_op jit(solution)/shard_map/ppermute | solution.py:20
  119.7 48.2 %collective-permute-start.26 = (bf16[1024,512]{1,0:T(8,128)(2,1)}, bf16[1024,512]{1,0:T(8,128)(2,1)}, u32[]{:S(2)}, u32[]{:S(2)}) collective-permute-start(bf16[1024,512]{1,0:T(8,128)(2,1)} %refs_0_.1), channel_id=1, source_target_pairs={{0,96},{32,0},{64,32},{96,64},{1,97},{33,1},{65,33},{97,65},{2,98}... | collective-permute-start | bytes 3145736 | tf_op jit(solution)/shard_map/ppermute | solution.py:20
  146.1 1.4 copy-start
  151.6 35.2 %all-to-all-start.2 = ((bf16[16,32,16,128]{3,2,1,0:T(8,128)(2,1)}), bf16[16,32,16,128]{3,2,1,0:T(8,128)(2,1)S(1)}, u32[]{:S(2)}, u32[]{:S(2)}) async-start(bf16[16,32,16,128]{3,2,1,0:T(8,128)(2,1)} %bitcast.27), calls=%async_computation.2 | async-start | bytes 4194304 | tf_op jit(solution)/shard_map/all_to_all | solution.py:281
  157.8 15.6 %copy-start.21 = (f32[256]{0:T(256)S(1)}, f32[256]{0:T(256)}, u32[]{:S(2)}) copy-start(f32[256]{0:T(256)} %param.13) | copy-start | bytes 3076
  157.8 26.1 %copy-start.8 = (f32[32]{0:T(128)S(1)}, f32[32]{0:T(128)}, u32[]{:S(2)}) copy-start(f32[32]{0:T(128)} %param.11) | copy-start | bytes 388
  157.8 26.8 %copy-start.9 = (f32[32]{0:T(128)S(1)}, f32[32]{0:T(128)}, u32[]{:S(2)}) copy-start(f32[32]{0:T(128)} %param.12) | copy-start | bytes 388
  166.9 19.8 %copy-start.2 = (bf16[1024,512]{1,0:T(8,128)(2,1)}, bf16[1024,512]{1,0:T(8,128)(2,1)S(1)}, u32[]{:S(2)}) copy-start(bf16[1024,512]{1,0:T(8,128)(2,1)S(1)} %collective-permute-done.24.refs_2_) | copy-start | bytes 3145732
  167.8 14.9 %collective-permute-start.28 = (bf16[512,512]{1,0:T(8,128)(2,1)}, bf16[512,512]{1,0:T(8,128)(2,1)}, u32[]{:S(2)}, u32[]{:S(2)}) collective-permute-start(bf16[512,512]{1,0:T(8,128)(2,1)} %slice.8), channel_id=1, source_target_pairs={{0,32},{32,64},{64,96},{96,0},{1,33},{33,65},{65,97},{97,1},{2,34}... | collective-permute-start | bytes 1572872 | tf_op jit(solution)/shard_map/ppermute | solution.py:20
  169.7 14.1 %collective-permute-start.30 = (bf16[512,512]{1,0:T(8,128)(2,1)}, bf16[512,512]{1,0:T(8,128)(2,1)}, u32[]{:S(2)}, u32[]{:S(2)}) collective-permute-start(bf16[512,512]{1,0:T(8,128)(2,1)} %slice.9), channel_id=1, source_target_pairs={{0,96},{32,0},{64,32},{96,64},{1,97},{33,1},{65,33},{97,65},{2,98}... | collective-permute-start | bytes 1572872 | tf_op jit(solution)/shard_map/ppermute | solution.py:20
  172.9 13.2 %collective-permute-start.23 = (bf16[1024,512]{1,0:T(8,128)(2,1)}, bf16[1024,512]{1,0:T(8,128)(2,1)}, u32[]{:S(2)}, u32[]{:S(2)}) collective-permute-start(bf16[1024,512]{1,0:T(8,128)(2,1)} %refs_0_.1), channel_id=1, source_target_pairs={{0,16},{16,0},{1,17},{17,1},{2,18},{18,2},{3,19},{19,3},{4,20},{20... | collective-permute-start | bytes 3145736 | tf_op jit(solution)/shard_map/ppermute | solution.py:24
  172.9 13.2 %collective-permute-start.25 = (bf16[1024,512]{1,0:T(8,128)(2,1)S(1)}, bf16[1024,512]{1,0:T(8,128)(2,1)}, u32[]{:S(2)}, u32[]{:S(2)}) collective-permute-start(bf16[1024,512]{1,0:T(8,128)(2,1)S(1)} %collective-permute-done.24.refs_2_), channel_id=1, source_target_pairs={{0,16},{16,0},{1,17},{17,1},{2,18},{18,2},{3,19},{19,3},{4,20},{20... | collective-permute-start | bytes 3145736 | tf_op jit(solution)/shard_map/ppermute | solution.py:24
  173.4 12.7 %collective-permute-start.27 = (bf16[1024,512]{1,0:T(8,128)(2,1)}, bf16[1024,512]{1,0:T(8,128)(2,1)}, u32[]{:S(2)}, u32[]{:S(2)}) collective-permute-start(bf16[1024,512]{1,0:T(8,128)(2,1)} %collective-permute-done.26.refs_4_), channel_id=1, source_target_pairs={{0,16},{16,0},{1,17},{17,1},{2,18},{18,2},{3,19},{19,3},{4,20},{20... | collective-permute-start | bytes 3145736 | tf_op jit(solution)/shard_map/ppermute | solution.py:24
  182.7 3.3 %collective-permute-start.29 = (bf16[512,512]{1,0:T(8,128)(2,1)}, bf16[512,512]{1,0:T(8,128)(2,1)}, u32[]{:S(2)}, u32[]{:S(2)}) collective-permute-start(bf16[512,512]{1,0:T(8,128)(2,1)} %collective-permute-done.28.refs_6_), channel_id=1, source_target_pairs={{0,16},{16,0},{1,17},{17,1},{2,18},{18,2},{3,19},{19,3},{4,20},{20... | collective-permute-start | bytes 1572872 | tf_op jit(solution)/shard_map/ppermute | solution.py:24
  183.9 2.3 %collective-permute-start.31 = (bf16[512,512]{1,0:T(8,128)(2,1)}, bf16[512,512]{1,0:T(8,128)(2,1)}, u32[]{:S(2)}, u32[]{:S(2)}) collective-permute-start(bf16[512,512]{1,0:T(8,128)(2,1)} %collective-permute-done.30.refs_8_), channel_id=1, source_target_pairs={{0,16},{16,0},{1,17},{17,1},{2,18},{18,2},{3,19},{19,3},{4,20},{20... | collective-permute-start | bytes 1572872 | tf_op jit(solution)/shard_map/ppermute | solution.py:24
  186.7 1.4 copy-start.1

commit v3 on v2

--- a/solution.py
+++ b/solution.py
@@ -176,9 +176,7 @@
             swapped[pl.ds(group * per + k, nj, stride=nb), :] = jnp.concatenate(
                 [flipped[i * nj : (i + 1) * nj, :] for i in range(ni)], axis=1
             )
-    held = swapped[...].astype(BF16)
-    for p in range(holes_ref.shape[0]):
-        holes_ref[p] = held
+    holes_ref[...] = swapped[...].astype(BF16)
 
 
 def settle(parts):
@@ -187,41 +185,60 @@
         settle_kernel,
         out_shape=(
             jax.ShapeDtypeStruct((128, 512), F32),
-            jax.ShapeDtypeStruct((16, rows, wide), BF16),
+            jax.ShapeDtypeStruct((rows, wide), BF16),
         ),
         scratch_shapes=[pltpu.VMEM((rows, wide), F32), pltpu.VMEM((rows, wide), F32)],
         name="settle",
     )(parts)
 
 
-def cycle_kernel(where_ref, holes_ref, *refs):
-    pieces, (direct_ref, row_ref, col_ref, out_ref) = refs[:10], refs[10:]
-    peers, _, nb, wide = holes_ref.shape
-    acc = direct_ref[...]
-    chunks = [(s, side, n * 2 + side, 0, 4) for n, s in enumerate((0, 3, 1)) for side in (0, 1)]
-    chunks += [(2, side, 6 + 2 * part + side, 2 * part, 2) for part in (0, 1) for side in (0, 1)]
-    for shift, side, at, base, count in chunks:
-        owner = ((where_ref[0] + shift) % 4) * 2 + (where_ref[1] ^ side)
-        lhs = jnp.concatenate(
-            [
-                holes_ref[:, owner * 4 + base + k].reshape(peers * nb, wide).T
-                for k in range(count)
-            ],
-            axis=1,
-        )
-        acc = acc + jnp.dot(lhs, pieces[at][...], preferred_element_type=F32)
-    out_ref[...] = acc / (row_ref[...] + col_ref[...])
-
-
-def finish(where, holes, pieces, direct, row, col):
+def cycle_kernel(where_ref, *refs):
+    holes, pieces, direct_ref = refs[:4], refs[4:20], refs[20]
+    outs, held, lhs = refs[21:25], refs[25], refs[26]
+    _, nb, wide = holes[0].shape
+    deep = 4 * 4 * nb
+    for far, ref in enumerate(holes):
+        start = pl.multiple_of((where_ref[2] + 4 - far) % 4 * nb, nb)
+        held[:, pl.ds(start, nb), :] = ref[...]
+    for n in range(8):
+        owner = (where_ref[0] + SHIFTS[n // 2]) % 4 * 2 + (where_ref[1] ^ (n % 2))
+        block = held[pl.ds(owner * 4, 4)].reshape(deep, wide)
+        lhs[:, n * deep : (n + 1) * deep] = block.T
+    for column in range(4):
+        acc = None
+        for n in range(8):
+            ref = pieces[n // 2 * 4 + column // 2 * 2 + n % 2]
+            row = column % 2 * deep
+            got = jnp.dot(
+                lhs[:, n * deep : (n + 1) * deep],
+                ref[row : row + deep, :],
+                preferred_element_type=F32,
+            )
+            acc = got if acc is None else acc + got
+        if column == 0:
+            outs[0][...] = direct_ref[...] + acc
+        else:
+            outs[column][...] = acc.astype(BF16)
+
+
+SHIFTS = (0, 3, 1, 2)
+
+
+def partial_cycle(where, holes, pieces, direct):
+    nk, nb, wide = holes[0].shape
     return pl.pallas_call(
         cycle_kernel,
         in_specs=[pl.BlockSpec(memory_space=pltpu.SMEM)]
-        + [pl.BlockSpec(memory_space=pltpu.VMEM)] * (len(pieces) + 4),
-        out_specs=pl.BlockSpec(memory_space=pltpu.VMEM),
-        out_shape=jax.ShapeDtypeStruct(direct.shape, F32),
+        + [pl.BlockSpec(memory_space=pltpu.VMEM)] * (len(pieces) + 5),
+        out_specs=[pl.BlockSpec(memory_space=pltpu.VMEM)] * 4,
+        out_shape=[jax.ShapeDtypeStruct(direct.shape, F32)]
+        + [jax.ShapeDtypeStruct(direct.shape, BF16)] * 3,
+        scratch_shapes=[
+            pltpu.VMEM((nk, 4 * nb, wide), BF16),
+            pltpu.VMEM((wide, 8 * 16 * nb), BF16),
+        ],
         name="cycle",
-    )(where, holes, *pieces, direct, row, col)
+    )(where, *holes, *pieces, direct)
 
 
 def update(
@@ -255,6 +272,15 @@
     ]
     own = turn(scalars(half), *own)
 
+    grid = cycle_matrix.reshape(nj // 8, 4, -1, cycle_matrix.shape[1])
+    mixed = []
+    for k in range(4):
+        v = lax.dynamic_index_in_dim(grid, (x + k) % 4, 1, keepdims=False)
+        v = v.reshape(-1, grid.shape[3])
+        mixed.append(ring(v, "x", k) if k else v)
+    base = [jnp.concatenate(mixed[:2]), jnp.concatenate(mixed[2:])]
+    base, own = lax.optimization_barrier((base, own))
+
     low, high = own
     left_low, right_high = ring(low, "x", 1), ring(high, "x", -1)
     left_high, right_low = ring(high, "x", 1), ring(low, "x", -1)
@@ -262,7 +288,9 @@
     turned = pair_factor.transpose(1, 0, 2)
     turned, *own = lax.optimization_barrier((turned, *own))
     pair = [lax.ppermute(turned, ("core", "z"), amplitude_route(alpha)) for alpha in range(2)]
-    before, after = ring(cycle_matrix, "y", 1), ring(cycle_matrix, "y", -1)
+    before, after = [ring(base[0], "y", 1)], [ring(base[1], "y", -1)]
+    before.append(ring(base[1], "y", 1))
+    after.insert(0, ring(base[0], "y", -1))
     far = [ring(left_low, "x", 1), ring(right_high, "x", -1)]
     pair += [sibling(v) for v in pair]
     amps = []
@@ -271,20 +299,20 @@
     for v in far:
         amps += [v, sibling(v)]
 
+    ends = [ring(before[0], "y", 1), ring(after[1], "y", -1)]
+
     w = form_integrals(scalars(y), pair, blocks)
 
     spots = scalars(x, (x + 3) % 4, (x + 1) % 4, (x + 2) % 4, core, 2 * core + half)
     parts = partial_ladder(spots, amps, w)
     parts = parts.reshape(32, -1, parts.shape[-1])
     parts = lax.all_to_all(parts, ("y", "core", "z"), 0, 0, tiled=True)
+    matrix = []
+    for v in (*base, *before, *after, *ends):
+        matrix += [v, sibling(v)]
     direct, holes = settle(parts.reshape(4, 2, 4, -1, parts.shape[-1]))
-    holes = lax.all_to_all(holes.reshape(16, nj, 16, 128), VIR, 0, 0, tiled=True)
-
-    mid = cycle_matrix.shape[0] // 2
-    matrix = []
-    ends = ring(before[:mid], "y", 1), ring(after[mid:], "y", -1)
-    for v in (cycle_matrix, before, after, *ends):
-        matrix += [v, sibling(v)]
+    holes = holes.reshape(nj, -1, holes.shape[1])
+    holes = [holes] + [ring(holes, "z", k) for k in (1, 2, 3)]
 
     occ_rows = nj // 8
     cols = virt_energy.shape[0] // 16
@@ -292,7 +320,10 @@
     virt_here = lax.dynamic_slice_in_dim(virt_energy, (4 * x + z) * cols, cols, 0)
     row = (block_energy[None, :] - occ_here[:, None]).reshape(-1, 1)
     col = (virt_here[:, None] - occ_energy[None, :]).reshape(1, -1)
-    return finish(scalars(y, core), holes, matrix, direct, row, col)
+    total, *sums = partial_cycle(scalars(y, core, z), holes, matrix, direct)
+    for k, v in enumerate(sums):
+        total = total + ring(v, "x", -k - 1).astype(F32)
+    return total / (row + col)
 
 
 def solution(mesh):

time: 196 us -> 226 us (1.15)
  waiting for transfers between devices: 87 us -> 113 us
  starting transfers between devices: 53.1 us -> 59.4 us
  local copies, waits for them, and re-layouts: 13.7 us -> 10.7 us
  other arithmetic: 0.73 us -> 3.59 us
    ppermute x13 -> x24, waiting for transfers between devices: 53.1 us -> 110 us  [ring(): return lax.ppermute(value, axis, [(i, (i + shift) % n) for i in range(n)])]
    all_to_all x1, waiting for transfers between devices: 25 us -> 0.01 us  [update(): parts = lax.all_to_all(parts, ('y', 'core', 'z'), 0, 0, tiled=True)]
    ppermute x13 -> x24, starting transfers between devices: 21.1 us -> 35.6 us  [ring(): return lax.ppermute(value, axis, [(i, (i + shift) % n) for i in range(n)])]
    all_to_all x1 -> x0, starting transfers between devices: 6.21 us -> none  [update(): lax.all_to_all(holes.reshape(16, nj, 16, 128), VIR, 0, 0, tiled=True)]
    all_to_all x1, waiting for transfers between devices: 6.68 us -> 3.19 us  [update(): lax.all_to_all(block.reshape(32, na // 2, nq, nc // 2), ('core', 'x', 'z'...]
    slice x2 -> x0, local copies, waits for them, and re-layouts: 2.77 us -> none  [update(): ends = (ring(before[:mid], 'y', 1), ring(after[mid:], 'y', -1))]
    unnamed x46 -> x62, local copies, waits for them, and re-layouts: 5.32 us -> 5.37 us
  transfers between devices with their start and end apart: 35 -> 48, of which waited for: 14 -> 19; matrix products, arithmetic and copies ran while one was open for 4% -> 3% of each run, Pallas kernels for 9% -> 7%
where the time goes in v3:
time: 226 us; the launch traced here: 225 us
  waiting for transfers between devices  113 us (50%)
  starting transfers between devices  59.4 us (26%)
  Pallas kernels  38.1 us (17%)
  local copies, waits for them, and re-layouts  10.7 us (5%)
  other arithmetic  3.59 us (2%)
    ppermute x24, waiting for transfers between devices, ring(): return lax.ppermute(value, axis, [(i, (i + shift) % n) for i in range(n)])  110 us
    ppermute x24, starting transfers between devices, ring(): return lax.ppermute(value, axis, [(i, (i + shift) % n) for i in range(n)])  35.6 us
    pallas_call x1, Pallas kernels, partial_ladder(): pl.pallas_call(ladder_kernel, grid_spec=pltpu.PrefetchScalarGridSpec(num_...  16.1 us
    pallas_call x1, Pallas kernels, form_integrals(): pl.pallas_call(integrals_kernel, grid_spec=pltpu.PrefetchScalarGridSpec(n...  10.6 us
    all_to_all x1, starting transfers between devices, update(): lax.all_to_all(block.reshape(32, na // 2, nq, nc // 2), ('core', 'x', 'z'...  8.27 us
    all_to_all x1, starting transfers between devices, update(): parts = lax.all_to_all(parts, ('y', 'core', 'z'), 0, 0, tiled=True)  7.23 us
    pallas_call x1, Pallas kernels, partial_cycle(): pl.pallas_call(cycle_kernel, in_specs=[pl.BlockSpec(memory_space=pltpu.SM...  5.67 us
    unnamed x62, local copies, waits for them, and re-layouts  5.37 us
  transfers between devices with their start and end apart: 48, of which 19 were waited for; matrix products, arithmetic and copies ran while one was open for 3% of the time, Pallas kernels for 7%

profile of v3, /device:TPU:0, one launch (start us, length us, event | category | flops | bytes accessed | tf_op | source)
XLA Modules:
  0.0 225.1 jit_solution(6049418811235327507)
XLA Ops:
  0.0 1.0 reshape.81
  1.1 1.1 broadcast_in_dim.2
  2.1 8.3 %all-to-all-start = ((bf16[32,16,4,128]{3,2,1,0:T(4,128)(2,1)}), bf16[32,16,4,128]{3,2,1,0:T(4,128)(2,1)S(1)}, u32[]{:S(2)}, u32[]{:S(2)}) async-start(bf16[32,16,4,128]{3,2,1,0:T(4,128)(2,1)} %bitcast.19), calls=%async_computation | async-start | bytes 1048576 | tf_op jit(solution)/shard_map/all_to_all | solution.py:257
  10.5 0.8 constant_dynamic-slice_fusion.1
  11.3 3.3 %collective-permute-start.1 = (bf16[256,512]{1,0:T(8,128)(2,1)}, bf16[256,512]{1,0:T(8,128)(2,1)}, u32[]{:S(2)}, u32[]{:S(2)}) collective-permute-start(bf16[256,512]{1,0:T(8,128)(2,1)} %bitcast.12), channel_id=1, source_target_pairs={{0,8},{4,12},{8,0},{12,4},{1,9},{5,13},{9,1},{13,5},{2,10},{6,14},... | collective-permute-start | bytes 786440 | tf_op jit(solution)/shard_map/ppermute | solution.py:20
  14.6 0.6 copy.20
  15.2 1.2 dynamic-slice_bitcast_fusion
  16.4 1.7 collective-permute-start.3
  18.1 1.5 collective-permute-start.4
  19.5 3.2 %all-to-all-done = bf16[32,16,4,128]{3,2,1,0:T(4,128)(2,1)S(1)} async-done(((bf16[32,16,4,128]{3,2,1,0:T(4,128)(2,1)}), bf16[32,16,4,128]{3,2,1,0:T(4,128)(2,1)S(1)}, u32[]{:S(2)}, u32[]{:S(2)}) %all-to-all-start) | async-done | bytes 524320 | tf_op jit(solution)/shard_map/all_to_all | solution.py:257
  23.0 1.6 collective-permute-start.23
  24.6 0.7 collective-permute-start.2
  25.3 0.9 collective-permute-done.1
  26.1 0.6 collective-permute-start
  27.0 4.9 %collective-permute-done.2 = bf16[256,512]{1,0:T(8,128)(2,1)S(1)} collective-permute-done((bf16[256,512]{1,0:T(8,128)(2,1)S(1)}, bf16[256,512]{1,0:T(8,128)(2,1)S(1)}, u32[]{:S(2)}, u32[]{:S(2)}) %collective-permute-start.2) | collective-permute-done | bytes 262176 | tf_op jit(solution)/shard_map/ppermute | solution.py:20
  31.9 1.0 pad_maximum_fusion.1.refs_6_
  32.9 2.2 collective-permute-done
  35.2 3.1 %collective-permute-start.24 = (bf16[16,128,128]{2,1,0:T(8,128)(2,1)S(1)}, bf16[16,128,128]{2,1,0:T(8,128)(2,1)S(1)}, u32[]{:S(2)}, u32[]{:S(2)}) collective-permute-start(bf16[16,128,128]{2,1,0:T(8,128)(2,1)S(1)} %bitcast.46), channel_id=1, source_target_pairs={{0,96},{32,0},{64,32},{96,64},{1,97},{33,1},{65,33},{97,65},{2,98}... | collective-permute-start | bytes 1572872 | tf_op jit(solution)/shard_map/ppermute | solution.py:20
  38.3 0.6 collective-permute-start.25
  38.9 0.8 copy-done.13
  39.7 2.4 %turn.1 = (bf16[2048,128]{1,0:T(8,128)(2,1)}, bf16[2048,128]{1,0:T(8,128)(2,1)}) custom-call(s32[1]{0:T(128)} %bitcast.14.where_ref, bf16[32,64,128]{2,1,0:T(8,128)(2,1)} %copy-done.13, bf16[32,64,128]{2,1,0:T(8,128)(2,1)} %collective-permute-done.4.one_ref), custom_call_target="tpu_custom_call" | custom-call | tf_op jit(solution)/shard_map/turn/pallas_call | solution.py:80
  42.1 0.7 collective-permute-start.19
  42.8 1.6 collective-permute-start.20
  44.4 15.2 %collective-permute-done.24.refs_6_ = bf16[16,128,128]{2,1,0:T(8,128)(2,1)S(1)} collective-permute-done((bf16[16,128,128]{2,1,0:T(8,128)(2,1)S(1)}, bf16[16,128,128]{2,1,0:T(8,128)(2,1)S(1)}, u32[]{:S(2)}, u32[]{:S(2)}) %collective-permute-start.24) | collective-permute-done | bytes 524320 | tf_op jit(solution)/shard_map/ppermute | solution.py:20
  59.6 0.7 collective-permute-start.13
  60.3 1.3 collective-permute-start.9
  61.6 2.0 collective-permute-start.11
  64.1 7.2 %collective-permute-done.13.refs_10_ = bf16[2048,128]{1,0:T(8,128)(2,1)} collective-permute-done((bf16[2048,128]{1,0:T(8,128)(2,1)}, bf16[2048,128]{1,0:T(8,128)(2,1)}, u32[]{:S(2)}, u32[]{:S(2)}) %collective-permute-start.13) | collective-permute-done | bytes 524320 | tf_op jit(solution)/shard_map/ppermute | solution.py:20
  71.3 0.6 collective-permute-done.9.refs_6_
  71.9 6.5 %collective-permute-done.11.refs_8_ = bf16[2048,128]{1,0:T(8,128)(2,1)} collective-permute-done((bf16[2048,128]{1,0:T(8,128)(2,1)}, bf16[2048,128]{1,0:T(8,128)(2,1)}, u32[]{:S(2)}, u32[]{:S(2)}) %collective-permute-start.11) | collective-permute-done | bytes 524320 | tf_op jit(solution)/shard_map/ppermute | solution.py:20
  78.4 3.2 %collective-permute-start.17 = (bf16[2048,128]{1,0:T(8,128)(2,1)}, bf16[2048,128]{1,0:T(8,128)(2,1)}, u32[]{:S(2)}, u32[]{:S(2)}) collective-permute-start(bf16[2048,128]{1,0:T(8,128)(2,1)} %collective-permute-done.13.refs_10_), channel_id=1, source_target_pairs={{0,12},{4,0},{8,4},{12,8},{1,13},{5,1},{9,5},{13,9},{2,14},{6,2},{... | collective-permute-start | bytes 1572872 | tf_op jit(solution)/shard_map/ppermute | solution.py:20
  82.2 6.6 %collective-permute-done.15.refs_12_ = bf16[2048,128]{1,0:T(8,128)(2,1)} collective-permute-done((bf16[2048,128]{1,0:T(8,128)(2,1)S(1)}, bf16[2048,128]{1,0:T(8,128)(2,1)}, u32[]{:S(2)}, u32[]{:S(2)}) %collective-permute-start.15) | collective-permute-done | bytes 524320 | tf_op jit(solution)/shard_map/ppermute | solution.py:20
  88.9 0.5 collective-permute-start.16
  89.4 0.8 copy-done.27
  90.3 0.7 stack.44.where_ref
  91.0 10.6 %integrals.1.refs_16_ = bf16[1024,4096]{1,0:T(8,128)(2,1)} custom-call(s32[1]{0:T(128)} %bitcast.where_ref, bf16[32,16,512]{2,1,0:T(8,128)(2,1)} %copy-done.21, bf16[32,16,512]{2,1,0:T(8,128)(2,1)} %copy-done.23, bf16[32,16,512]{2,1,0:T(8,128)(2,1)} %copy-done.26, bf16[32,16,512]{2,1,0:T(8,128)(2,1)} %copy-done.28, bf16[16,128,128]{2,1,0:T(8,128)(2,1)} %bitcast.48, ...), custom_call_target="tpu_custom_call" | custom-call | flops 4294967296 | bytes 12582912 | tf_op jit(solution)/shard_map/integrals/pallas_call | solution.py:50
  101.7 16.1 %ladder.1 = bf16[4,2,4,16,16,128]{5,4,3,2,1,0:T(8,128)(2,1)} custom-call(s32[6]{0:T(128)} %stack.44.where_ref, bf16[2048,128]{1,0:T(8,128)(2,1)} %get-tuple-element.24.refs_0_, bf16[2048,128]{1,0:T(8,128)(2,1)} %copy-done.24, bf16[2048,128]{1,0:T(8,128)(2,1)} %get-tuple-element.25.refs_2_, bf16[2048,128]{1,0:T(8,128)(2,1)} %copy-done.25, ...), custom_call_target="tpu_custom_call" | custom-call | flops 8589934592 | bytes 18874368 | tf_op jit(solution)/shard_map/ladder/pallas_call | solution.py:134
  117.9 7.2 %all-to-all-start.1 = ((bf16[32,256,128]{2,1,0:T(8,128)(2,1)}), bf16[32,256,128]{2,1,0:T(8,128)(2,1)S(1)}, u32[]{:S(2)}, u32[]{:S(2)}) async-start(bf16[32,256,128]{2,1,0:T(8,128)(2,1)} %bitcast.41), calls=%async_computation.1 | async-start | bytes 4194304 | tf_op jit(solution)/shard_map/all_to_all | solution.py:309
  125.1 1.9 collective-permute-start.31
  127.0 1.4 collective-permute-start.37
  128.4 0.6 collective-permute-start.33
  129.0 2.7 %collective-permute-start.35 = (bf16[512,512]{1,0:T(8,128)(2,1)S(1)}, bf16[512,512]{1,0:T(8,128)(2,1)}, u32[]{:S(2)}, u32[]{:S(2)}) collective-permute-start(bf16[512,512]{1,0:T(8,128)(2,1)S(1)} %pad_maximum_fusion.refs_4_), channel_id=1, source_target_pairs={{0,96},{32,0},{64,32},{96,64},{1,97},{33,1},{65,33},{97,65},{2,98}... | collective-permute-start | bytes 1572872 | tf_op jit(solution)/shard_map/ppermute | solution.py:20
  131.7 31.8 %collective-permute-done.31.refs_8_ = bf16[512,512]{1,0:T(8,128)(2,1)S(1)} collective-permute-done((bf16[512,512]{1,0:T(8,128)(2,1)S(1)}, bf16[512,512]{1,0:T(8,128)(2,1)S(1)}, u32[]{:S(2)}, u32[]{:S(2)}) %collective-permute-start.31) | collective-permute-done | bytes 524320 | tf_op jit(solution)/shard_map/ppermute | solution.py:20
  163.5 1.0 collective-permute-done.37.refs_14_
  164.5 10.3 %collective-permute-done.33.refs_10_ = bf16[512,512]{1,0:T(8,128)(2,1)} collective-permute-done((bf16[512,512]{1,0:T(8,128)(2,1)S(1)}, bf16[512,512]{1,0:T(8,128)(2,1)}, u32[]{:S(2)}, u32[]{:S(2)}) %collective-permute-start.33) | collective-permute-done | bytes 524320 | tf_op jit(solution)/shard_map/ppermute | solution.py:20
  174.8 1.1 collective-permute-start.41
  176.6 8.9 %collective-permute-done.39.refs_16_ = bf16[512,512]{1,0:T(8,128)(2,1)} collective-permute-done((bf16[512,512]{1,0:T(8,128)(2,1)S(1)}, bf16[512,512]{1,0:T(8,128)(2,1)}, u32[]{:S(2)}, u32[]{:S(2)}) %collective-permute-start.39) | collective-permute-done | bytes 524320 | tf_op jit(solution)/shard_map/ppermute | solution.py:20
  185.5 2.5 %collective-permute-done.41.refs_18_ = bf16[512,512]{1,0:T(8,128)(2,1)} collective-permute-done((bf16[512,512]{1,0:T(8,128)(2,1)}, bf16[512,512]{1,0:T(8,128)(2,1)}, u32[]{:S(2)}, u32[]{:S(2)}) %collective-permute-start.41) | collective-permute-done | bytes 524320 | tf_op jit(solution)/shard_map/ppermute | solution.py:20
  188.0 0.8 copy-done.8
  189.4 1.3 copy-done
  190.7 3.2 %settle.1 = (f32[128,512]{1,0:T(8,128)}, bf16[512,128]{1,0:T(8,128)(2,1)}) custom-call(bf16[4,2,4,256,128]{4,3,2,1,0:T(8,128)(2,1)} %bitcast.39), custom_call_target="tpu_custom_call" | custom-call | tf_op jit(solution)/shard_map/settle/pallas_call | solution.py:184
  194.0 1.8 collective-permute-start.26
  195.8 2.5 %collective-permute-start.27 = (bf16[32,16,128]{2,1,0:T(8,128)(2,1)}, bf16[32,16,128]{2,1,0:T(8,128)(2,1)S(1)}, u32[]{:S(2)}, u32[]{:S(2)}) collective-permute-start(bf16[32,16,128]{2,1,0:T(8,128)(2,1)} %bitcast.55), channel_id=1, source_target_pairs={{0,2},{1,3},{2,0},{3,1},{4,6},{5,7},{6,4},{7,5},{8,10},{9,11},{10,... | collective-permute-start | bytes 393224 | tf_op jit(solution)/shard_map/ppermute | solution.py:20
  198.3 1.5 collective-permute-start.28
  200.0 0.7 pad_add_fusion.where_ref
  200.8 3.9 %collective-permute-done.27.refs_2_ = bf16[32,16,128]{2,1,0:T(8,128)(2,1)S(1)} collective-permute-done((bf16[32,16,128]{2,1,0:T(8,128)(2,1)}, bf16[32,16,128]{2,1,0:T(8,128)(2,1)S(1)}, u32[]{:S(2)}, u32[]{:S(2)}) %collective-permute-start.27) | collective-permute-done | bytes 131104 | tf_op jit(solution)/shard_map/ppermute | solution.py:20
  204.8 0.6 copy-done.15
  205.4 5.7 %cycle.1 = (f32[128,512]{1,0:T(8,128)}, bf16[128,512]{1,0:T(8,128)(2,1)}, bf16[128,512]{1,0:T(8,128)(2,1)}, bf16[128,512]{1,0:T(8,128)(2,1)}) custom-call(s32[3]{0:T(128)} %pad_add_fusion.where_ref, bf16[32,16,128]{2,1,0:T(8,128)(2,1)} %bitcast.57, bf16[32,16,128]{2,1,0:T(8,128)(2,1)} %copy-done.14, bf16[32,16,128]{2,1,0:T(8,128)(2,1)} %copy-done.15, ...), custom_call_target="tpu_custom_call" | custom-call | tf_op jit(solution)/shard_map/cycle/pallas_call | solution.py:229
  211.1 3.4 %collective-permute-start.43 = (bf16[128,512]{1,0:T(8,128)(2,1)}, bf16[128,512]{1,0:T(8,128)(2,1)S(1)}, u32[]{:S(2)}, u32[]{:S(2)}) collective-permute-start(bf16[128,512]{1,0:T(8,128)(2,1)} %get-tuple-element.32), channel_id=1, source_target_pairs={{0,12},{4,0},{8,4},{12,8},{1,13},{5,1},{9,5},{13,9},{2,14},{6,2},{... | collective-permute-start | bytes 393224 | tf_op jit(solution)/shard_map/ppermute | solution.py:20
  214.8 1.3 collective-permute-start.45
  216.3 3.4 %collective-permute-done.43 = bf16[128,512]{1,0:T(8,128)(2,1)S(1)} collective-permute-done((bf16[128,512]{1,0:T(8,128)(2,1)}, bf16[128,512]{1,0:T(8,128)(2,1)S(1)}, u32[]{:S(2)}, u32[]{:S(2)}) %collective-permute-start.43) | collective-permute-done | bytes 131104 | tf_op jit(solution)/shard_map/ppermute | solution.py:20
  219.7 2.2 collective-permute-done.44
  222.0 1.3 collective-permute-done.45
  223.3 1.8 add_divide_fusion
  (116 shorter events, 4.0 us)
Async XLA Ops:
  0.0 14.6 %copy-start.4 = (bf16[2,32,32,256]{3,2,1,0:T(8,128)(2,1)S(1)}, bf16[2,32,32,256]{3,2,1,0:T(8,128)(2,1)}, u32[]{:S(2)}) copy-start(bf16[2,32,32,256]{3,2,1,0:T(8,128)(2,1)} %param.7) | copy-start | bytes 3145732
  2.1 20.6 %all-to-all-start = ((bf16[32,16,4,128]{3,2,1,0:T(4,128)(2,1)}), bf16[32,16,4,128]{3,2,1,0:T(4,128)(2,1)S(1)}, u32[]{:S(2)}, u32[]{:S(2)}) async-start(bf16[32,16,4,128]{3,2,1,0:T(4,128)(2,1)} %bitcast.19), calls=%async_computation | async-start | bytes 1048576 | tf_op jit(solution)/shard_map/all_to_all | solution.py:257
  11.3 14.9 %collective-permute-start.1 = (bf16[256,512]{1,0:T(8,128)(2,1)}, bf16[256,512]{1,0:T(8,128)(2,1)}, u32[]{:S(2)}, u32[]{:S(2)}) collective-permute-start(bf16[256,512]{1,0:T(8,128)(2,1)} %bitcast.12), channel_id=1, source_target_pairs={{0,8},{4,12},{8,0},{12,4},{1,9},{5,13},{9,1},{13,5},{2,10},{6,14},... | collective-permute-start | bytes 786440 | tf_op jit(solution)/shard_map/ppermute | solution.py:20
  15.2 11.6 %copy-start.11 = (bf16[16,32,512]{2,1,0:T(8,128)(2,1)S(1)}, bf16[16,32,512]{2,1,0:T(8,128)(2,1)}, u32[]{:S(2)}) copy-start(bf16[16,32,512]{2,1,0:T(8,128)(2,1)} %param.8) | copy-start | bytes 1572868
  16.4 22.5 %collective-permute-start.3 = (bf16[32,64,128]{2,1,0:T(8,128)(2,1)}, bf16[32,64,128]{2,1,0:T(8,128)(2,1)S(1)}, u32[]{:S(2)}, u32[]{:S(2)}) collective-permute-start(bf16[32,64,128]{2,1,0:T(8,128)(2,1)} %get-tuple-element.36), channel_id=1, source_target_pairs={{0,0},{1,1},{2,16},{3,17},{16,2},{17,3},{18,18},{19,19},{4,4},{5,5... | collective-permute-start | bytes 1572872 | tf_op jit(solution)/shard_map/ppermute | solution.py:264
  18.1 20.9 %collective-permute-start.4 = (bf16[32,64,128]{2,1,0:T(8,128)(2,1)}, bf16[32,64,128]{2,1,0:T(8,128)(2,1)}, u32[]{:S(2)}, u32[]{:S(2)}) collective-permute-start(bf16[32,64,128]{2,1,0:T(8,128)(2,1)} %get-tuple-element.35), channel_id=1, source_target_pairs={{0,1},{1,0},{2,17},{3,16},{16,3},{17,2},{18,19},{19,18},{4,5},{5,4... | collective-permute-start | bytes 1572872 | tf_op jit(solution)/shard_map/ppermute | solution.py:264
  22.9 19.2 %copy-start.12 = (bf16[16,32,4,128]{3,2,1,0:T(4,128)(2,1)}, bf16[16,32,4,128]{3,2,1,0:T(4,128)(2,1)S(1)}, u32[]{:S(2)}) copy-start(bf16[16,32,4,128]{3,2,1,0:T(4,128)(2,1)S(1)} %copy.22) | copy-start | bytes 1572868
  23.0 21.4 %collective-permute-start.23 = (bf16[16,128,128]{2,1,0:T(8,128)(2,1)S(1)}, bf16[16,128,128]{2,1,0:T(8,128)(2,1)}, u32[]{:S(2)}, u32[]{:S(2)}) collective-permute-start(bf16[16,128,128]{2,1,0:T(8,128)(2,1)S(1)} %bitcast.45), channel_id=1, source_target_pairs={{0,32},{32,64},{64,96},{96,0},{1,33},{33,65},{65,97},{97,1},{2,34}... | collective-permute-start | bytes 1572872 | tf_op jit(solution)/shard_map/ppermute | solution.py:20
  24.6 7.3 %collective-permute-start.2 = (bf16[256,512]{1,0:T(8,128)(2,1)S(1)}, bf16[256,512]{1,0:T(8,128)(2,1)S(1)}, u32[]{:S(2)}, u32[]{:S(2)}) collective-permute-start(bf16[256,512]{1,0:T(8,128)(2,1)S(1)} %bitcast.52), channel_id=1, source_target_pairs={{0,12},{4,0},{8,4},{12,8},{1,13},{5,1},{9,5},{13,9},{2,14},{6,2},{... | collective-permute-start | bytes 786440 | tf_op jit(solution)/shard_map/ppermute | solution.py:20
  26.1 9.0 %collective-permute-start = (bf16[256,512]{1,0:T(8,128)(2,1)S(1)}, bf16[256,512]{1,0:T(8,128)(2,1)S(1)}, u32[]{:S(2)}, u32[]{:S(2)}) collective-permute-start(bf16[256,512]{1,0:T(8,128)(2,1)S(1)} %bitcast.51), channel_id=1, source_target_pairs={{0,4},{4,8},{8,12},{12,0},{1,5},{5,9},{9,13},{13,1},{2,6},{6,10},{... | collective-permute-start | bytes 786440 | tf_op jit(solution)/shard_map/ppermute | solution.py:20
  32.9 130.6 %copy-start.1 = (bf16[512,512]{1,0:T(8,128)(2,1)}, bf16[512,512]{1,0:T(8,128)(2,1)S(1)}, u32[]{:S(2)}) copy-start(bf16[512,512]{1,0:T(8,128)(2,1)S(1)} %pad_maximum_fusion.1.refs_6_) | copy-start | bytes 1572868
  35.2 96.5 %copy-start.2 = (bf16[512,512]{1,0:T(8,128)(2,1)}, bf16[512,512]{1,0:T(8,128)(2,1)S(1)}, u32[]{:S(2)}) copy-start(bf16[512,512]{1,0:T(8,128)(2,1)S(1)} %pad_maximum_fusion.refs_4_) | copy-start | bytes 1572868
  35.2 24.4 %collective-permute-start.24 = (bf16[16,128,128]{2,1,0:T(8,128)(2,1)S(1)}, bf16[16,128,128]{2,1,0:T(8,128)(2,1)S(1)}, u32[]{:S(2)}, u32[]{:S(2)}) collective-permute-start(bf16[16,128,128]{2,1,0:T(8,128)(2,1)S(1)} %bitcast.46), channel_id=1, source_target_pairs={{0,96},{32,0},{64,32},{96,64},{1,97},{33,1},{65,33},{97,65},{2,98}... | collective-permute-start | bytes 1572872 | tf_op jit(solution)/shard_map/ppermute | solution.py:20
  38.3 22.1 %collective-permute-start.25 = (bf16[16,128,128]{2,1,0:T(8,128)(2,1)S(1)}, bf16[16,128,128]{2,1,0:T(8,128)(2,1)}, u32[]{:S(2)}, u32[]{:S(2)}) collective-permute-start(bf16[16,128,128]{2,1,0:T(8,128)(2,1)S(1)} %bitcast.47), channel_id=1, source_target_pairs={{0,64},{32,96},{64,0},{96,32},{1,65},{33,97},{65,1},{97,33},{2,66}... | collective-permute-start | bytes 1572872 | tf_op jit(solution)/shard_map/ppermute | solution.py:20
  42.1 19.5 %collective-permute-start.19 = (bf16[32,16,512]{2,1,0:T(8,128)(2,1)S(1)}, bf16[32,16,512]{2,1,0:T(8,128)(2,1)S(1)}, u32[]{:S(2)}, u32[]{:S(2)}) collective-permute-start(bf16[32,16,512]{2,1,0:T(8,128)(2,1)S(1)} %bitcast.49), channel_id=1, source_target_pairs={{0,0},{1,1},{2,16},{3,17},{16,2},{17,3},{18,18},{19,19},{4,4},{5,5... | collective-permute-start | bytes 1572872 | tf_op jit(solution)/shard_map/ppermute | solution.py:290
  42.8 20.7 %collective-permute-start.20 = (bf16[32,16,512]{2,1,0:T(8,128)(2,1)S(1)}, bf16[32,16,512]{2,1,0:T(8,128)(2,1)S(1)}, u32[]{:S(2)}, u32[]{:S(2)}) collective-permute-start(bf16[32,16,512]{2,1,0:T(8,128)(2,1)S(1)} %bitcast.50), channel_id=1, source_target_pairs={{0,1},{1,0},{2,17},{3,16},{16,3},{17,2},{18,19},{19,18},{4,5},{5,4... | collective-permute-start | bytes 1572872 | tf_op jit(solution)/shard_map/ppermute | solution.py:290
  44.4 19.2 %collective-permute-start.7 = (bf16[2048,128]{1,0:T(8,128)(2,1)}, bf16[2048,128]{1,0:T(8,128)(2,1)S(1)}, u32[]{:S(2)}, u32[]{:S(2)}) collective-permute-start(bf16[2048,128]{1,0:T(8,128)(2,1)} %get-tuple-element.24.refs_0_), channel_id=1, source_target_pairs={{0,4},{4,8},{8,12},{12,0},{1,5},{5,9},{9,13},{13,1},{2,6},{6,10},{... | collective-permute-start | bytes 1572872 | tf_op jit(solution)/shard_map/ppermute | solution.py:20
  59.6 31.4 %copy-start.19 = (bf16[16,128,128]{2,1,0:T(8,128)(2,1)}, bf16[16,128,128]{2,1,0:T(8,128)(2,1)S(1)}, u32[]{:S(2)}) copy-start(bf16[16,128,128]{2,1,0:T(8,128)(2,1)S(1)} %collective-permute-done.24.refs_6_) | copy-start | bytes 1572868
  59.6 11.7 %collective-permute-start.13 = (bf16[2048,128]{1,0:T(8,128)(2,1)}, bf16[2048,128]{1,0:T(8,128)(2,1)}, u32[]{:S(2)}, u32[]{:S(2)}) collective-permute-start(bf16[2048,128]{1,0:T(8,128)(2,1)} %get-tuple-element.25.refs_2_), channel_id=1, source_target_pairs={{0,12},{4,0},{8,4},{12,8},{1,13},{5,1},{9,5},{13,9},{2,14},{6,2},{... | collective-permute-start | bytes 1572872 | tf_op jit(solution)/shard_map/ppermute | solution.py:20
  60.3 11.5 %collective-permute-start.9 = (bf16[2048,128]{1,0:T(8,128)(2,1)}, bf16[2048,128]{1,0:T(8,128)(2,1)S(1)}, u32[]{:S(2)}, u32[]{:S(2)}) collective-permute-start(bf16[2048,128]{1,0:T(8,128)(2,1)} %get-tuple-element.25.refs_2_), channel_id=1, source_target_pairs={{0,4},{4,8},{8,12},{12,0},{1,5},{5,9},{9,13},{13,1},{2,6},{6,10},{... | collective-permute-start | bytes 1572872 | tf_op jit(solution)/shard_map/ppermute | solution.py:20
  61.6 27.3 %copy-start.21 = (bf16[32,16,512]{2,1,0:T(8,128)(2,1)}, bf16[32,16,512]{2,1,0:T(8,128)(2,1)S(1)}, u32[]{:S(2)}) copy-start(bf16[32,16,512]{2,1,0:T(8,128)(2,1)S(1)} %collective-permute-done.19.refs_0_) | copy-start | bytes 1572868
  61.6 16.8 %collective-permute-start.11 = (bf16[2048,128]{1,0:T(8,128)(2,1)}, bf16[2048,128]{1,0:T(8,128)(2,1)}, u32[]{:S(2)}, u32[]{:S(2)}) collective-permute-start(bf16[2048,128]{1,0:T(8,128)(2,1)} %get-tuple-element.24.refs_0_), channel_id=1, source_target_pairs={{0,12},{4,0},{8,4},{12,8},{1,13},{5,1},{9,5},{13,9},{2,14},{6,2},{... | collective-permute-start | bytes 1572872 | tf_op jit(solution)/shard_map/ppermute | solution.py:20
  63.6 25.8 %copy-start.23 = (bf16[32,16,512]{2,1,0:T(8,128)(2,1)}, bf16[32,16,512]{2,1,0:T(8,128)(2,1)S(1)}, u32[]{:S(2)}) copy-start(bf16[32,16,512]{2,1,0:T(8,128)(2,1)S(1)} %collective-permute-done.20.refs_1_) | copy-start | bytes 1572868
  63.6 14.8 %collective-permute-start.5 = (bf16[2048,128]{1,0:T(8,128)(2,1)}, bf16[2048,128]{1,0:T(8,128)(2,1)S(1)}, u32[]{:S(2)}, u32[]{:S(2)}) collective-permute-start(bf16[2048,128]{1,0:T(8,128)(2,1)} %get-tuple-element.24.refs_0_), channel_id=1, source_target_pairs={{0,16},{16,0},{1,17},{17,1},{2,18},{18,2},{3,19},{19,3},{4,20},{20... | collective-permute-start | bytes 1572872 | tf_op jit(solution)/shard_map/ppermute | solution.py:24
  63.6 38.0 %copy-start.20 = (bf16[2048,128]{1,0:T(8,128)(2,1)}, bf16[2048,128]{1,0:T(8,128)(2,1)S(1)}, u32[]{:S(2)}) copy-start(bf16[2048,128]{1,0:T(8,128)(2,1)S(1)} %collective-permute-done.7.refs_4_) | copy-start | bytes 1572868
  63.6 18.0 %collective-permute-start.6 = (bf16[2048,128]{1,0:T(8,128)(2,1)}, bf16[2048,128]{1,0:T(8,128)(2,1)S(1)}, u32[]{:S(2)}, u32[]{:S(2)}) collective-permute-start(bf16[2048,128]{1,0:T(8,128)(2,1)} %get-tuple-element.25.refs_2_), channel_id=1, source_target_pairs={{0,16},{16,0},{1,17},{17,1},{2,18},{18,2},{3,19},{19,3},{4,20},{20... | collective-permute-start | bytes 1572872 | tf_op jit(solution)/shard_map/ppermute | solution.py:24
  71.3 10.4 %collective-permute-start.21 = (bf16[32,16,512]{2,1,0:T(8,128)(2,1)S(1)}, bf16[32,16,512]{2,1,0:T(8,128)(2,1)S(1)}, u32[]{:S(2)}, u32[]{:S(2)}) collective-permute-start(bf16[32,16,512]{2,1,0:T(8,128)(2,1)S(1)} %collective-permute-done.19.refs_0_), channel_id=1, source_target_pairs={{0,16},{16,0},{1,17},{17,1},{2,18},{18,2},{3,19},{19,3},{4,20},{20... | collective-permute-start | bytes 1572872 | tf_op jit(solution)/shard_map/ppermute | solution.py:24
  71.9 29.8 %copy-start.22 = (bf16[2048,128]{1,0:T(8,128)(2,1)}, bf16[2048,128]{1,0:T(8,128)(2,1)S(1)}, u32[]{:S(2)}) copy-start(bf16[2048,128]{1,0:T(8,128)(2,1)S(1)} %collective-permute-done.9.refs_6_) | copy-start | bytes 1572868
  71.9 10.3 %collective-permute-start.22 = (bf16[32,16,512]{2,1,0:T(8,128)(2,1)S(1)}, bf16[32,16,512]{2,1,0:T(8,128)(2,1)S(1)}, u32[]{:S(2)}, u32[]{:S(2)}) collective-permute-start(bf16[32,16,512]{2,1,0:T(8,128)(2,1)S(1)} %collective-permute-done.20.refs_1_), channel_id=1, source_target_pairs={{0,16},{16,0},{1,17},{17,1},{2,18},{18,2},{3,19},{19,3},{4,20},{20... | collective-permute-start | bytes 1572872 | tf_op jit(solution)/shard_map/ppermute | solution.py:24
  78.4 10.5 %collective-permute-start.15 = (bf16[2048,128]{1,0:T(8,128)(2,1)S(1)}, bf16[2048,128]{1,0:T(8,128)(2,1)}, u32[]{:S(2)}, u32[]{:S(2)}) collective-permute-start(bf16[2048,128]{1,0:T(8,128)(2,1)S(1)} %collective-permute-done.7.refs_4_), channel_id=1, source_target_pairs={{0,4},{4,8},{8,12},{12,0},{1,5},{5,9},{9,13},{13,1},{2,6},{6,10},{... | collective-permute-start | bytes 1572872 | tf_op jit(solution)/shard_map/ppermute | solution.py:20
  78.4 23.3 %copy-start.24 = (bf16[2048,128]{1,0:T(8,128)(2,1)}, bf16[2048,128]{1,0:T(8,128)(2,1)S(1)}, u32[]{:S(2)}) copy-start(bf16[2048,128]{1,0:T(8,128)(2,1)S(1)} %collective-permute-done.5.refs_1_) | copy-start | bytes 1572868
  78.4 10.5 %collective-permute-start.17 = (bf16[2048,128]{1,0:T(8,128)(2,1)}, bf16[2048,128]{1,0:T(8,128)(2,1)}, u32[]{:S(2)}, u32[]{:S(2)}) collective-permute-start(bf16[2048,128]{1,0:T(8,128)(2,1)} %collective-permute-done.13.refs_10_), channel_id=1, source_target_pairs={{0,12},{4,0},{8,4},{12,8},{1,13},{5,1},{9,5},{13,9},{2,14},{6,2},{... | collective-permute-start | bytes 1572872 | tf_op jit(solution)/shard_map/ppermute | solution.py:20
  81.6 7.8 %collective-permute-start.10 = (bf16[2048,128]{1,0:T(8,128)(2,1)S(1)}, bf16[2048,128]{1,0:T(8,128)(2,1)S(1)}, u32[]{:S(2)}, u32[]{:S(2)}) collective-permute-start(bf16[2048,128]{1,0:T(8,128)(2,1)S(1)} %collective-permute-done.9.refs_6_), channel_id=1, source_target_pairs={{0,16},{16,0},{1,17},{17,1},{2,18},{18,2},{3,19},{19,3},{4,20},{20... | collective-permute-start | bytes 1572872 | tf_op jit(solution)/shard_map/ppermute | solution.py:24
  81.7 20.0 %collective-permute-start.14 = (bf16[2048,128]{1,0:T(8,128)(2,1)}, bf16[2048,128]{1,0:T(8,128)(2,1)}, u32[]{:S(2)}, u32[]{:S(2)}) collective-permute-start(bf16[2048,128]{1,0:T(8,128)(2,1)} %collective-permute-done.13.refs_10_), channel_id=1, source_target_pairs={{0,16},{16,0},{1,17},{17,1},{2,18},{18,2},{3,19},{19,3},{4,20},{20... | collective-permute-start | bytes 1572872 | tf_op jit(solution)/shard_map/ppermute | solution.py:24
  82.1 19.5 %collective-permute-start.8 = (bf16[2048,128]{1,0:T(8,128)(2,1)S(1)}, bf16[2048,128]{1,0:T(8,128)(2,1)}, u32[]{:S(2)}, u32[]{:S(2)}) collective-permute-start(bf16[2048,128]{1,0:T(8,128)(2,1)S(1)} %collective-permute-done.7.refs_4_), channel_id=1, source_target_pairs={{0,16},{16,0},{1,17},{17,1},{2,18},{18,2},{3,19},{19,3},{4,20},{20... | collective-permute-start | bytes 1572872 | tf_op jit(solution)/shard_map/ppermute | solution.py:24
  88.9 12.8 %collective-permute-start.12 = (bf16[2048,128]{1,0:T(8,128)(2,1)}, bf16[2048,128]{1,0:T(8,128)(2,1)}, u32[]{:S(2)}, u32[]{:S(2)}) collective-permute-start(bf16[2048,128]{1,0:T(8,128)(2,1)} %collective-permute-done.11.refs_8_), channel_id=1, source_target_pairs={{0,16},{16,0},{1,17},{17,1},{2,18},{18,2},{3,19},{19,3},{4,20},{20... | collective-permute-start | bytes 1572872 | tf_op jit(solution)/shard_map/ppermute | solution.py:24
  88.9 12.8 %collective-permute-start.16 = (bf16[2048,128]{1,0:T(8,128)(2,1)}, bf16[2048,128]{1,0:T(8,128)(2,1)}, u32[]{:S(2)}, u32[]{:S(2)}) collective-permute-start(bf16[2048,128]{1,0:T(8,128)(2,1)} %collective-permute-done.15.refs_12_), channel_id=1, source_target_pairs={{0,16},{16,0},{1,17},{17,1},{2,18},{18,2},{3,19},{19,3},{4,20},{20... | collective-permute-start | bytes 1572872 | tf_op jit(solution)/shard_map/ppermute | solution.py:24
  90.2 11.5 %collective-permute-start.18 = (bf16[2048,128]{1,0:T(8,128)(2,1)}, bf16[2048,128]{1,0:T(8,128)(2,1)}, u32[]{:S(2)}, u32[]{:S(2)}) collective-permute-start(bf16[2048,128]{1,0:T(8,128)(2,1)} %collective-permute-done.17.refs_14_), channel_id=1, source_target_pairs={{0,16},{16,0},{1,17},{17,1},{2,18},{18,2},{3,19},{19,3},{4,20},{20... | collective-permute-start | bytes 1572872 | tf_op jit(solution)/shard_map/ppermute | solution.py:24
  117.9 71.5 %copy-start.29 = (f32[256]{0:T(256)S(1)}, f32[256]{0:T(256)}, u32[]{:S(2)}) copy-start(f32[256]{0:T(256)} %param.13) | copy-start | bytes 3076
  117.9 71.5 %all-to-all-start.1 = ((bf16[32,256,128]{2,1,0:T(8,128)(2,1)}), bf16[32,256,128]{2,1,0:T(8,128)(2,1)S(1)}, u32[]{:S(2)}, u32[]{:S(2)}) async-start(bf16[32,256,128]{2,1,0:T(8,128)(2,1)} %bitcast.41), calls=%async_computation.1 | async-start | bytes 4194304 | tf_op jit(solution)/shard_map/all_to_all | solution.py:309
  125.1 74.7 %copy-start.17 = (f32[32]{0:T(128)S(1)}, f32[32]{0:T(128)}, u32[]{:S(2)}) copy-start(f32[32]{0:T(128)} %param.11) | copy-start | bytes 388
  125.1 38.4 %collective-permute-start.31 = (bf16[512,512]{1,0:T(8,128)(2,1)S(1)}, bf16[512,512]{1,0:T(8,128)(2,1)S(1)}, u32[]{:S(2)}, u32[]{:S(2)}) collective-permute-start(bf16[512,512]{1,0:T(8,128)(2,1)S(1)} %pad_maximum_fusion.refs_4_), channel_id=1, source_target_pairs={{0,32},{32,64},{64,96},{96,0},{1,33},{33,65},{65,97},{97,1},{2,34}... | collective-permute-start | bytes 1572872 | tf_op jit(solution)/shard_map/ppermute | solution.py:20
  127.0 37.5 %collective-permute-start.37 = (bf16[512,512]{1,0:T(8,128)(2,1)S(1)}, bf16[512,512]{1,0:T(8,128)(2,1)}, u32[]{:S(2)}, u32[]{:S(2)}) collective-permute-start(bf16[512,512]{1,0:T(8,128)(2,1)S(1)} %pad_maximum_fusion.1.refs_6_), channel_id=1, source_target_pairs={{0,96},{32,0},{64,32},{96,64},{1,97},{33,1},{65,33},{97,65},{2,98}... | collective-permute-start | bytes 1572872 | tf_op jit(solution)/shard_map/ppermute | solution.py:20
  128.4 46.4 %collective-permute-start.33 = (bf16[512,512]{1,0:T(8,128)(2,1)S(1)}, bf16[512,512]{1,0:T(8,128)(2,1)}, u32[]{:S(2)}, u32[]{:S(2)}) collective-permute-start(bf16[512,512]{1,0:T(8,128)(2,1)S(1)} %pad_maximum_fusion.1.refs_6_), channel_id=1, source_target_pairs={{0,32},{32,64},{64,96},{96,0},{1,33},{33,65},{65,97},{97,1},{2,34}... | collective-permute-start | bytes 1572872 | tf_op jit(solution)/shard_map/ppermute | solution.py:20
  129.0 46.9 %collective-permute-start.35 = (bf16[512,512]{1,0:T(8,128)(2,1)S(1)}, bf16[512,512]{1,0:T(8,128)(2,1)}, u32[]{:S(2)}, u32[]{:S(2)}) collective-permute-start(bf16[512,512]{1,0:T(8,128)(2,1)S(1)} %pad_maximum_fusion.refs_4_), channel_id=1, source_target_pairs={{0,96},{32,0},{64,32},{96,64},{1,97},{33,1},{65,33},{97,65},{2,98}... | collective-permute-start | bytes 1572872 | tf_op jit(solution)/shard_map/ppermute | solution.py:20
  131.7 44.3 %collective-permute-start.29 = (bf16[512,512]{1,0:T(8,128)(2,1)S(1)}, bf16[512,512]{1,0:T(8,128)(2,1)S(1)}, u32[]{:S(2)}, u32[]{:S(2)}) collective-permute-start(bf16[512,512]{1,0:T(8,128)(2,1)S(1)} %pad_maximum_fusion.refs_4_), channel_id=1, source_target_pairs={{0,16},{16,0},{1,17},{17,1},{2,18},{18,2},{3,19},{19,3},{4,20},{20... | collective-permute-start | bytes 1572872 | tf_op jit(solution)/shard_map/ppermute | solution.py:24
  163.5 13.0 %copy-start.5 = (bf16[512,512]{1,0:T(8,128)(2,1)}, bf16[512,512]{1,0:T(8,128)(2,1)S(1)}, u32[]{:S(2)}) copy-start(bf16[512,512]{1,0:T(8,128)(2,1)S(1)} %collective-permute-done.31.refs_8_) | copy-start | bytes 1572868
  163.5 13.0 %collective-permute-start.30 = (bf16[512,512]{1,0:T(8,128)(2,1)S(1)}, bf16[512,512]{1,0:T(8,128)(2,1)S(1)}, u32[]{:S(2)}, u32[]{:S(2)}) collective-permute-start(bf16[512,512]{1,0:T(8,128)(2,1)S(1)} %pad_maximum_fusion.1.refs_6_), channel_id=1, source_target_pairs={{0,16},{16,0},{1,17},{17,1},{2,18},{18,2},{3,19},{19,3},{4,20},{20... | collective-permute-start | bytes 1572872 | tf_op jit(solution)/shard_map/ppermute | solution.py:24
  164.5 21.0 %collective-permute-start.39 = (bf16[512,512]{1,0:T(8,128)(2,1)S(1)}, bf16[512,512]{1,0:T(8,128)(2,1)}, u32[]{:S(2)}, u32[]{:S(2)}) collective-permute-start(bf16[512,512]{1,0:T(8,128)(2,1)S(1)} %collective-permute-done.31.refs_8_), channel_id=1, source_target_pairs={{0,32},{32,64},{64,96},{96,0},{1,33},{33,65},{65,97},{97,1},{2,34}... | collective-permute-start | bytes 1572872 | tf_op jit(solution)/shard_map/ppermute | solution.py:20
  174.8 13.2 %collective-permute-start.41 = (bf16[512,512]{1,0:T(8,128)(2,1)}, bf16[512,512]{1,0:T(8,128)(2,1)}, u32[]{:S(2)}, u32[]{:S(2)}) collective-permute-start(bf16[512,512]{1,0:T(8,128)(2,1)} %collective-permute-done.37.refs_14_), channel_id=1, source_target_pairs={{0,96},{32,0},{64,32},{96,64},{1,97},{33,1},{65,33},{97,65},{2,98}... | collective-permute-start | bytes 1572872 | tf_op jit(solution)/shard_map/ppermute | solution.py:20
  176.0 12.1 %collective-permute-start.32 = (bf16[512,512]{1,0:T(8,128)(2,1)S(1)}, bf16[512,512]{1,0:T(8,128)(2,1)S(1)}, u32[]{:S(2)}, u32[]{:S(2)}) collective-permute-start(bf16[512,512]{1,0:T(8,128)(2,1)S(1)} %collective-permute-done.31.refs_8_), channel_id=1, source_target_pairs={{0,16},{16,0},{1,17},{17,1},{2,18},{18,2},{3,19},{19,3},{4,20},{20... | collective-permute-start | bytes 1572872 | tf_op jit(solution)/shard_map/ppermute | solution.py:24
  176.0 12.0 %copy-start.6 = (bf16[512,512]{1,0:T(8,128)(2,1)}, bf16[512,512]{1,0:T(8,128)(2,1)S(1)}, u32[]{:S(2)}) copy-start(bf16[512,512]{1,0:T(8,128)(2,1)S(1)} %collective-permute-done.29.refs_5_) | copy-start | bytes 1572868
  176.0 18.0 %collective-permute-start.34 = (bf16[512,512]{1,0:T(8,128)(2,1)}, bf16[512,512]{1,0:T(8,128)(2,1)S(1)}, u32[]{:S(2)}, u32[]{:S(2)}) collective-permute-start(bf16[512,512]{1,0:T(8,128)(2,1)} %collective-permute-done.33.refs_10_), channel_id=1, source_target_pairs={{0,16},{16,0},{1,17},{17,1},{2,18},{18,2},{3,19},{19,3},{4,20},{20... | collective-permute-start | bytes 1572872 | tf_op jit(solution)/shard_map/ppermute | solution.py:24
  176.5 11.5 %copy-start.7 = (bf16[512,512]{1,0:T(8,128)(2,1)}, bf16[512,512]{1,0:T(8,128)(2,1)S(1)}, u32[]{:S(2)}) copy-start(bf16[512,512]{1,0:T(8,128)(2,1)S(1)} %collective-permute-done.30.refs_7_) | copy-start | bytes 1572868
  176.5 19.3 %collective-permute-start.36 = (bf16[512,512]{1,0:T(8,128)(2,1)}, bf16[512,512]{1,0:T(8,128)(2,1)S(1)}, u32[]{:S(2)}, u32[]{:S(2)}) collective-permute-start(bf16[512,512]{1,0:T(8,128)(2,1)} %collective-permute-done.35.refs_12_), channel_id=1, source_target_pairs={{0,16},{16,0},{1,17},{17,1},{2,18},{18,2},{3,19},{19,3},{4,20},{20... | collective-permute-start | bytes 1572872 | tf_op jit(solution)/shard_map/ppermute | solution.py:24
  185.5 12.8 %collective-permute-start.38 = (bf16[512,512]{1,0:T(8,128)(2,1)}, bf16[512,512]{1,0:T(8,128)(2,1)}, u32[]{:S(2)}, u32[]{:S(2)}) collective-permute-start(bf16[512,512]{1,0:T(8,128)(2,1)} %collective-permute-done.37.refs_14_), channel_id=1, source_target_pairs={{0,16},{16,0},{1,17},{17,1},{2,18},{18,2},{3,19},{19,3},{4,20},{20... | collective-permute-start | bytes 1572872 | tf_op jit(solution)/shard_map/ppermute | solution.py:24
  188.0 12.7 %collective-permute-start.40 = (bf16[512,512]{1,0:T(8,128)(2,1)}, bf16[512,512]{1,0:T(8,128)(2,1)}, u32[]{:S(2)}, u32[]{:S(2)}) collective-permute-start(bf16[512,512]{1,0:T(8,128)(2,1)} %collective-permute-done.39.refs_16_), channel_id=1, source_target_pairs={{0,16},{16,0},{1,17},{17,1},{2,18},{18,2},{3,19},{19,3},{4,20},{20... | collective-permute-start | bytes 1572872 | tf_op jit(solution)/shard_map/ppermute | solution.py:24
  188.8 11.9 %collective-permute-start.42 = (bf16[512,512]{1,0:T(8,128)(2,1)}, bf16[512,512]{1,0:T(8,128)(2,1)}, u32[]{:S(2)}, u32[]{:S(2)}) collective-permute-start(bf16[512,512]{1,0:T(8,128)(2,1)} %collective-permute-done.41.refs_18_), channel_id=1, source_target_pairs={{0,16},{16,0},{1,17},{17,1},{2,18},{18,2},{3,19},{19,3},{4,20},{20... | collective-permute-start | bytes 1572872 | tf_op jit(solution)/shard_map/ppermute | solution.py:24
  194.0 6.8 %collective-permute-start.26 = (bf16[32,16,128]{2,1,0:T(8,128)(2,1)}, bf16[32,16,128]{2,1,0:T(8,128)(2,1)S(1)}, u32[]{:S(2)}, u32[]{:S(2)}) collective-permute-start(bf16[32,16,128]{2,1,0:T(8,128)(2,1)} %bitcast.54), channel_id=1, source_target_pairs={{0,1},{1,2},{2,3},{3,0},{4,5},{5,6},{6,7},{7,4},{8,9},{9,10},{10,1... | collective-permute-start | bytes 393224 | tf_op jit(solution)/shard_map/ppermute | solution.py:20
  195.8 8.9 %collective-permute-start.27 = (bf16[32,16,128]{2,1,0:T(8,128)(2,1)}, bf16[32,16,128]{2,1,0:T(8,128)(2,1)S(1)}, u32[]{:S(2)}, u32[]{:S(2)}) collective-permute-start(bf16[32,16,128]{2,1,0:T(8,128)(2,1)} %bitcast.55), channel_id=1, source_target_pairs={{0,2},{1,3},{2,0},{3,1},{4,6},{5,7},{6,4},{7,5},{8,10},{9,11},{10,... | collective-permute-start | bytes 393224 | tf_op jit(solution)/shard_map/ppermute | solution.py:20
  198.3 6.4 %collective-permute-start.28 = (bf16[32,16,128]{2,1,0:T(8,128)(2,1)}, bf16[32,16,128]{2,1,0:T(8,128)(2,1)S(1)}, u32[]{:S(2)}, u32[]{:S(2)}) collective-permute-start(bf16[32,16,128]{2,1,0:T(8,128)(2,1)} %bitcast.56), channel_id=1, source_target_pairs={{0,3},{1,0},{2,1},{3,2},{4,7},{5,4},{6,5},{7,6},{8,11},{9,8},{10,9... | collective-permute-start | bytes 393224 | tf_op jit(solution)/shard_map/ppermute | solution.py:20
  211.1 8.6 %collective-permute-start.43 = (bf16[128,512]{1,0:T(8,128)(2,1)}, bf16[128,512]{1,0:T(8,128)(2,1)S(1)}, u32[]{:S(2)}, u32[]{:S(2)}) collective-permute-start(bf16[128,512]{1,0:T(8,128)(2,1)} %get-tuple-element.32), channel_id=1, source_target_pairs={{0,12},{4,0},{8,4},{12,8},{1,13},{5,1},{9,5},{13,9},{2,14},{6,2},{... | collective-permute-start | bytes 393224 | tf_op jit(solution)/shard_map/ppermute | solution.py:20
  214.5 7.4 %collective-permute-start.44 = (bf16[128,512]{1,0:T(8,128)(2,1)}, bf16[128,512]{1,0:T(8,128)(2,1)S(1)}, u32[]{:S(2)}, u32[]{:S(2)}) collective-permute-start(bf16[128,512]{1,0:T(8,128)(2,1)} %get-tuple-element.33), channel_id=1, source_target_pairs={{0,8},{4,12},{8,0},{12,4},{1,9},{5,13},{9,1},{13,5},{2,10},{6,14},... | collective-permute-start | bytes 393224 | tf_op jit(solution)/shard_map/ppermute | solution.py:20
  214.8 8.5 %collective-permute-start.45 = (bf16[128,512]{1,0:T(8,128)(2,1)}, bf16[128,512]{1,0:T(8,128)(2,1)S(1)}, u32[]{:S(2)}, u32[]{:S(2)}) collective-permute-start(bf16[128,512]{1,0:T(8,128)(2,1)} %get-tuple-element.34), channel_id=1, source_target_pairs={{0,4},{4,8},{8,12},{12,0},{1,5},{5,9},{9,13},{13,1},{2,6},{6,10},{... | collective-permute-start | bytes 393224 | tf_op jit(solution)/shard_map/ppermute | solution.py:20
  (14 other events, 72.7 us)

commit v4 on v3

--- a/solution.py
+++ b/solution.py
@@ -103,20 +103,15 @@
             load(n).start()
 
     _, _, nz, na, nb, _ = out_ref.shape
-    for part in range(2):
-
-        @pl.when(g == 0)
-        def _():
-            for n in range(8 * part, 8 * part + 8):
-                load(n).wait()
-
+
+    def product(begin, count):
         got = jnp.dot(
             w_ref[...],
-            turned[:, 4 * part * wide : 4 * (part + 1) * wide],
+            turned[:, begin * wide : (begin + count) * wide],
             preferred_element_type=F32,
         ).astype(BF16)
-        for n in range(4):
-            y = where_ref[2 * part + n // 2]
+        for n in range(count):
+            y = where_ref[(begin + n) // 2]
             c = where_ref[4] ^ (n % 2)
             for s in range(nz):
                 for a in range(na):
@@ -125,11 +120,22 @@
                         row : row + nb, n * wide : (n + 1) * wide
                     ]
 
+    @pl.when(g == 0)
+    def _():
+        for part in range(2):
+            for n in range(8 * part, 8 * part + 8):
+                load(n).wait()
+            product(4 * part, 4)
+
+    @pl.when(g > 0)
+    def _():
+        product(0, 8)
+
 
 def partial_ladder(where, amps, w):
     wide = amps[0].shape[1]
     nrow, depth = w.shape
-    step, nz, nb = 512, 4, 16
+    step, nz, nb = 256, 4, 16
     na = step // (nz * nb)
     return pl.pallas_call(
         ladder_kernel,
@@ -257,7 +263,6 @@
     block = lax.all_to_all(
         block.reshape(32, na // 2, nq, nc // 2), ("core", "x", "z"), 0, 0, tiled=True
     )
-    block = block.transpose(1, 0, 2, 3).reshape(na // 2, 32 * nq, nc // 2)
 
     flat = amplitudes.reshape(ni * nj, nd, nc)
     own = [
@@ -284,6 +289,8 @@
     low, high = own
     left_low, right_high = ring(low, "x", 1), ring(high, "x", -1)
     left_high, right_low = ring(high, "x", 1), ring(low, "x", -1)
+    block, _ = lax.optimization_barrier((block, low))
+    block = block.transpose(1, 0, 2, 3).reshape(na // 2, 32 * nq, nc // 2)
     blocks = [block] + [ring(block, "y", k) for k in (1, 3, 2)]
     turned = pair_factor.transpose(1, 0, 2)
     turned, *own = lax.optimization_barrier((turned, *own))

time: 226 us -> 235 us (1.040)
  waiting for transfers between devices: 113 us -> 120 us
  starting transfers between devices: 59.4 us -> 62.5 us
    ppermute x24, waiting for transfers between devices: 110 us -> 120 us  [ring(): return lax.ppermute(value, axis, [(i, (i + shift) % n) for i in range(n)])]
    all_to_all x1, waiting for transfers between devices: 3.19 us -> 0.01 us  [update(): lax.all_to_all(block.reshape(32, na // 2, nq, nc // 2), ('core', 'x', 'z'...]
    all_to_all x1, starting transfers between devices: 7.23 us -> 9.95 us  [update(): parts = lax.all_to_all(parts, ('y', 'core', 'z'), 0, 0, tiled=True)]
    unnamed x62 -> x74, local copies, waits for them, and re-layouts: 5.37 us -> 6.9 us
  transfers between devices with their start and end apart: 48 -> 48, of which waited for: 19 -> 19; matrix products, arithmetic and copies ran while one was open for 3% -> 2% of each run, Pallas kernels for 7% -> 7%
where the time goes in v4:
time: 235 us; the launch traced here: 234 us
  waiting for transfers between devices  120 us (51%)
  starting transfers between devices  62.5 us (27%)
  Pallas kernels  37.2 us (16%)
  local copies, waits for them, and re-layouts  10.4 us (4%)
  other arithmetic  3.59 us (2%)
    ppermute x24, waiting for transfers between devices, ring(): return lax.ppermute(value, axis, [(i, (i + shift) % n) for i in range(n)])  120 us
    ppermute x24, starting transfers between devices, ring(): return lax.ppermute(value, axis, [(i, (i + shift) % n) for i in range(n)])  35.9 us
    pallas_call x1, Pallas kernels, partial_ladder(): pl.pallas_call(ladder_kernel, grid_spec=pltpu.PrefetchScalarGridSpec(num_...  15.2 us
    pallas_call x1, Pallas kernels, form_integrals(): pl.pallas_call(integrals_kernel, grid_spec=pltpu.PrefetchScalarGridSpec(n...  10.6 us
    all_to_all x1, starting transfers between devices, update(): parts = lax.all_to_all(parts, ('y', 'core', 'z'), 0, 0, tiled=True)  9.95 us
    all_to_all x1, starting transfers between devices, update(): lax.all_to_all(block.reshape(32, na // 2, nq, nc // 2), ('core', 'x', 'z'...  7.83 us
    unnamed x74, local copies, waits for them, and re-layouts  6.9 us
    pallas_call x1, Pallas kernels, partial_cycle(): pl.pallas_call(cycle_kernel, in_specs=[pl.BlockSpec(memory_space=pltpu.SM...  5.68 us
  transfers between devices with their start and end apart: 48, of which 19 were waited for; matrix products, arithmetic and copies ran while one was open for 2% of the time, Pallas kernels for 7%

profile of v4, /device:TPU:0, one launch (start us, length us, event | category | flops | bytes accessed | tf_op | source)
XLA Modules:
  0.0 233.9 jit_solution(14948460468686546388)
XLA Ops:
  0.0 1.9 copy.20
  1.9 1.2 dynamic-slice_bitcast_fusion
  3.1 1.7 collective-permute-start.3
  4.8 2.0 collective-permute-start.4
  7.0 3.1 %collective-permute-start.1 = (bf16[256,512]{1,0:T(8,128)(2,1)S(1)}, bf16[256,512]{1,0:T(8,128)(2,1)}, u32[]{:S(2)}, u32[]{:S(2)}) collective-permute-start(bf16[256,512]{1,0:T(8,128)(2,1)S(1)} %bitcast.53), channel_id=1, source_target_pairs={{0,8},{4,12},{8,0},{12,4},{1,9},{5,13},{9,1},{13,5},{2,10},{6,14},... | collective-permute-start | bytes 786440 | tf_op jit(solution)/shard_map/ppermute | solution.py:20
  10.1 1.1 collective-permute-start.2
  11.3 1.0 broadcast_in_dim.2
  12.3 7.8 %all-to-all-start = ((bf16[32,16,4,128]{3,2,1,0:T(4,128)(2,1)}), bf16[32,16,4,128]{3,2,1,0:T(4,128)(2,1)S(1)}, u32[]{:S(2)}, u32[]{:S(2)}) async-start(bf16[32,16,4,128]{3,2,1,0:T(4,128)(2,1)} %bitcast.19), calls=%async_computation | async-start | bytes 1048576 | tf_op jit(solution)/shard_map/all_to_all | solution.py:263
  20.1 1.9 collective-permute-start
  22.3 1.1 pad_maximum_fusion.1.refs_6_
  23.4 12.1 %collective-permute-done = bf16[256,512]{1,0:T(8,128)(2,1)S(1)} collective-permute-done((bf16[256,512]{1,0:T(8,128)(2,1)S(1)}, bf16[256,512]{1,0:T(8,128)(2,1)S(1)}, u32[]{:S(2)}, u32[]{:S(2)}) %collective-permute-start) | collective-permute-done | bytes 262176 | tf_op jit(solution)/shard_map/ppermute | solution.py:20
  35.6 0.8 copy-done.12
  36.6 2.4 %turn.1 = (bf16[2048,128]{1,0:T(8,128)(2,1)}, bf16[2048,128]{1,0:T(8,128)(2,1)}) custom-call(s32[1]{0:T(128)} %bitcast.14.where_ref, bf16[32,64,128]{2,1,0:T(8,128)(2,1)} %copy-done.12, bf16[32,64,128]{2,1,0:T(8,128)(2,1)} %copy-done.13), custom_call_target="tpu_custom_call" | custom-call | tf_op jit(solution)/shard_map/turn/pallas_call | solution.py:80
  39.3 1.6 collective-permute-start.23
  41.2 1.7 collective-permute-start.24
  43.0 2.0 collective-permute-start.25
  45.0 0.7 collective-permute-start.19
  45.6 1.5 collective-permute-start.20
  47.2 7.1 %collective-permute-done.23.refs_5_ = bf16[16,128,128]{2,1,0:T(8,128)(2,1)S(1)} collective-permute-done((bf16[16,128,128]{2,1,0:T(8,128)(2,1)S(1)}, bf16[16,128,128]{2,1,0:T(8,128)(2,1)S(1)}, u32[]{:S(2)}, u32[]{:S(2)}) %collective-permute-start.23) | collective-permute-done | bytes 524320 | tf_op jit(solution)/shard_map/ppermute | solution.py:20
  54.3 10.9 %collective-permute-done.24.refs_6_ = bf16[16,128,128]{2,1,0:T(8,128)(2,1)S(1)} collective-permute-done((bf16[16,128,128]{2,1,0:T(8,128)(2,1)S(1)}, bf16[16,128,128]{2,1,0:T(8,128)(2,1)S(1)}, u32[]{:S(2)}, u32[]{:S(2)}) %collective-permute-start.24) | collective-permute-done | bytes 524320 | tf_op jit(solution)/shard_map/ppermute | solution.py:20
  65.1 0.7 collective-permute-start.13
  65.8 0.8 collective-permute-done.25.refs_7_
  66.6 0.5 collective-permute-start.9
  67.2 2.7 %collective-permute-start.11 = (bf16[2048,128]{1,0:T(8,128)(2,1)S(1)}, bf16[2048,128]{1,0:T(8,128)(2,1)}, u32[]{:S(2)}, u32[]{:S(2)}) collective-permute-start(bf16[2048,128]{1,0:T(8,128)(2,1)S(1)} %copy-done.20), channel_id=1, source_target_pairs={{0,12},{4,0},{8,4},{12,8},{1,13},{5,1},{9,5},{13,9},{2,14},{6,2},{... | collective-permute-start | bytes 1572872 | tf_op jit(solution)/shard_map/ppermute | solution.py:20
  69.9 0.5 collective-permute-start.6
  70.4 9.1 %collective-permute-done.13.refs_10_ = bf16[2048,128]{1,0:T(8,128)(2,1)} collective-permute-done((bf16[2048,128]{1,0:T(8,128)(2,1)S(1)}, bf16[2048,128]{1,0:T(8,128)(2,1)}, u32[]{:S(2)}, u32[]{:S(2)}) %collective-permute-start.13) | collective-permute-done | bytes 524320 | tf_op jit(solution)/shard_map/ppermute | solution.py:20
  79.5 1.0 collective-permute-done.9.refs_6_
  80.6 5.7 %collective-permute-done.11.refs_8_ = bf16[2048,128]{1,0:T(8,128)(2,1)} collective-permute-done((bf16[2048,128]{1,0:T(8,128)(2,1)S(1)}, bf16[2048,128]{1,0:T(8,128)(2,1)}, u32[]{:S(2)}, u32[]{:S(2)}) %collective-permute-start.11) | collective-permute-done | bytes 524320 | tf_op jit(solution)/shard_map/ppermute | solution.py:20
  86.3 3.2 %collective-permute-start.17 = (bf16[2048,128]{1,0:T(8,128)(2,1)}, bf16[2048,128]{1,0:T(8,128)(2,1)S(1)}, u32[]{:S(2)}, u32[]{:S(2)}) collective-permute-start(bf16[2048,128]{1,0:T(8,128)(2,1)} %collective-permute-done.13.refs_10_), channel_id=1, source_target_pairs={{0,12},{4,0},{8,4},{12,8},{1,13},{5,1},{9,5},{13,9},{2,14},{6,2},{... | collective-permute-start | bytes 1572872 | tf_op jit(solution)/shard_map/ppermute | solution.py:20
  90.1 6.6 %collective-permute-done.15.refs_12_ = bf16[2048,128]{1,0:T(8,128)(2,1)} collective-permute-done((bf16[2048,128]{1,0:T(8,128)(2,1)S(1)}, bf16[2048,128]{1,0:T(8,128)(2,1)}, u32[]{:S(2)}, u32[]{:S(2)}) %collective-permute-start.15) | collective-permute-done | bytes 524320 | tf_op jit(solution)/shard_map/ppermute | solution.py:20
  96.8 0.6 collective-permute-start.16
  97.4 0.8 copy-done.33
  98.2 0.6 stack.44.where_ref
  98.8 10.6 %integrals.1.refs_16_ = bf16[1024,4096]{1,0:T(8,128)(2,1)} custom-call(s32[1]{0:T(128)} %bitcast.where_ref, bf16[32,16,512]{2,1,0:T(8,128)(2,1)} %copy-done.26, bf16[32,16,512]{2,1,0:T(8,128)(2,1)} %copy-done.28, bf16[32,16,512]{2,1,0:T(8,128)(2,1)} %copy-done.32, bf16[32,16,512]{2,1,0:T(8,128)(2,1)} %copy-done.34, bf16[16,128,128]{2,1,0:T(8,128)(2,1)} %bitcast.48, ...), custom_call_target="tpu_custom_call" | custom-call | flops 4294967296 | bytes 12582912 | tf_op jit(solution)/shard_map/integrals/pallas_call | solution.py:50
  109.5 15.2 %ladder.1 = bf16[4,2,4,16,16,128]{5,4,3,2,1,0:T(8,128)(2,1)} custom-call(s32[6]{0:T(128)} %stack.44.where_ref, bf16[2048,128]{1,0:T(8,128)(2,1)} %get-tuple-element.25.refs_0_, bf16[2048,128]{1,0:T(8,128)(2,1)} %copy-done.29, bf16[2048,128]{1,0:T(8,128)(2,1)} %get-tuple-element.26.refs_2_, bf16[2048,128]{1,0:T(8,128)(2,1)} %copy-done.30, ...), custom_call_target="tpu_custom_call" | custom-call | flops 8589934592 | bytes 18874368 | tf_op jit(solution)/shard_map/ladder/pallas_call | solution.py:140
  124.8 9.9 %all-to-all-start.1 = ((bf16[32,256,128]{2,1,0:T(8,128)(2,1)}), bf16[32,256,128]{2,1,0:T(8,128)(2,1)S(1)}, u32[]{:S(2)}, u32[]{:S(2)}) async-start(bf16[32,256,128]{2,1,0:T(8,128)(2,1)} %bitcast.41), calls=%async_computation.1 | async-start | bytes 4194304 | tf_op jit(solution)/shard_map/all_to_all | solution.py:316
  134.7 1.9 collective-permute-start.31
  136.6 1.4 collective-permute-start.37
  138.0 0.6 collective-permute-start.33
  138.6 2.7 %collective-permute-start.35 = (bf16[512,512]{1,0:T(8,128)(2,1)S(1)}, bf16[512,512]{1,0:T(8,128)(2,1)}, u32[]{:S(2)}, u32[]{:S(2)}) collective-permute-start(bf16[512,512]{1,0:T(8,128)(2,1)S(1)} %pad_maximum_fusion.refs_4_), channel_id=1, source_target_pairs={{0,96},{32,0},{64,32},{96,64},{1,97},{33,1},{65,33},{97,65},{2,98}... | collective-permute-start | bytes 1572872 | tf_op jit(solution)/shard_map/ppermute | solution.py:20
  141.3 31.8 %collective-permute-done.31.refs_8_ = bf16[512,512]{1,0:T(8,128)(2,1)S(1)} collective-permute-done((bf16[512,512]{1,0:T(8,128)(2,1)S(1)}, bf16[512,512]{1,0:T(8,128)(2,1)S(1)}, u32[]{:S(2)}, u32[]{:S(2)}) %collective-permute-start.31) | collective-permute-done | bytes 524320 | tf_op jit(solution)/shard_map/ppermute | solution.py:20
  173.1 1.0 collective-permute-done.37.refs_14_
  174.1 10.3 %collective-permute-done.33.refs_10_ = bf16[512,512]{1,0:T(8,128)(2,1)} collective-permute-done((bf16[512,512]{1,0:T(8,128)(2,1)S(1)}, bf16[512,512]{1,0:T(8,128)(2,1)}, u32[]{:S(2)}, u32[]{:S(2)}) %collective-permute-start.33) | collective-permute-done | bytes 524320 | tf_op jit(solution)/shard_map/ppermute | solution.py:20
  184.4 1.1 collective-permute-start.41
  185.6 0.5 collective-permute-start.34
  186.2 8.9 %collective-permute-done.39.refs_16_ = bf16[512,512]{1,0:T(8,128)(2,1)} collective-permute-done((bf16[512,512]{1,0:T(8,128)(2,1)S(1)}, bf16[512,512]{1,0:T(8,128)(2,1)}, u32[]{:S(2)}, u32[]{:S(2)}) %collective-permute-start.39) | collective-permute-done | bytes 524320 | tf_op jit(solution)/shard_map/ppermute | solution.py:20
  195.1 2.5 %collective-permute-done.41.refs_18_ = bf16[512,512]{1,0:T(8,128)(2,1)} collective-permute-done((bf16[512,512]{1,0:T(8,128)(2,1)}, bf16[512,512]{1,0:T(8,128)(2,1)}, u32[]{:S(2)}, u32[]{:S(2)}) %collective-permute-start.41) | collective-permute-done | bytes 524320 | tf_op jit(solution)/shard_map/ppermute | solution.py:20
  197.6 0.8 copy-done.7
  198.4 0.5 collective-permute-start.42
  199.0 1.3 copy-done
  200.3 3.2 %settle.1 = (f32[128,512]{1,0:T(8,128)}, bf16[512,128]{1,0:T(8,128)(2,1)}) custom-call(bf16[4,2,4,256,128]{4,3,2,1,0:T(8,128)(2,1)} %bitcast.39), custom_call_target="tpu_custom_call" | custom-call | tf_op jit(solution)/shard_map/settle/pallas_call | solution.py:190
  203.6 1.8 collective-permute-start.26
  205.4 2.5 %collective-permute-start.27 = (bf16[32,16,128]{2,1,0:T(8,128)(2,1)}, bf16[32,16,128]{2,1,0:T(8,128)(2,1)S(1)}, u32[]{:S(2)}, u32[]{:S(2)}) collective-permute-start(bf16[32,16,128]{2,1,0:T(8,128)(2,1)} %bitcast.56), channel_id=1, source_target_pairs={{0,2},{1,3},{2,0},{3,1},{4,6},{5,7},{6,4},{7,5},{8,10},{9,11},{10,... | collective-permute-start | bytes 393224 | tf_op jit(solution)/shard_map/ppermute | solution.py:20
  207.9 1.5 collective-permute-start.28
  209.6 0.6 pad_add_fusion.where_ref
  210.4 3.9 %collective-permute-done.27.refs_2_ = bf16[32,16,128]{2,1,0:T(8,128)(2,1)S(1)} collective-permute-done((bf16[32,16,128]{2,1,0:T(8,128)(2,1)}, bf16[32,16,128]{2,1,0:T(8,128)(2,1)S(1)}, u32[]{:S(2)}, u32[]{:S(2)}) %collective-permute-start.27) | collective-permute-done | bytes 131104 | tf_op jit(solution)/shard_map/ppermute | solution.py:20
  214.4 0.6 copy-done.15
  215.1 5.7 %cycle.1 = (f32[128,512]{1,0:T(8,128)}, bf16[128,512]{1,0:T(8,128)(2,1)}, bf16[128,512]{1,0:T(8,128)(2,1)}, bf16[128,512]{1,0:T(8,128)(2,1)}) custom-call(s32[3]{0:T(128)} %pad_add_fusion.where_ref, bf16[32,16,128]{2,1,0:T(8,128)(2,1)} %bitcast.58, bf16[32,16,128]{2,1,0:T(8,128)(2,1)} %copy-done.14, bf16[32,16,128]{2,1,0:T(8,128)(2,1)} %copy-done.15, ...), custom_call_target="tpu_custom_call" | custom-call | tf_op jit(solution)/shard_map/cycle/pallas_call | solution.py:235
  220.7 2.9 %collective-permute-start.43 = (bf16[128,512]{1,0:T(8,128)(2,1)}, bf16[128,512]{1,0:T(8,128)(2,1)S(1)}, u32[]{:S(2)}, u32[]{:S(2)}) collective-permute-start(bf16[128,512]{1,0:T(8,128)(2,1)} %get-tuple-element.34), channel_id=1, source_target_pairs={{0,12},{4,0},{8,4},{12,8},{1,13},{5,1},{9,5},{13,9},{2,14},{6,2},{... | collective-permute-start | bytes 393224 | tf_op jit(solution)/shard_map/ppermute | solution.py:20
  223.6 0.9 collective-permute-start.45
  224.7 4.1 %collective-permute-done.43 = bf16[128,512]{1,0:T(8,128)(2,1)S(1)} collective-permute-done((bf16[128,512]{1,0:T(8,128)(2,1)}, bf16[128,512]{1,0:T(8,128)(2,1)S(1)}, u32[]{:S(2)}, u32[]{:S(2)}) %collective-permute-start.43) | collective-permute-done | bytes 131104 | tf_op jit(solution)/shard_map/ppermute | solution.py:20
  228.8 2.2 collective-permute-done.44
  231.0 1.1 collective-permute-done.45
  232.1 1.8 add_divide_fusion
  (128 shorter events, 2.9 us)
Async XLA Ops:
  3.1 32.4 %collective-permute-start.3 = (bf16[32,64,128]{2,1,0:T(8,128)(2,1)}, bf16[32,64,128]{2,1,0:T(8,128)(2,1)S(1)}, u32[]{:S(2)}, u32[]{:S(2)}) collective-permute-start(bf16[32,64,128]{2,1,0:T(8,128)(2,1)} %get-tuple-element.38), channel_id=1, source_target_pairs={{0,0},{1,1},{2,16},{3,17},{16,2},{17,3},{18,18},{19,19},{4,4},{5,5... | collective-permute-start | bytes 1572872 | tf_op jit(solution)/shard_map/ppermute | solution.py:269
  4.8 30.8 %collective-permute-start.4 = (bf16[32,64,128]{2,1,0:T(8,128)(2,1)}, bf16[32,64,128]{2,1,0:T(8,128)(2,1)S(1)}, u32[]{:S(2)}, u32[]{:S(2)}) collective-permute-start(bf16[32,64,128]{2,1,0:T(8,128)(2,1)} %get-tuple-element.37), channel_id=1, source_target_pairs={{0,1},{1,0},{2,17},{3,16},{16,3},{17,2},{18,19},{19,18},{4,5},{5,4... | collective-permute-start | bytes 1572872 | tf_op jit(solution)/shard_map/ppermute | solution.py:269
  7.0 15.1 %collective-permute-start.1 = (bf16[256,512]{1,0:T(8,128)(2,1)S(1)}, bf16[256,512]{1,0:T(8,128)(2,1)}, u32[]{:S(2)}, u32[]{:S(2)}) collective-permute-start(bf16[256,512]{1,0:T(8,128)(2,1)S(1)} %bitcast.53), channel_id=1, source_target_pairs={{0,8},{4,12},{8,0},{12,4},{1,9},{5,13},{9,1},{13,5},{2,10},{6,14},... | collective-permute-start | bytes 786440 | tf_op jit(solution)/shard_map/ppermute | solution.py:20
  10.1 12.2 %collective-permute-start.2 = (bf16[256,512]{1,0:T(8,128)(2,1)S(1)}, bf16[256,512]{1,0:T(8,128)(2,1)}, u32[]{:S(2)}, u32[]{:S(2)}) collective-permute-start(bf16[256,512]{1,0:T(8,128)(2,1)S(1)} %bitcast.52), channel_id=1, source_target_pairs={{0,12},{4,0},{8,4},{12,8},{1,13},{5,1},{9,5},{13,9},{2,14},{6,2},{... | collective-permute-start | bytes 786440 | tf_op jit(solution)/shard_map/ppermute | solution.py:20
  12.3 26.7 %all-to-all-start = ((bf16[32,16,4,128]{3,2,1,0:T(4,128)(2,1)}), bf16[32,16,4,128]{3,2,1,0:T(4,128)(2,1)S(1)}, u32[]{:S(2)}, u32[]{:S(2)}) async-start(bf16[32,16,4,128]{3,2,1,0:T(4,128)(2,1)} %bitcast.19), calls=%async_computation | async-start | bytes 1048576 | tf_op jit(solution)/shard_map/all_to_all | solution.py:263
  20.1 20.8 %copy-start.10 = (bf16[16,32,512]{2,1,0:T(8,128)(2,1)S(1)}, bf16[16,32,512]{2,1,0:T(8,128)(2,1)}, u32[]{:S(2)}) copy-start(bf16[16,32,512]{2,1,0:T(8,128)(2,1)} %param.8) | copy-start | bytes 1572868
  20.1 15.4 %collective-permute-start = (bf16[256,512]{1,0:T(8,128)(2,1)S(1)}, bf16[256,512]{1,0:T(8,128)(2,1)S(1)}, u32[]{:S(2)}, u32[]{:S(2)}) collective-permute-start(bf16[256,512]{1,0:T(8,128)(2,1)S(1)} %bitcast.51), channel_id=1, source_target_pairs={{0,4},{4,8},{8,12},{12,0},{1,5},{5,9},{9,13},{13,1},{2,6},{6,10},{... | collective-permute-start | bytes 786440 | tf_op jit(solution)/shard_map/ppermute | solution.py:20
  23.4 149.7 %copy-start.1 = (bf16[512,512]{1,0:T(8,128)(2,1)}, bf16[512,512]{1,0:T(8,128)(2,1)S(1)}, u32[]{:S(2)}) copy-start(bf16[512,512]{1,0:T(8,128)(2,1)S(1)} %pad_maximum_fusion.1.refs_6_) | copy-start | bytes 1572868
  35.5 105.7 %copy-start.2 = (bf16[512,512]{1,0:T(8,128)(2,1)}, bf16[512,512]{1,0:T(8,128)(2,1)S(1)}, u32[]{:S(2)}) copy-start(bf16[512,512]{1,0:T(8,128)(2,1)S(1)} %pad_maximum_fusion.refs_4_) | copy-start | bytes 1572868
  39.0 15.2 %copy-start.20 = (bf16[2048,128]{1,0:T(8,128)(2,1)S(1)}, bf16[2048,128]{1,0:T(8,128)(2,1)}, u32[]{:S(2)}) copy-start(bf16[2048,128]{1,0:T(8,128)(2,1)} %get-tuple-element.25.refs_0_) | copy-start | bytes 1572868
  39.0 26.1 %copy-start.21 = (bf16[2048,128]{1,0:T(8,128)(2,1)S(1)}, bf16[2048,128]{1,0:T(8,128)(2,1)}, u32[]{:S(2)}) copy-start(bf16[2048,128]{1,0:T(8,128)(2,1)} %get-tuple-element.26.refs_2_) | copy-start | bytes 1572868
  39.3 59.6 %copy-start.11 = (bf16[16,32,4,128]{3,2,1,0:T(4,128)(2,1)}, bf16[16,32,4,128]{3,2,1,0:T(4,128)(2,1)S(1)}, u32[]{:S(2)}) copy-start(bf16[16,32,4,128]{3,2,1,0:T(4,128)(2,1)S(1)} %copy.22) | copy-start | bytes 1572868
  39.3 15.0 %collective-permute-start.23 = (bf16[16,128,128]{2,1,0:T(8,128)(2,1)S(1)}, bf16[16,128,128]{2,1,0:T(8,128)(2,1)S(1)}, u32[]{:S(2)}, u32[]{:S(2)}) collective-permute-start(bf16[16,128,128]{2,1,0:T(8,128)(2,1)S(1)} %bitcast.45), channel_id=1, source_target_pairs={{0,32},{32,64},{64,96},{96,0},{1,33},{33,65},{65,97},{97,1},{2,34}... | collective-permute-start | bytes 1572872 | tf_op jit(solution)/shard_map/ppermute | solution.py:20
  41.2 23.9 %collective-permute-start.24 = (bf16[16,128,128]{2,1,0:T(8,128)(2,1)S(1)}, bf16[16,128,128]{2,1,0:T(8,128)(2,1)S(1)}, u32[]{:S(2)}, u32[]{:S(2)}) collective-permute-start(bf16[16,128,128]{2,1,0:T(8,128)(2,1)S(1)} %bitcast.46), channel_id=1, source_target_pairs={{0,96},{32,0},{64,32},{96,64},{1,97},{33,1},{65,33},{97,65},{2,98}... | collective-permute-start | bytes 1572872 | tf_op jit(solution)/shard_map/ppermute | solution.py:20
  43.0 23.7 %collective-permute-start.25 = (bf16[16,128,128]{2,1,0:T(8,128)(2,1)S(1)}, bf16[16,128,128]{2,1,0:T(8,128)(2,1)S(1)}, u32[]{:S(2)}, u32[]{:S(2)}) collective-permute-start(bf16[16,128,128]{2,1,0:T(8,128)(2,1)S(1)} %bitcast.47), channel_id=1, source_target_pairs={{0,64},{32,96},{64,0},{96,32},{1,65},{33,97},{65,1},{97,33},{2,66}... | collective-permute-start | bytes 1572872 | tf_op jit(solution)/shard_map/ppermute | solution.py:20
  45.0 22.2 %collective-permute-start.19 = (bf16[32,16,512]{2,1,0:T(8,128)(2,1)S(1)}, bf16[32,16,512]{2,1,0:T(8,128)(2,1)S(1)}, u32[]{:S(2)}, u32[]{:S(2)}) collective-permute-start(bf16[32,16,512]{2,1,0:T(8,128)(2,1)S(1)} %bitcast.49), channel_id=1, source_target_pairs={{0,0},{1,1},{2,16},{3,17},{16,2},{17,3},{18,18},{19,19},{4,4},{5,5... | collective-permute-start | bytes 1572872 | tf_op jit(solution)/shard_map/ppermute | solution.py:297
  45.6 24.2 %collective-permute-start.20 = (bf16[32,16,512]{2,1,0:T(8,128)(2,1)S(1)}, bf16[32,16,512]{2,1,0:T(8,128)(2,1)S(1)}, u32[]{:S(2)}, u32[]{:S(2)}) collective-permute-start(bf16[32,16,512]{2,1,0:T(8,128)(2,1)S(1)} %bitcast.50), channel_id=1, source_target_pairs={{0,1},{1,0},{2,17},{3,16},{16,3},{17,2},{18,19},{19,18},{4,5},{5,4... | collective-permute-start | bytes 1572872 | tf_op jit(solution)/shard_map/ppermute | solution.py:297
  54.3 42.5 %copy-start.23 = (bf16[16,128,128]{2,1,0:T(8,128)(2,1)}, bf16[16,128,128]{2,1,0:T(8,128)(2,1)S(1)}, u32[]{:S(2)}) copy-start(bf16[16,128,128]{2,1,0:T(8,128)(2,1)S(1)} %collective-permute-done.23.refs_5_) | copy-start | bytes 1572868
  54.3 15.6 %collective-permute-start.7 = (bf16[2048,128]{1,0:T(8,128)(2,1)S(1)}, bf16[2048,128]{1,0:T(8,128)(2,1)S(1)}, u32[]{:S(2)}, u32[]{:S(2)}) collective-permute-start(bf16[2048,128]{1,0:T(8,128)(2,1)S(1)} %copy-done.20), channel_id=1, source_target_pairs={{0,4},{4,8},{8,12},{12,0},{1,5},{5,9},{9,13},{13,1},{2,6},{6,10},{... | collective-permute-start | bytes 1572872 | tf_op jit(solution)/shard_map/ppermute | solution.py:20
  65.1 31.6 %copy-start.24 = (bf16[16,128,128]{2,1,0:T(8,128)(2,1)}, bf16[16,128,128]{2,1,0:T(8,128)(2,1)S(1)}, u32[]{:S(2)}) copy-start(bf16[16,128,128]{2,1,0:T(8,128)(2,1)S(1)} %collective-permute-done.24.refs_6_) | copy-start | bytes 1572868
  65.1 14.4 %collective-permute-start.13 = (bf16[2048,128]{1,0:T(8,128)(2,1)S(1)}, bf16[2048,128]{1,0:T(8,128)(2,1)}, u32[]{:S(2)}, u32[]{:S(2)}) collective-permute-start(bf16[2048,128]{1,0:T(8,128)(2,1)S(1)} %copy-done.21), channel_id=1, source_target_pairs={{0,12},{4,0},{8,4},{12,8},{1,13},{5,1},{9,5},{13,9},{2,14},{6,2},{... | collective-permute-start | bytes 1572872 | tf_op jit(solution)/shard_map/ppermute | solution.py:20
  66.6 30.1 %copy-start.25 = (bf16[16,128,128]{2,1,0:T(8,128)(2,1)}, bf16[16,128,128]{2,1,0:T(8,128)(2,1)S(1)}, u32[]{:S(2)}) copy-start(bf16[16,128,128]{2,1,0:T(8,128)(2,1)S(1)} %collective-permute-done.25.refs_7_) | copy-start | bytes 1572868
  66.6 13.9 %collective-permute-start.9 = (bf16[2048,128]{1,0:T(8,128)(2,1)S(1)}, bf16[2048,128]{1,0:T(8,128)(2,1)S(1)}, u32[]{:S(2)}, u32[]{:S(2)}) collective-permute-start(bf16[2048,128]{1,0:T(8,128)(2,1)S(1)} %copy-done.21), channel_id=1, source_target_pairs={{0,4},{4,8},{8,12},{12,0},{1,5},{5,9},{9,13},{13,1},{2,6},{6,10},{... | collective-permute-start | bytes 1572872 | tf_op jit(solution)/shard_map/ppermute | solution.py:20
  67.2 30.2 %copy-start.26 = (bf16[32,16,512]{2,1,0:T(8,128)(2,1)}, bf16[32,16,512]{2,1,0:T(8,128)(2,1)S(1)}, u32[]{:S(2)}) copy-start(bf16[32,16,512]{2,1,0:T(8,128)(2,1)S(1)} %collective-permute-done.19.refs_0_) | copy-start | bytes 1572868
  67.2 19.1 %collective-permute-start.11 = (bf16[2048,128]{1,0:T(8,128)(2,1)S(1)}, bf16[2048,128]{1,0:T(8,128)(2,1)}, u32[]{:S(2)}, u32[]{:S(2)}) collective-permute-start(bf16[2048,128]{1,0:T(8,128)(2,1)S(1)} %copy-done.20), channel_id=1, source_target_pairs={{0,12},{4,0},{8,4},{12,8},{1,13},{5,1},{9,5},{13,9},{2,14},{6,2},{... | collective-permute-start | bytes 1572872 | tf_op jit(solution)/shard_map/ppermute | solution.py:20
  69.9 27.5 %copy-start.28 = (bf16[32,16,512]{2,1,0:T(8,128)(2,1)}, bf16[32,16,512]{2,1,0:T(8,128)(2,1)S(1)}, u32[]{:S(2)}) copy-start(bf16[32,16,512]{2,1,0:T(8,128)(2,1)S(1)} %collective-permute-done.20.refs_1_) | copy-start | bytes 1572868
  69.9 16.4 %collective-permute-start.5 = (bf16[2048,128]{1,0:T(8,128)(2,1)S(1)}, bf16[2048,128]{1,0:T(8,128)(2,1)S(1)}, u32[]{:S(2)}, u32[]{:S(2)}) collective-permute-start(bf16[2048,128]{1,0:T(8,128)(2,1)S(1)} %copy-done.20), channel_id=1, source_target_pairs={{0,16},{16,0},{1,17},{17,1},{2,18},{18,2},{3,19},{19,3},{4,20},{20... | collective-permute-start | bytes 1572872 | tf_op jit(solution)/shard_map/ppermute | solution.py:24
  69.9 39.6 %copy-start.22 = (bf16[2048,128]{1,0:T(8,128)(2,1)}, bf16[2048,128]{1,0:T(8,128)(2,1)S(1)}, u32[]{:S(2)}) copy-start(bf16[2048,128]{1,0:T(8,128)(2,1)S(1)} %collective-permute-done.7.refs_4_) | copy-start | bytes 1572868
  69.9 19.6 %collective-permute-start.6 = (bf16[2048,128]{1,0:T(8,128)(2,1)S(1)}, bf16[2048,128]{1,0:T(8,128)(2,1)S(1)}, u32[]{:S(2)}, u32[]{:S(2)}) collective-permute-start(bf16[2048,128]{1,0:T(8,128)(2,1)S(1)} %copy-done.21), channel_id=1, source_target_pairs={{0,16},{16,0},{1,17},{17,1},{2,18},{18,2},{3,19},{19,3},{4,20},{20... | collective-permute-start | bytes 1572872 | tf_op jit(solution)/shard_map/ppermute | solution.py:24
  79.5 10.0 %collective-permute-start.21 = (bf16[32,16,512]{2,1,0:T(8,128)(2,1)S(1)}, bf16[32,16,512]{2,1,0:T(8,128)(2,1)S(1)}, u32[]{:S(2)}, u32[]{:S(2)}) collective-permute-start(bf16[32,16,512]{2,1,0:T(8,128)(2,1)S(1)} %collective-permute-done.19.refs_0_), channel_id=1, source_target_pairs={{0,16},{16,0},{1,17},{17,1},{2,18},{18,2},{3,19},{19,3},{4,20},{20... | collective-permute-start | bytes 1572872 | tf_op jit(solution)/shard_map/ppermute | solution.py:24
  80.6 16.8 %copy-start.27 = (bf16[2048,128]{1,0:T(8,128)(2,1)}, bf16[2048,128]{1,0:T(8,128)(2,1)S(1)}, u32[]{:S(2)}) copy-start(bf16[2048,128]{1,0:T(8,128)(2,1)S(1)} %collective-permute-done.9.refs_6_) | copy-start | bytes 1572868
  80.6 9.5 %collective-permute-start.22 = (bf16[32,16,512]{2,1,0:T(8,128)(2,1)S(1)}, bf16[32,16,512]{2,1,0:T(8,128)(2,1)S(1)}, u32[]{:S(2)}, u32[]{:S(2)}) collective-permute-start(bf16[32,16,512]{2,1,0:T(8,128)(2,1)S(1)} %collective-permute-done.20.refs_1_), channel_id=1, source_target_pairs={{0,16},{16,0},{1,17},{17,1},{2,18},{18,2},{3,19},{19,3},{4,20},{20... | collective-permute-start | bytes 1572872 | tf_op jit(solution)/shard_map/ppermute | solution.py:24
  86.2 10.5 %collective-permute-start.15 = (bf16[2048,128]{1,0:T(8,128)(2,1)S(1)}, bf16[2048,128]{1,0:T(8,128)(2,1)}, u32[]{:S(2)}, u32[]{:S(2)}) collective-permute-start(bf16[2048,128]{1,0:T(8,128)(2,1)S(1)} %collective-permute-done.7.refs_4_), channel_id=1, source_target_pairs={{0,4},{4,8},{8,12},{12,0},{1,5},{5,9},{9,13},{13,1},{2,6},{6,10},{... | collective-permute-start | bytes 1572872 | tf_op jit(solution)/shard_map/ppermute | solution.py:20
  86.3 23.2 %copy-start.29 = (bf16[2048,128]{1,0:T(8,128)(2,1)}, bf16[2048,128]{1,0:T(8,128)(2,1)S(1)}, u32[]{:S(2)}) copy-start(bf16[2048,128]{1,0:T(8,128)(2,1)S(1)} %collective-permute-done.5.refs_1_) | copy-start | bytes 1572868
  86.3 10.5 %collective-permute-start.17 = (bf16[2048,128]{1,0:T(8,128)(2,1)}, bf16[2048,128]{1,0:T(8,128)(2,1)S(1)}, u32[]{:S(2)}, u32[]{:S(2)}) collective-permute-start(bf16[2048,128]{1,0:T(8,128)(2,1)} %collective-permute-done.13.refs_10_), channel_id=1, source_target_pairs={{0,12},{4,0},{8,4},{12,8},{1,13},{5,1},{9,5},{13,9},{2,14},{6,2},{... | collective-permute-start | bytes 1572872 | tf_op jit(solution)/shard_map/ppermute | solution.py:20
  89.5 7.9 %collective-permute-start.10 = (bf16[2048,128]{1,0:T(8,128)(2,1)S(1)}, bf16[2048,128]{1,0:T(8,128)(2,1)S(1)}, u32[]{:S(2)}, u32[]{:S(2)}) collective-permute-start(bf16[2048,128]{1,0:T(8,128)(2,1)S(1)} %collective-permute-done.9.refs_6_), channel_id=1, source_target_pairs={{0,16},{16,0},{1,17},{17,1},{2,18},{18,2},{3,19},{19,3},{4,20},{20... | collective-permute-start | bytes 1572872 | tf_op jit(solution)/shard_map/ppermute | solution.py:24
  89.5 20.0 %collective-permute-start.14 = (bf16[2048,128]{1,0:T(8,128)(2,1)}, bf16[2048,128]{1,0:T(8,128)(2,1)}, u32[]{:S(2)}, u32[]{:S(2)}) collective-permute-start(bf16[2048,128]{1,0:T(8,128)(2,1)} %collective-permute-done.13.refs_10_), channel_id=1, source_target_pairs={{0,16},{16,0},{1,17},{17,1},{2,18},{18,2},{3,19},{19,3},{4,20},{20... | collective-permute-start | bytes 1572872 | tf_op jit(solution)/shard_map/ppermute | solution.py:24
  90.0 19.5 %collective-permute-start.8 = (bf16[2048,128]{1,0:T(8,128)(2,1)S(1)}, bf16[2048,128]{1,0:T(8,128)(2,1)}, u32[]{:S(2)}, u32[]{:S(2)}) collective-permute-start(bf16[2048,128]{1,0:T(8,128)(2,1)S(1)} %collective-permute-done.7.refs_4_), channel_id=1, source_target_pairs={{0,16},{16,0},{1,17},{17,1},{2,18},{18,2},{3,19},{19,3},{4,20},{20... | collective-permute-start | bytes 1572872 | tf_op jit(solution)/shard_map/ppermute | solution.py:24
  96.7 12.7 %collective-permute-start.12 = (bf16[2048,128]{1,0:T(8,128)(2,1)}, bf16[2048,128]{1,0:T(8,128)(2,1)}, u32[]{:S(2)}, u32[]{:S(2)}) collective-permute-start(bf16[2048,128]{1,0:T(8,128)(2,1)} %collective-permute-done.11.refs_8_), channel_id=1, source_target_pairs={{0,16},{16,0},{1,17},{17,1},{2,18},{18,2},{3,19},{19,3},{4,20},{20... | collective-permute-start | bytes 1572872 | tf_op jit(solution)/shard_map/ppermute | solution.py:24
  96.8 12.7 %collective-permute-start.16 = (bf16[2048,128]{1,0:T(8,128)(2,1)}, bf16[2048,128]{1,0:T(8,128)(2,1)}, u32[]{:S(2)}, u32[]{:S(2)}) collective-permute-start(bf16[2048,128]{1,0:T(8,128)(2,1)} %collective-permute-done.15.refs_12_), channel_id=1, source_target_pairs={{0,16},{16,0},{1,17},{17,1},{2,18},{18,2},{3,19},{19,3},{4,20},{20... | collective-permute-start | bytes 1572872 | tf_op jit(solution)/shard_map/ppermute | solution.py:24
  98.2 11.3 %collective-permute-start.18 = (bf16[2048,128]{1,0:T(8,128)(2,1)S(1)}, bf16[2048,128]{1,0:T(8,128)(2,1)}, u32[]{:S(2)}, u32[]{:S(2)}) collective-permute-start(bf16[2048,128]{1,0:T(8,128)(2,1)S(1)} %collective-permute-done.17.refs_14_), channel_id=1, source_target_pairs={{0,16},{16,0},{1,17},{17,1},{2,18},{18,2},{3,19},{19,3},{4,20},{20... | collective-permute-start | bytes 1572872 | tf_op jit(solution)/shard_map/ppermute | solution.py:24
  124.7 74.2 %copy-start.35 = (f32[256]{0:T(256)S(1)}, f32[256]{0:T(256)}, u32[]{:S(2)}) copy-start(f32[256]{0:T(256)} %param.13) | copy-start | bytes 3076
  124.8 74.3 %all-to-all-start.1 = ((bf16[32,256,128]{2,1,0:T(8,128)(2,1)}), bf16[32,256,128]{2,1,0:T(8,128)(2,1)S(1)}, u32[]{:S(2)}, u32[]{:S(2)}) async-start(bf16[32,256,128]{2,1,0:T(8,128)(2,1)} %bitcast.41), calls=%async_computation.1 | async-start | bytes 4194304 | tf_op jit(solution)/shard_map/all_to_all | solution.py:316
  134.7 74.7 %copy-start.18 = (f32[32]{0:T(128)S(1)}, f32[32]{0:T(128)}, u32[]{:S(2)}) copy-start(f32[32]{0:T(128)} %param.11) | copy-start | bytes 388
  134.7 38.4 %collective-permute-start.31 = (bf16[512,512]{1,0:T(8,128)(2,1)S(1)}, bf16[512,512]{1,0:T(8,128)(2,1)S(1)}, u32[]{:S(2)}, u32[]{:S(2)}) collective-permute-start(bf16[512,512]{1,0:T(8,128)(2,1)S(1)} %pad_maximum_fusion.refs_4_), channel_id=1, source_target_pairs={{0,32},{32,64},{64,96},{96,0},{1,33},{33,65},{65,97},{97,1},{2,34}... | collective-permute-start | bytes 1572872 | tf_op jit(solution)/shard_map/ppermute | solution.py:20
  136.6 37.5 %collective-permute-start.37 = (bf16[512,512]{1,0:T(8,128)(2,1)S(1)}, bf16[512,512]{1,0:T(8,128)(2,1)}, u32[]{:S(2)}, u32[]{:S(2)}) collective-permute-start(bf16[512,512]{1,0:T(8,128)(2,1)S(1)} %pad_maximum_fusion.1.refs_6_), channel_id=1, source_target_pairs={{0,96},{32,0},{64,32},{96,64},{1,97},{33,1},{65,33},{97,65},{2,98}... | collective-permute-start | bytes 1572872 | tf_op jit(solution)/shard_map/ppermute | solution.py:20
  138.0 46.4 %collective-permute-start.33 = (bf16[512,512]{1,0:T(8,128)(2,1)S(1)}, bf16[512,512]{1,0:T(8,128)(2,1)}, u32[]{:S(2)}, u32[]{:S(2)}) collective-permute-start(bf16[512,512]{1,0:T(8,128)(2,1)S(1)} %pad_maximum_fusion.1.refs_6_), channel_id=1, source_target_pairs={{0,32},{32,64},{64,96},{96,0},{1,33},{33,65},{65,97},{97,1},{2,34}... | collective-permute-start | bytes 1572872 | tf_op jit(solution)/shard_map/ppermute | solution.py:20
  138.6 46.9 %collective-permute-start.35 = (bf16[512,512]{1,0:T(8,128)(2,1)S(1)}, bf16[512,512]{1,0:T(8,128)(2,1)}, u32[]{:S(2)}, u32[]{:S(2)}) collective-permute-start(bf16[512,512]{1,0:T(8,128)(2,1)S(1)} %pad_maximum_fusion.refs_4_), channel_id=1, source_target_pairs={{0,96},{32,0},{64,32},{96,64},{1,97},{33,1},{65,33},{97,65},{2,98}... | collective-permute-start | bytes 1572872 | tf_op jit(solution)/shard_map/ppermute | solution.py:20
  141.3 44.3 %collective-permute-start.29 = (bf16[512,512]{1,0:T(8,128)(2,1)S(1)}, bf16[512,512]{1,0:T(8,128)(2,1)S(1)}, u32[]{:S(2)}, u32[]{:S(2)}) collective-permute-start(bf16[512,512]{1,0:T(8,128)(2,1)S(1)} %pad_maximum_fusion.refs_4_), channel_id=1, source_target_pairs={{0,16},{16,0},{1,17},{17,1},{2,18},{18,2},{3,19},{19,3},{4,20},{20... | collective-permute-start | bytes 1572872 | tf_op jit(solution)/shard_map/ppermute | solution.py:24
  173.1 13.0 %collective-permute-start.30 = (bf16[512,512]{1,0:T(8,128)(2,1)S(1)}, bf16[512,512]{1,0:T(8,128)(2,1)S(1)}, u32[]{:S(2)}, u32[]{:S(2)}) collective-permute-start(bf16[512,512]{1,0:T(8,128)(2,1)S(1)} %pad_maximum_fusion.1.refs_6_), channel_id=1, source_target_pairs={{0,16},{16,0},{1,17},{17,1},{2,18},{18,2},{3,19},{19,3},{4,20},{20... | collective-permute-start | bytes 1572872 | tf_op jit(solution)/shard_map/ppermute | solution.py:24
  174.1 21.0 %collective-permute-start.39 = (bf16[512,512]{1,0:T(8,128)(2,1)S(1)}, bf16[512,512]{1,0:T(8,128)(2,1)}, u32[]{:S(2)}, u32[]{:S(2)}) collective-permute-start(bf16[512,512]{1,0:T(8,128)(2,1)S(1)} %collective-permute-done.31.refs_8_), channel_id=1, source_target_pairs={{0,32},{32,64},{64,96},{96,0},{1,33},{33,65},{65,97},{97,1},{2,34}... | collective-permute-start | bytes 1572872 | tf_op jit(solution)/shard_map/ppermute | solution.py:20
  184.4 13.2 %collective-permute-start.41 = (bf16[512,512]{1,0:T(8,128)(2,1)}, bf16[512,512]{1,0:T(8,128)(2,1)}, u32[]{:S(2)}, u32[]{:S(2)}) collective-permute-start(bf16[512,512]{1,0:T(8,128)(2,1)} %collective-permute-done.37.refs_14_), channel_id=1, source_target_pairs={{0,96},{32,0},{64,32},{96,64},{1,97},{33,1},{65,33},{97,65},{2,98}... | collective-permute-start | bytes 1572872 | tf_op jit(solution)/shard_map/ppermute | solution.py:20
  185.6 12.1 %collective-permute-start.32 = (bf16[512,512]{1,0:T(8,128)(2,1)S(1)}, bf16[512,512]{1,0:T(8,128)(2,1)S(1)}, u32[]{:S(2)}, u32[]{:S(2)}) collective-permute-start(bf16[512,512]{1,0:T(8,128)(2,1)S(1)} %collective-permute-done.31.refs_8_), channel_id=1, source_target_pairs={{0,16},{16,0},{1,17},{17,1},{2,18},{18,2},{3,19},{19,3},{4,20},{20... | collective-permute-start | bytes 1572872 | tf_op jit(solution)/shard_map/ppermute | solution.py:24
  185.6 18.0 %collective-permute-start.34 = (bf16[512,512]{1,0:T(8,128)(2,1)}, bf16[512,512]{1,0:T(8,128)(2,1)S(1)}, u32[]{:S(2)}, u32[]{:S(2)}) collective-permute-start(bf16[512,512]{1,0:T(8,128)(2,1)} %collective-permute-done.33.refs_10_), channel_id=1, source_target_pairs={{0,16},{16,0},{1,17},{17,1},{2,18},{18,2},{3,19},{19,3},{4,20},{20... | collective-permute-start | bytes 1572872 | tf_op jit(solution)/shard_map/ppermute | solution.py:24
  186.1 19.3 %collective-permute-start.36 = (bf16[512,512]{1,0:T(8,128)(2,1)}, bf16[512,512]{1,0:T(8,128)(2,1)S(1)}, u32[]{:S(2)}, u32[]{:S(2)}) collective-permute-start(bf16[512,512]{1,0:T(8,128)(2,1)} %collective-permute-done.35.refs_12_), channel_id=1, source_target_pairs={{0,16},{16,0},{1,17},{17,1},{2,18},{18,2},{3,19},{19,3},{4,20},{20... | collective-permute-start | bytes 1572872 | tf_op jit(solution)/shard_map/ppermute | solution.py:24
  195.1 12.8 %collective-permute-start.38 = (bf16[512,512]{1,0:T(8,128)(2,1)}, bf16[512,512]{1,0:T(8,128)(2,1)}, u32[]{:S(2)}, u32[]{:S(2)}) collective-permute-start(bf16[512,512]{1,0:T(8,128)(2,1)} %collective-permute-done.37.refs_14_), channel_id=1, source_target_pairs={{0,16},{16,0},{1,17},{17,1},{2,18},{18,2},{3,19},{19,3},{4,20},{20... | collective-permute-start | bytes 1572872 | tf_op jit(solution)/shard_map/ppermute | solution.py:24
  197.6 12.6 %collective-permute-start.40 = (bf16[512,512]{1,0:T(8,128)(2,1)}, bf16[512,512]{1,0:T(8,128)(2,1)}, u32[]{:S(2)}, u32[]{:S(2)}) collective-permute-start(bf16[512,512]{1,0:T(8,128)(2,1)} %collective-permute-done.39.refs_16_), channel_id=1, source_target_pairs={{0,16},{16,0},{1,17},{17,1},{2,18},{18,2},{3,19},{19,3},{4,20},{20... | collective-permute-start | bytes 1572872 | tf_op jit(solution)/shard_map/ppermute | solution.py:24
  198.4 11.8 %collective-permute-start.42 = (bf16[512,512]{1,0:T(8,128)(2,1)}, bf16[512,512]{1,0:T(8,128)(2,1)}, u32[]{:S(2)}, u32[]{:S(2)}) collective-permute-start(bf16[512,512]{1,0:T(8,128)(2,1)} %collective-permute-done.41.refs_18_), channel_id=1, source_target_pairs={{0,16},{16,0},{1,17},{17,1},{2,18},{18,2},{3,19},{19,3},{4,20},{20... | collective-permute-start | bytes 1572872 | tf_op jit(solution)/shard_map/ppermute | solution.py:24
  203.6 6.8 %collective-permute-start.26 = (bf16[32,16,128]{2,1,0:T(8,128)(2,1)}, bf16[32,16,128]{2,1,0:T(8,128)(2,1)S(1)}, u32[]{:S(2)}, u32[]{:S(2)}) collective-permute-start(bf16[32,16,128]{2,1,0:T(8,128)(2,1)} %bitcast.55), channel_id=1, source_target_pairs={{0,1},{1,2},{2,3},{3,0},{4,5},{5,6},{6,7},{7,4},{8,9},{9,10},{10,1... | collective-permute-start | bytes 393224 | tf_op jit(solution)/shard_map/ppermute | solution.py:20
  205.4 8.9 %collective-permute-start.27 = (bf16[32,16,128]{2,1,0:T(8,128)(2,1)}, bf16[32,16,128]{2,1,0:T(8,128)(2,1)S(1)}, u32[]{:S(2)}, u32[]{:S(2)}) collective-permute-start(bf16[32,16,128]{2,1,0:T(8,128)(2,1)} %bitcast.56), channel_id=1, source_target_pairs={{0,2},{1,3},{2,0},{3,1},{4,6},{5,7},{6,4},{7,5},{8,10},{9,11},{10,... | collective-permute-start | bytes 393224 | tf_op jit(solution)/shard_map/ppermute | solution.py:20
  207.9 6.4 %collective-permute-start.28 = (bf16[32,16,128]{2,1,0:T(8,128)(2,1)}, bf16[32,16,128]{2,1,0:T(8,128)(2,1)S(1)}, u32[]{:S(2)}, u32[]{:S(2)}) collective-permute-start(bf16[32,16,128]{2,1,0:T(8,128)(2,1)} %bitcast.57), channel_id=1, source_target_pairs={{0,3},{1,0},{2,1},{3,2},{4,7},{5,4},{6,5},{7,6},{8,11},{9,8},{10,9... | collective-permute-start | bytes 393224 | tf_op jit(solution)/shard_map/ppermute | solution.py:20
  220.7 8.1 %collective-permute-start.43 = (bf16[128,512]{1,0:T(8,128)(2,1)}, bf16[128,512]{1,0:T(8,128)(2,1)S(1)}, u32[]{:S(2)}, u32[]{:S(2)}) collective-permute-start(bf16[128,512]{1,0:T(8,128)(2,1)} %get-tuple-element.34), channel_id=1, source_target_pairs={{0,12},{4,0},{8,4},{12,8},{1,13},{5,1},{9,5},{13,9},{2,14},{6,2},{... | collective-permute-start | bytes 393224 | tf_op jit(solution)/shard_map/ppermute | solution.py:20
  223.6 7.4 %collective-permute-start.44 = (bf16[128,512]{1,0:T(8,128)(2,1)}, bf16[128,512]{1,0:T(8,128)(2,1)S(1)}, u32[]{:S(2)}, u32[]{:S(2)}) collective-permute-start(bf16[128,512]{1,0:T(8,128)(2,1)} %get-tuple-element.35), channel_id=1, source_target_pairs={{0,8},{4,12},{8,0},{12,4},{1,9},{5,13},{9,1},{13,5},{2,10},{6,14},... | collective-permute-start | bytes 393224 | tf_op jit(solution)/shard_map/ppermute | solution.py:20
  223.6 8.5 %collective-permute-start.45 = (bf16[128,512]{1,0:T(8,128)(2,1)}, bf16[128,512]{1,0:T(8,128)(2,1)S(1)}, u32[]{:S(2)}, u32[]{:S(2)}) collective-permute-start(bf16[128,512]{1,0:T(8,128)(2,1)} %get-tuple-element.36), channel_id=1, source_target_pairs={{0,4},{4,8},{8,12},{12,0},{1,5},{5,9},{9,13},{13,1},{2,6},{6,10},{... | collective-permute-start | bytes 393224 | tf_op jit(solution)/shard_map/ppermute | solution.py:20
  (20 other events, 127.9 us)
